TPU v7x, 32 devices: a whole 2x2x4 slice. The times are simulated.
32 devices in a mesh: data: 32 (over z, y, x, core).
Axes of the slice: x: 2, y: 2, z: 4, core: 2. Of those that a mesh axis runs over, the one named last changes fastest.
Arguments:
- feat_a: bfloat16 [16384, 2048], P('data')
- feat_b: bfloat16 [16384, 2048], P('data')
- w_in: bfloat16 [2048, 2048], replicated
- w_mid: bfloat16 [2048, 2048], replicated
- w_out: bfloat16 [2048, 2048], replicated
- t_in: bfloat16 [2048, 2048], replicated
- t_mid: bfloat16 [2048, 2048], replicated
- t_out: bfloat16 [2048, 2048], replicated
- gain_1: float32 [2048], replicated
- bias_1: float32 [2048], replicated
- gain_2: float32 [2048], replicated
- bias_2: float32 [2048], replicated
- off_weight: float32 [], replicated
Outputs:
- output 1: float32 [], replicated
- output 2: float32 [16384, 2048], P('data')
- output 3: float32 [2048, 2048], replicated
- output 4: float32 [2048, 2048], replicated
- output 5: float32 [2048, 2048], replicated
- output 6: float32 [2048], replicated
- output 7: float32 [2048], replicated
- output 8: float32 [2048], replicated
- output 9: float32 [2048], replicated
All inputs are finite; a program needn't handle non-finite values.
Results may differ from a plain program's by a relative error of at most 0.00413.
Values are sent between devices in bfloat16 or wider.
A program may use at most 1 GiB of HBM per device.

v0:
```python
import jax
import jax.numpy as jnp
from jax import lax
from jax.sharding import PartitionSpec as P

NORM_EPS = 1e-5
DATA_AXIS = "data"


def contract_rows(left_op, right_op):
    return lax.dot_general(left_op, right_op, (((0,), (0,)), ((), ())), preferred_element_type=jnp.float32)


def contract_cols(left_op, right_op):
    return lax.dot_general(left_op, right_op, (((1,), (1,)), ((), ())), preferred_element_type=jnp.float32)


def solution(mesh):
    shards = mesh.shape[DATA_AXIS]
    row_part = P(DATA_AXIS, None)
    replicated = P()

    def local_step(feat_a, feat_b, w_in, w_mid, w_out, t_in, t_mid, t_out, gain_1, bias_1, gain_2, bias_2, off_weight):
        row_count = feat_a.shape[0] * shards

        def norm_pair(pre_a, pre_b):
            stat_sums = jnp.stack([jnp.sum(pre_a, axis=0), jnp.sum(pre_a * pre_a, axis=0), jnp.sum(pre_b, axis=0), jnp.sum(pre_b * pre_b, axis=0)])
            stat_means = lax.psum(stat_sums, DATA_AXIS) / row_count
            inv_a = lax.rsqrt(stat_means[1] - stat_means[0] * stat_means[0] + NORM_EPS)
            inv_b = lax.rsqrt(stat_means[3] - stat_means[2] * stat_means[2] + NORM_EPS)
            return (pre_a - stat_means[0]) * inv_a, inv_a, (pre_b - stat_means[2]) * inv_b

        def hidden_pair(in_a, in_b, weight_a, weight_b, gain_vec, bias_vec):
            normed_a, inv_a, normed_b = norm_pair(jnp.dot(in_a, weight_a, preferred_element_type=jnp.float32), jnp.dot(in_b, weight_b, preferred_element_type=jnp.float32))
            pre_act = normed_a * gain_vec + bias_vec
            act_a = jnp.maximum(pre_act, 0.0).astype(jnp.bfloat16)
            act_b = jnp.maximum(normed_b * gain_vec + bias_vec, 0.0).astype(jnp.bfloat16)
            return act_a, act_b, normed_a, inv_a, pre_act > 0.0

        def norm_back(grad_n, normed, inv_std):
            stat_means = lax.psum(jnp.stack([jnp.sum(grad_n, axis=0), jnp.sum(grad_n * normed, axis=0)]), DATA_AXIS) / row_count
            return (grad_n - stat_means[0] - normed * stat_means[1]) * inv_std

        def affine_back(grad_pre, normed, inv_std, gain_vec):
            stat_sums = lax.psum(jnp.stack([jnp.sum(grad_pre * normed, axis=0), jnp.sum(grad_pre, axis=0)]), DATA_AXIS)
            grad_u = (grad_pre - stat_sums[1] / row_count - normed * (stat_sums[0] / row_count)) * (gain_vec * inv_std)
            return grad_u.astype(jnp.bfloat16), stat_sums[0], stat_sums[1]

        act_1, teach_1, normed_1, inv_1, mask_1 = hidden_pair(feat_a, feat_b, w_in, t_in, gain_1, bias_1)
        act_2, teach_2, normed_2, inv_2, mask_2 = hidden_pair(act_1, teach_1, w_mid, t_mid, gain_2, bias_2)
        zh_a, inv_z, zh_b = norm_pair(jnp.dot(act_2, w_out, preferred_element_type=jnp.float32), jnp.dot(teach_2, t_out, preferred_element_type=jnp.float32))
        emb_a = zh_a.astype(jnp.bfloat16)
        emb_b = zh_b.astype(jnp.bfloat16)
        corr_mat = lax.psum(contract_rows(emb_a, emb_b), DATA_AXIS) / row_count
        proj_width = corr_mat.shape[0]
        on_diag = lax.broadcasted_iota(jnp.int32, (proj_width, proj_width), 0) == lax.broadcasted_iota(jnp.int32, (proj_width, proj_width), 1)
        loss_value = jnp.sum(jnp.where(on_diag, jnp.square(1.0 - corr_mat), off_weight * jnp.square(corr_mat)))
        grad_c = jnp.where(on_diag, -2.0 * (1.0 - corr_mat), 2.0 * off_weight * corr_mat).astype(jnp.bfloat16)
        grad_emb = contract_cols(emb_b, grad_c) / row_count
        grad_z = norm_back(grad_emb, zh_a, inv_z).astype(jnp.bfloat16)
        grad_w_out = contract_rows(act_2, grad_z)
        grad_pre_2 = jnp.where(mask_2, contract_cols(grad_z, w_out), 0.0)
        grad_u_2, grad_gain_2, grad_bias_2 = affine_back(grad_pre_2, normed_2, inv_2, gain_2)
        grad_w_mid = contract_rows(act_1, grad_u_2)
        grad_pre_1 = jnp.where(mask_1, contract_cols(grad_u_2, w_mid), 0.0)
        grad_u_1, grad_gain_1, grad_bias_1 = affine_back(grad_pre_1, normed_1, inv_1, gain_1)
        grad_w_in = contract_rows(feat_a, grad_u_1)
        weight_grads = lax.psum((grad_w_in, grad_w_mid, grad_w_out), DATA_AXIS)
        return (loss_value, grad_emb, weight_grads[0], weight_grads[1], weight_grads[2], grad_gain_1, grad_bias_1, grad_gain_2, grad_bias_2)

    return jax.shard_map(local_step, mesh=mesh, in_specs=(row_part, row_part) + (replicated,) * 11, out_specs=(replicated, row_part) + (replicated,) * 7, check_vma=False)
```

profile of v0, /device:TPU:0, one launch (start us, length us, event | category | flops | bytes accessed | tf_op | source)
XLA Modules:
  0.0 1443.7 jit_solution(9255854788270067221)
XLA Ops:
  7.2 0.0 all-reduce.4.cloned.1.call-start
  7.2 10.7 fusion.47
  18.0 6.1 fusion.46
  24.1 42.1 %psum.70 = f32[4,2048]{1,0:T(4,128)S(1)} all-reduce(f32[4,2048]{1,0:T(4,128)S(1)} %pad_maximum_fusion), channel_id=1, replica_groups=mesh['data'=32] {'data'}, use_global_device_ids=true, to_apply=%region_4.0 | all-reduce | flops 8192 | bytes 65536 | tf_op jit(solution)/shard_map/psum | solution.py:28
  66.3 11.3 fusion.45
  77.6 9.6 fusion.44
  87.2 40.5 %psum.71 = f32[4,2048]{1,0:T(4,128)S(1)} all-reduce(f32[4,2048]{1,0:T(4,128)S(1)} %pad_maximum_fusion.1), channel_id=1, replica_groups=mesh['data'=32] {'data'}, use_global_device_ids=true, to_apply=%region_9.0 | all-reduce | flops 8192 | bytes 65536 | tf_op jit(solution)/shard_map/psum | solution.py:28
  127.9 11.3 fusion.43
  139.1 9.5 fusion.42
  148.7 39.8 %psum.72 = f32[4,2048]{1,0:T(4,128)S(1)} all-reduce(f32[4,2048]{1,0:T(4,128)S(1)} %pad_maximum_fusion.2), channel_id=1, replica_groups=mesh['data'=32] {'data'}, use_global_device_ids=true, to_apply=%region_14.0 | all-reduce | flops 8192 | bytes 65536 | tf_op jit(solution)/shard_map/psum | solution.py:28
  188.6 14.2 fusion.3
  202.9 0.3 all-reduce.6.cloned.1.call-start
  203.8 277.1 %all-reduce.4.cloned.1.call-done = f32[2048,2048]{1,0:T(8,128)} async-done(((f32[2048,2048]{1,0:T(8,128)}), f32[2048,2048]{1,0:T(8,128)}) %all-reduce.4.cloned.1.call-update) | async-done | bytes 16777232 | tf_op jit(solution)/shard_map/psum | solution.py:54
  480.9 13.0 fusion.41
  494.0 40.3 %psum.74 = f32[2,2048]{1,0:T(2,128)S(1)} all-reduce(f32[2,2048]{1,0:T(2,128)S(1)} %pad_maximum_fusion.3), channel_id=1, replica_groups=mesh['data'=32] {'data'}, use_global_device_ids=true, to_apply=%region_19.20 | all-reduce | flops 4096 | bytes 32768 | tf_op jit(solution)/shard_map/psum | solution.py:41
  534.3 4.7 multiply_convert_fusion.2
  539.0 10.2 multiply_reduce_fusion.1
  549.2 8.6 fusion.39
  557.9 39.4 %psum.75 = f32[2,2048]{1,0:T(2,128)S(1)} all-reduce(f32[2,2048]{1,0:T(2,128)S(1)} %pad_maximum_fusion.4), channel_id=1, replica_groups=mesh['data'=32] {'data'}, use_global_device_ids=true, to_apply=%region_22.23 | all-reduce | flops 4096 | bytes 32768 | tf_op jit(solution)/shard_map/psum | solution.py:45
  597.3 0.6 fusion.51
  597.9 4.7 multiply_convert_fusion.1
  602.6 10.2 multiply_reduce_fusion
  612.9 8.6 fusion.37
  621.5 41.0 %psum.76 = f32[2,2048]{1,0:T(2,128)S(1)} all-reduce(f32[2,2048]{1,0:T(2,128)S(1)} %pad_maximum_fusion.5), channel_id=1, replica_groups=mesh['data'=32] {'data'}, use_global_device_ids=true, to_apply=%region_25.26 | all-reduce | flops 4096 | bytes 32768 | tf_op jit(solution)/shard_map/psum | solution.py:45
  662.5 0.6 fusion.52
  663.1 12.2 convolution_bitcast_fusion
  675.3 8.8 select_reduce_fusion
  684.1 712.2 %all-reduce.6.cloned.1.call-done = (f32[2048,2048]{0,1:T(8,128)}, f32[2048,2048]{1,0:T(8,128)}, f32[2048,2048]{1,0:T(8,128)}) async-done(((f32[2048,2048]{0,1:T(8,128)}, f32[2048,2048]{1,0:T(8,128)}, f32[2048,2048]{1,0:T(8,128)}), (f32[2048,2048]{0,1:T(8,128)}, f32[2048,2048]{1,0:T(8,128)}, f32[2048,2048]{1,0:T(8,128)})) %all-reduce.6.cloned.1.call-update) | async-done | bytes 50331664 | tf_op jit(solution)/shard_map/psum | solution.py:68
  1396.2 17.6 %copy.22 = f32[2048,2048]{1,0:T(8,128)} copy(f32[2048,2048]{0,1:T(8,128)} %get-tuple-element.36) | data formatting | bytes 33554432
  1413.8 12.7 copy.28
  1426.5 3.7 copy-done.1
  1430.3 6.2 copy.29
  (39 shorter events, 0.4 us)
Async XLA Ops:
  7.2 10.8 copy-start
  7.2 473.7 %all-reduce.4.cloned.1.call-start = ((), (), s32[]{:S(2)}) async-start(), calls=%async_computation | async-start | bytes 33554432 | tf_op jit(solution)/shard_map/psum | solution.py:54
  7.2 10.7 copy-start.6
  17.9 48.3 %copy-start.5 = (f32[2048]{0:T(1024)S(1)}, f32[2048]{0:T(1024)}, u32[]{:S(2)}) copy-start(f32[2048]{0:T(1024)} %param.21) | copy-start | bytes 24580
  17.9 48.3 %copy-start.8 = (f32[2048]{0:T(1024)S(1)}, f32[2048]{0:T(1024)}, u32[]{:S(2)}) copy-start(f32[2048]{0:T(1024)} %param.22) | copy-start | bytes 24580
  66.3 11.3 copy-start.9
  77.6 50.2 %copy-start.4 = (f32[2048]{0:T(1024)S(1)}, f32[2048]{0:T(1024)}, u32[]{:S(2)}) copy-start(f32[2048]{0:T(1024)} %param.23) | copy-start | bytes 24580
  77.6 50.2 %copy-start.7 = (f32[2048]{0:T(1024)S(1)}, f32[2048]{0:T(1024)}, u32[]{:S(2)}) copy-start(f32[2048]{0:T(1024)} %param.24) | copy-start | bytes 24580
  127.8 11.3 copy-start.2
  202.9 1193.4 %all-reduce.6.cloned.1.call-start = ((), (), s32[]{:S(2)}) async-start(), calls=%async_computation.1 | async-start | bytes 100663296 | tf_op jit(solution)/shard_map/psum | solution.py:68
  534.3 4.7 copy-start.3
  597.9 4.7 copy-start.10
  1413.8 16.4 %copy-start.1 = (f32[2048,2048]{1,0:T(8,128)S(1)}, f32[2048,2048]{1,0:T(8,128)}, u32[]{:S(2)}) copy-start(f32[2048,2048]{1,0:T(8,128)} %get-tuple-element.76) | copy-start | bytes 50331652
Sparse Core Ops, SparseCore 0:
  203.0 277.8 all-reduce.3
  675.4 720.7 all-reduce.5
where the time goes:
time: 1450 us; the launch traced here: 1440 us
  waiting for transfers between devices  989 us (68%)
  blocking collectives  243 us (17%)
  matrix products  136 us (9%)
  local copies, waits for them, and re-layouts  40.2 us (3%)
  other arithmetic  19.8 us (1%)
  between operations  15.4 us (1%)
    psum x1, waiting for transfers between devices, local_step(): weight_grads = lax.psum((grad_w_in, grad_w_mid, grad_w_out), DATA_AXIS)  712 us
    psum x1, waiting for transfers between devices, local_step(): corr_mat = lax.psum(contract_rows(emb_a, emb_b), DATA_AXIS) / row_count  277 us
    psum x3, blocking collectives, norm_pair(): stat_means = lax.psum(stat_sums, DATA_AXIS) / row_count  122 us
    psum x2, blocking collectives, affine_back(): lax.psum(jnp.stack([jnp.sum(grad_pre * normed, axis=0), jnp.sum(grad_pre,...  80.5 us
    dot_general x4, matrix products, contract_rows(): lax.dot_general(left_op, right_op, (((0,), (0,)), ((), ())), preferred_el...  43.6 us
    psum x1, blocking collectives, norm_back(): lax.psum(jnp.stack([jnp.sum(grad_n, axis=0), jnp.sum(grad_n * normed, axi...  40.3 us
    unnamed x25, local copies, waits for them, and re-layouts  40.2 us
    dot_general x3, matrix products, contract_cols(): lax.dot_general(left_op, right_op, (((1,), (1,)), ((), ())), preferred_el...  33.5 us
  transfers between devices with their start and end apart: 2, of which 2 were waited for; matrix products, arithmetic and copies ran while one was open for 1% of the time, Pallas kernels for 0%

commit v1 on v0

v1 whole, which is shorter than its diff:
```python
import functools

import jax
import jax.numpy as jnp
from jax import lax
from jax.experimental import pallas as pl
from jax.experimental.pallas import tpu as pltpu
from jax.sharding import PartitionSpec as P

NORM_EPS = 1e-5
DATA_AXIS = "data"
MESH = pl.DeviceIdType.MESH
VMEM_BYTES = 62 * 1024 * 1024
LANES = 128
PLANE = 8
DEPTH = 4
CORE, AXIS_X, AXIS_Y, AXIS_Z0, AXIS_Z1 = 1, 2, 4, 8, 16


def contract_rows(left_op, right_op):
    return lax.dot_general(left_op, right_op, (((0,), (0,)), ((), ())), preferred_element_type=jnp.float32)


def contract_cols(left_op, right_op):
    return lax.dot_general(left_op, right_op, (((1,), (1,)), ((), ())), preferred_element_type=jnp.float32)


def signal_all(sem, peers):
    for peer in peers:
        pl.semaphore_signal(sem, inc=1, device_id=(peer,), device_id_type=MESH)


def small_sum_kernel(x_ref, o_ref, plane_buf, depth_buf, own_buf, s1, r1, s2, r2, s3, r3):
    me = lax.axis_index(DATA_AXIS)
    pos, plane = me % PLANE, me // PLANE
    mates = [(pos + d) % PLANE for d in range(1, PLANE)]
    levels = [(plane + d) % DEPTH for d in range(1, DEPTH)]
    peers = [plane * PLANE + m for m in mates] + [lv * PLANE + pos for lv in levels]
    barrier = pltpu.get_barrier_semaphore()
    signal_all(barrier, peers)
    pl.semaphore_wait(barrier, len(peers))

    def plane_copy(src, dst, send, recv, mate):
        return pltpu.make_async_remote_copy(src, dst, send, recv, device_id=(plane * PLANE + mate,), device_id_type=MESH)

    out1 = [plane_copy(x_ref.at[m], plane_buf.at[pos], s1.at[m], r1.at[pos], m) for m in mates]
    for c in out1:
        c.start()
    plane_buf[pos] = x_ref[pos]
    for m in mates:
        plane_copy(x_ref.at[m], plane_buf.at[m], s1.at[m], r1.at[m], m).wait_recv()
    total = plane_buf[0]
    for i in range(1, PLANE):
        total = total + plane_buf[i]
    own_buf[0] = total
    depth_buf[plane] = total

    def depth_copy(slot, level):
        return pltpu.make_async_remote_copy(
            own_buf.at[0], depth_buf.at[slot], s2.at[level], r2.at[slot], device_id=(level * PLANE + pos,), device_id_type=MESH
        )

    out2 = [depth_copy(plane, lv) for lv in levels]
    for c in out2:
        c.start()
    for lv in levels:
        depth_copy(lv, lv).wait_recv()
    total = depth_buf[0]
    for i in range(1, DEPTH):
        total = total + depth_buf[i]
    own_buf[1] = total
    o_ref[pos] = total
    out3 = [plane_copy(own_buf.at[1], o_ref.at[pos], s3.at[m], r3.at[pos], m) for m in mates]
    for c in out3:
        c.start()
    for m in mates:
        plane_copy(own_buf.at[1], o_ref.at[m], s3.at[m], r3.at[m], m).wait_recv()
    for c in out1 + out2 + out3:
        c.wait_send()


def small_sum(rows):
    count, width = rows.shape
    tile = (PLANE, PLANE, LANES)
    size = PLANE * PLANE * LANES
    flat = jnp.pad(rows.reshape(-1), (0, size - count * width)).reshape(tile)
    total = pl.pallas_call(
        small_sum_kernel,
        name="small_sum",
        out_shape=jax.ShapeDtypeStruct(tile, jnp.float32),
        in_specs=[pl.BlockSpec(memory_space=pltpu.VMEM)],
        out_specs=pl.BlockSpec(memory_space=pltpu.VMEM),
        scratch_shapes=[
            pltpu.VMEM(tile, jnp.float32),
            pltpu.VMEM((DEPTH, PLANE, LANES), jnp.float32),
            pltpu.VMEM((2, PLANE, LANES), jnp.float32),
        ]
        + [pltpu.SemaphoreType.DMA((n,)) for n in (PLANE, PLANE, DEPTH, DEPTH, PLANE, PLANE)],
        compiler_params=pltpu.CompilerParams(collective_id=0, has_side_effects=True),
    )(flat)
    return total.reshape(-1)[: count * width].reshape(count, width)


LAGS = (0, 1, 3, 5, 6, 7, 8, 9, 11, 13)
ORDER = (0, 1, 5, 4, 6, 3, 7, 2, 8, 9)


def large_sum_kernel(mats, chunks, z_first, finish, *refs):
    ins, refs = refs[:mats], refs[mats:]
    extra, refs = refs[: finish.inputs], refs[finish.inputs :]
    outs, refs = refs[:mats], refs[mats:]
    extra_out, refs = refs[: finish.outputs], refs[finish.outputs :]
    acc, half, rx, ry, rz, rl, gathered, load_sem, store_sem, send, recv = refs
    if not finish.narrow:
        gathered = half
    chunk_rows = ins[0].shape[0] // chunks
    half_rows = chunk_rows // 2
    me = lax.axis_index(DATA_AXIS)
    core, bx, by, bz0, bz1 = me % 2, (me // 2) % 2, (me // 4) % 2, (me // 8) % 2, (me // 16) % 2

    barrier = pltpu.get_barrier_semaphore()
    mates = [me + s * (1 - 2 * b) for s, b in ((1, core), (2, bx), (4, by), (8, bz0), (16, bz1))]
    signal_all(barrier, mates)
    pl.semaphore_wait(barrier, len(mates))

    xy = ((2 + 2 * core, core * by + (1 - core) * bx), (4 - 2 * core, core * bx + (1 - core) * by))
    zz = ((8, bz0), (16, bz1))

    def steps_of(k):
        part = k % chunks
        zf = 0
        for z in z_first:
            same = part - z
            zf = zf + (1 - lax.min(same * same, 1))
        pairs = []
        for a, b in zip(xy + zz, zz + xy):
            stride = zf * b[0] + (1 - zf) * a[0]
            bit = zf * b[1] + (1 - zf) * a[1]
            pairs.append((me + stride * (1 - 2 * bit), bit))
        return pairs

    def offsets(pairs):
        offs, size = [0], half_rows
        for _, bit in pairs[:3]:
            size = size // 2
            offs.append(offs[-1] + bit * size)
        return offs

    def rows(off, size):
        return pl.ds(pl.multiple_of(off, size), size)

    def remote(src, dst, stage, k, mate):
        return pltpu.make_async_remote_copy(src, dst, send.at[stage, k], recv.at[stage, k], device_id=(mate,), device_id_type=MESH)

    def mat_row(k, side):
        return pl.multiple_of((k % chunks) * chunk_rows + side * half_rows, half_rows)

    other_core = mates[0]

    def first_copy(w, k):
        return remote(ins[w].at[pl.ds(mat_row(k, 1 - core), half_rows)], half.at[k], 0, k, other_core)

    def load_copy(w, k):
        return pltpu.make_async_copy(ins[w].at[pl.ds(mat_row(k, core), half_rows)], acc.at[k], load_sem.at[k])

    def last_copy(w, k, side):
        return remote(gathered.at[k], outs[w].at[pl.ds(mat_row(k, side), half_rows)], 8, k, other_core)

    def store_copy(w, k):
        return pltpu.make_async_copy(gathered.at[k], outs[w].at[pl.ds(mat_row(k, core), half_rows)], store_sem.at[k])

    landing = (rx, ry, rz, rl)

    def reduce_copy(i, k, pairs, offs):
        size = half_rows >> (i + 1)
        if i == 3:
            size = half_rows >> 3
            off = offs[3]
        else:
            off = offs[i] + (1 - pairs[i][1]) * size
        return remote(acc.at[k, rows(off, size)], landing[i].at[k], 1 + i, k, pairs[i][0])

    def gather_copy(i, k, pairs, offs):
        size = half_rows >> (i + 1)
        block = gathered.at[k, rows(offs[i + 1], size)]
        return remote(block, block, 7 - i, k, pairs[i][0])

    def add_rows(dst, k, off, size, buf):
        step = min(size, 16)

        def body(i, carry):
            at = pl.ds(pl.multiple_of(off + i * step, step), step)
            dst[k, at] = acc[k, at] + buf[k, pl.ds(pl.multiple_of(i * step, step), step)]
            return carry

        lax.fori_loop(0, size // step, body, 0)

    def for_mat(k, what):
        for w in range(mats):
            pl.when(k // chunks == w)(functools.partial(what, w))

    def stage(i, k):
        pairs = steps_of(k)
        offs = offsets(pairs)
        if i == 0:

            def begin(w):
                first_copy(w, k).start()
                load_copy(w, k).start()

            for_mat(k, begin)
        elif i == 1:

            def arrive(w):
                load_copy(w, k).wait()
                first_copy(w, k).wait_recv()

            for_mat(k, arrive)
            add_rows(acc, k, 0, half_rows, half)
            reduce_copy(0, k, pairs, offs).start()
        elif i < 5:
            reduce_copy(i - 2, k, pairs, offs).wait_recv()
            add_rows(acc, k, offs[i - 1], half_rows >> (i - 1), landing[i - 2])
            reduce_copy(i - 1, k, pairs, offs).start()
        elif i == 5:
            reduce_copy(3, k, pairs, offs).wait_recv()
            if finish.narrow:
                row = mat_row(k, core) + offs[3]
                finish.apply(extra, extra_out, acc, rl, gathered, k, offs[3], half_rows >> 3, row)
            else:
                add_rows(gathered, k, offs[3], half_rows >> 3, rl)
            gather_copy(2, k, pairs, offs).start()
        elif i < 8:
            gather_copy(8 - i, k, pairs, offs).wait_recv()
            gather_copy(7 - i, k, pairs, offs).start()
        elif i == 8:
            gather_copy(0, k, pairs, offs).wait_recv()

            def emit(w):
                last_copy(w, k, core).start()
                store_copy(w, k).start()

            for_mat(k, emit)
        else:

            def close(w):
                last_copy(w, k, 1 - core).wait_recv()
                store_copy(w, k).wait()
                last_copy(w, k, core).wait_send()
                first_copy(w, k).wait_send()

            for_mat(k, close)
            for n in range(4):
                reduce_copy(n, k, pairs, offs).wait_send()
            for n in range(3):
                gather_copy(n, k, pairs, offs).wait_send()

    if finish.narrow:
        finish.begin(extra_out)
    count = mats * chunks

    def slot(t, carry):
        for i in ORDER:
            k = t - LAGS[i]

            @pl.when((k >= 0) & (k < count))
            def _():
                stage(i, k)

        return carry

    lax.fori_loop(0, count + LAGS[-1], slot, 0)


class PlainFinish:
    narrow = False
    inputs = 0
    outputs = 0
    out_dtype = jnp.float32


class CorrFinish:
    narrow = True
    inputs = 1
    outputs = 1
    out_dtype = jnp.bfloat16

    def __init__(self, row_count):
        self.row_count = row_count

    def begin(self, extra_out):
        extra_out[0][...] = jnp.zeros_like(extra_out[0])

    def apply(self, extra, extra_out, acc, rl, gathered, k, off, size, row):
        width = acc.shape[-1]
        at = pl.ds(pl.multiple_of(off, size), size)
        corr = (acc[k, at] + rl[k]) / self.row_count
        diag = (row + lax.broadcasted_iota(jnp.int32, (size, width), 0)) == lax.broadcasted_iota(jnp.int32, (size, width), 1)
        off_weight = extra[0][0]
        miss = 1.0 - corr
        terms = jnp.where(diag, miss * miss, off_weight * (corr * corr))
        extra_out[0][...] += jnp.sum(terms, axis=0, keepdims=True)
        gathered[k, at] = jnp.where(diag, -2.0 * miss, 2.0 * off_weight * corr).astype(jnp.bfloat16)


def large_sum(arrays, chunks, z_first, finish, extra, collective_id):
    mats = len(arrays)
    n_rows, width = arrays[0].shape
    half_rows = n_rows // chunks // 2
    count = mats * chunks
    any_spec = pl.BlockSpec(memory_space=pl.ANY)
    out_shape = [jax.ShapeDtypeStruct((n_rows, width), finish.out_dtype) for _ in arrays]
    out_specs = [any_spec] * mats
    if finish.outputs:
        out_shape.append(jax.ShapeDtypeStruct((1, width), jnp.float32))
        out_specs.append(pl.BlockSpec(memory_space=pltpu.VMEM))

    def buf(rows, dtype=jnp.float32):
        return pltpu.VMEM((count, rows, width), dtype)

    narrow_buf = buf(half_rows, finish.out_dtype) if finish.narrow else pltpu.VMEM((8, LANES), jnp.float32)
    return pl.pallas_call(
        functools.partial(large_sum_kernel, mats, chunks, z_first, finish),
        name="large_sum",
        out_shape=out_shape,
        in_specs=[any_spec] * mats + [pl.BlockSpec(memory_space=pltpu.SMEM)] * len(extra),
        out_specs=out_specs,
        scratch_shapes=[
            buf(half_rows),
            buf(half_rows),
            buf(half_rows // 2),
            buf(half_rows // 4),
            buf(half_rows // 8),
            buf(half_rows // 8),
            narrow_buf,
            pltpu.SemaphoreType.DMA((count,)),
            pltpu.SemaphoreType.DMA((count,)),
            pltpu.SemaphoreType.DMA((9, count)),
            pltpu.SemaphoreType.DMA((9, count)),
        ],
        compiler_params=pltpu.CompilerParams(collective_id=collective_id, has_side_effects=True, vmem_limit_bytes=VMEM_BYTES),
    )(*arrays, *extra)


def solution(mesh):
    shards = mesh.shape[DATA_AXIS]
    row_part = P(DATA_AXIS, None)
    replicated = P()

    def local_step(feat_a, feat_b, w_in, w_mid, w_out, t_in, t_mid, t_out, gain_1, bias_1, gain_2, bias_2, off_weight):
        row_count = feat_a.shape[0] * shards

        def norm_pair(pre_a, pre_b):
            stat_sums = jnp.stack([jnp.sum(pre_a, axis=0), jnp.sum(pre_a * pre_a, axis=0), jnp.sum(pre_b, axis=0), jnp.sum(pre_b * pre_b, axis=0)])
            stat_means = small_sum(stat_sums) / row_count
            inv_a = lax.rsqrt(stat_means[1] - stat_means[0] * stat_means[0] + NORM_EPS)
            inv_b = lax.rsqrt(stat_means[3] - stat_means[2] * stat_means[2] + NORM_EPS)
            return (pre_a - stat_means[0]) * inv_a, inv_a, (pre_b - stat_means[2]) * inv_b

        def hidden_pair(in_a, in_b, weight_a, weight_b, gain_vec, bias_vec):
            normed_a, inv_a, normed_b = norm_pair(jnp.dot(in_a, weight_a, preferred_element_type=jnp.float32), jnp.dot(in_b, weight_b, preferred_element_type=jnp.float32))
            pre_act = normed_a * gain_vec + bias_vec
            act_a = jnp.maximum(pre_act, 0.0).astype(jnp.bfloat16)
            act_b = jnp.maximum(normed_b * gain_vec + bias_vec, 0.0).astype(jnp.bfloat16)
            return act_a, act_b, normed_a, inv_a, pre_act > 0.0

        def affine_back(grad_pre, normed, inv_std, gain_vec):
            stat_sums = small_sum(jnp.stack([jnp.sum(grad_pre * normed, axis=0), jnp.sum(grad_pre, axis=0)]))
            grad_u = (grad_pre - stat_sums[1] / row_count - normed * (stat_sums[0] / row_count)) * (gain_vec * inv_std)
            return grad_u.astype(jnp.bfloat16), stat_sums[0], stat_sums[1]

        act_1, teach_1, normed_1, inv_1, mask_1 = hidden_pair(feat_a, feat_b, w_in, t_in, gain_1, bias_1)
        act_2, teach_2, normed_2, inv_2, mask_2 = hidden_pair(act_1, teach_1, w_mid, t_mid, gain_2, bias_2)
        zh_a, inv_z, zh_b = norm_pair(jnp.dot(act_2, w_out, preferred_element_type=jnp.float32), jnp.dot(teach_2, t_out, preferred_element_type=jnp.float32))
        emb_a = zh_a.astype(jnp.bfloat16)
        emb_b = zh_b.astype(jnp.bfloat16)
        corr_part = contract_rows(emb_a, emb_b)
        grad_c, loss_cols = large_sum([corr_part], 8, (3, 7), CorrFinish(row_count), [off_weight.reshape(1)], 1)
        grad_emb = contract_cols(emb_b, grad_c) / row_count
        loss_row = jnp.sum(loss_cols, axis=0)
        stat_sums = small_sum(jnp.stack([jnp.sum(grad_emb, axis=0), jnp.sum(grad_emb * zh_a, axis=0), loss_row]))
        loss_value = jnp.sum(stat_sums[2]) * 0.5
        grad_z = ((grad_emb - stat_sums[0] / row_count - zh_a * (stat_sums[1] / row_count)) * inv_z).astype(jnp.bfloat16)
        grad_w_out = lax.psum(contract_rows(act_2, grad_z), DATA_AXIS)
        grad_pre_2 = jnp.where(mask_2, contract_cols(grad_z, w_out), 0.0)
        grad_u_2, grad_gain_2, grad_bias_2 = affine_back(grad_pre_2, normed_2, inv_2, gain_2)
        part_mid = contract_rows(act_1, grad_u_2)
        grad_pre_1 = jnp.where(mask_1, contract_cols(grad_u_2, w_mid), 0.0)
        grad_u_1, grad_gain_1, grad_bias_1 = affine_back(grad_pre_1, normed_1, inv_1, gain_1)
        part_in = contract_rows(feat_a, grad_u_1)
        grad_w_mid, grad_w_in = large_sum([part_mid, part_in], 8, (3, 7), PlainFinish, [], 2)
        return (loss_value, grad_emb, grad_w_in, grad_w_mid, grad_w_out, grad_gain_1, grad_bias_1, grad_gain_2, grad_bias_2)

    return jax.shard_map(local_step, mesh=mesh, in_specs=(row_part, row_part) + (replicated,) * 11, out_specs=(replicated, row_part) + (replicated,) * 7, check_vma=False)
```

time: 1450 us -> 825 us (0.57)
  waiting for transfers between devices: 989 us -> 0.04 us
  Pallas kernels: 0 us -> 614 us
  blocking collectives: 243 us -> 0 us
    psum x2 -> x1, waiting for transfers between devices: 989 us -> 0.02 us  [local_step(): grad_w_out = lax.psum(contract_rows(act_2, grad_z), DATA_AXIS)]
    pallas_call x0 -> x8, Pallas kernels: none -> 614 us  [the longest x2 529 us: large_sum(): pl.pallas_call(functools.partial(large_sum_kernel, mats, chunks, z_first,...]
    psum x6 -> x0, blocking collectives: 243 us -> none  [the longest x3 122 us: norm_pair(): stat_means = lax.psum(stat_sums, DATA_AXIS) / row_count]
    unnamed x25 -> x43, local copies, waits for them, and re-layouts: 40.2 us -> 33.7 us
  transfers between devices with their start and end apart: 2 -> 1, of which waited for: 2 -> 0; matrix products, arithmetic and copies ran while one was open for 1% -> 6% of each run, Pallas kernels for 0% -> 52%
where the time goes in v1:
time: 825 us; the launch traced here: 820 us
  Pallas kernels  614 us (74%)
  matrix products  135 us (16%)
  local copies, waits for them, and re-layouts  37.5 us (5%)
  between operations  17 us (2%)
  other arithmetic  15.9 us (2%)
    pallas_call x2, Pallas kernels, large_sum(): pl.pallas_call(functools.partial(large_sum_kernel, mats, chunks, z_first,...  529 us
    pallas_call x6, Pallas kernels, small_sum(): pl.pallas_call(small_sum_kernel, name='small_sum', out_shape=jax.ShapeDty...  84.9 us
    dot_general x4, matrix products, contract_rows(): lax.dot_general(left_op, right_op, (((0,), (0,)), ((), ())), preferred_el...  42.5 us
    unnamed x43, local copies, waits for them, and re-layouts  33.7 us
    dot_general x3, matrix products, contract_cols(): lax.dot_general(left_op, right_op, (((1,), (1,)), ((), ())), preferred_el...  33.7 us
    dot_general x2, matrix products, hidden_pair(): jnp.dot(in_a, weight_a, preferred_element_type=jnp.float32)  21.9 us
  transfers between devices with their start and end apart: 1, of which 0 were waited for; matrix products, arithmetic and copies ran while one was open for 6% of the time, Pallas kernels for 52%

profile of v1, /device:TPU:0, one launch (start us, length us, event | category | flops | bytes accessed | tf_op | source)
XLA Modules:
  0.0 819.9 jit_solution(15257470311167748407)
XLA Ops:
  7.2 10.7 %fusion.51 = (f32[2048]{0:T(1024)S(1)}, f32[2048]{0:T(1024)S(1)}, f32[512,2048]{1,0:T(8,128)}) fusion(bf16[512,2048]{1,0:T(8,128)(2,1)} %param.13, bf16[2048,2048]{1,0:T(8,128)(2,1)} %param.15), kind=kOutput, calls=%fused_computation.113 | convolution fusion | flops 4298108928 | bytes 14696448 | tf_op jit(solution)/shard_map/dot_general | solution.py:361
  18.0 6.3 fusion.52
  25.0 17.1 %small_sum.6 = f32[8,8,128]{2,1,0:T(8,128)} custom-call(f32[8,8,128]{2,1,0:T(8,128)} %reshape.172.x_ref), custom_call_target="tpu_custom_call" | custom-call | tf_op jit(solution)/shard_map/small_sum/pallas_call | solution.py:87
  42.9 11.2 %fusion.49 = (f32[2048]{0:T(1024)S(1)}, f32[2048]{0:T(1024)S(1)}, f32[512,2048]{1,0:T(8,128)}) fusion(bf16[2048,2048]{1,0:T(8,128)(2,1)} %param.16, f32[512,2048]{1,0:T(8,128)} %get-tuple-element.63, f32[2048]{0:T(1024)S(1)} %get-tuple-element.59, f32[2048]{0:T(1024)S(1)} %get-tuple-element.60, f32[2048]{0:T(1024)S(1)} %copy-done.9, f32[2048]{0:T(1024)S(1)} %copy-done.4), kind=kOutput, calls=%fused_computation.111 | convolution fusion | flops 4304400384 | bytes 16826368 | tf_op jit(solution)/shard_map/dot_general | solution.py:361
  54.1 9.6 %fusion.50 = (f32[2048]{0:T(1024)S(1)}, f32[2048]{0:T(1024)S(1)}, f32[512,2048]{1,0:T(8,128)}) fusion(bf16[2048,2048]{1,0:T(8,128)(2,1)} %param.19, f32[512,2048]{1,0:T(8,128)S(1)} %copy-done.13, f32[2048]{0:T(1024)S(1)} %copy-done.9, f32[2048]{0:T(1024)S(1)} %copy-done.4, f32[2048]{0:T(1024)S(1)} %get-tuple-element.61, f32[2048]{0:T(1024)S(1)} %get-tuple-element.58), kind=kOutput, calls=%fused_computation.112 | convolution fusion | flops 4304400384 | bytes 16826368 | tf_op jit(solution)/shard_map/dot_general | solution.py:361
  64.3 13.4 %small_sum.7 = f32[8,8,128]{2,1,0:T(8,128)} custom-call(f32[8,8,128]{2,1,0:T(8,128)} %reshape.173.x_ref), custom_call_target="tpu_custom_call" | custom-call | tf_op jit(solution)/shard_map/small_sum/pallas_call | solution.py:87
  78.6 11.3 %fusion.47 = (f32[2048]{0:T(1024)S(1)}, f32[2048]{0:T(1024)S(1)}, f32[512,2048]{1,0:T(8,128)}) fusion(bf16[2048,2048]{1,0:T(8,128)(2,1)} %param.17, f32[512,2048]{1,0:T(8,128)} %get-tuple-element.65, f32[2048]{0:T(1024)S(1)} %get-tuple-element.55, f32[2048]{0:T(1024)S(1)} %get-tuple-element.56, f32[2048]{0:T(1024)S(1)} %copy-done.8, f32[2048]{0:T(1024)S(1)} %copy-done.2), kind=kOutput, calls=%fused_computation.109 | convolution fusion | flops 4304400384 | bytes 16826368 | tf_op jit(solution)/shard_map/dot_general | solution.py:374
  89.9 10.0 %fusion.48 = (f32[2048]{0:T(1024)S(1)}, f32[2048]{0:T(1024)S(1)}, f32[512,2048]{1,0:T(8,128)}) fusion(bf16[2048,2048]{1,0:T(8,128)(2,1)} %param.20, f32[512,2048]{1,0:T(8,128)S(1)} %copy-done.14, f32[2048]{0:T(1024)S(1)} %copy-done.8, f32[2048]{0:T(1024)S(1)} %copy-done.2, f32[2048]{0:T(1024)S(1)} %get-tuple-element.57, f32[2048]{0:T(1024)S(1)} %get-tuple-element.54), kind=kOutput, calls=%fused_computation.110 | convolution fusion | flops 4304400384 | bytes 16826368 | tf_op jit(solution)/shard_map/dot_general | solution.py:374
  100.6 13.4 %small_sum.8 = f32[8,8,128]{2,1,0:T(8,128)} custom-call(f32[8,8,128]{2,1,0:T(8,128)} %reshape.174.x_ref), custom_call_target="tpu_custom_call" | custom-call | tf_op jit(solution)/shard_map/small_sum/pallas_call | solution.py:87
  115.5 14.2 %fusion.1.refs_0_ = f32[2048,2048]{1,0:T(8,128)} fusion(f32[512,2048]{1,0:T(8,128)} %get-tuple-element.67, f32[2048]{0:T(1024)S(1)} %get-tuple-element.51, f32[2048]{0:T(1024)S(1)} %get-tuple-element.52, f32[512,2048]{1,0:T(8,128)} %get-tuple-element.66, f32[2048]{0:T(1024)S(1)} %get-tuple-element.53, f32[2048]{0:T(1024)S(1)} %get-tuple-element.50), kind=kOutput, calls=%fused_computation.27 | convolution fusion | flops 4301258752 | bytes 25198592 | tf_op jit(solution)/shard_map/dot_general | solution.py:21
  129.7 128.8 %large_sum.2 = (bf16[2048,2048]{1,0:T(8,128)(2,1)}, f32[1,2048]{1,0:T(1,128)}) custom-call(f32[2048,2048]{1,0:T(8,128)} %fusion.1.refs_0_, f32[1]{0:T(128)} %bitcast.109.refs_1_), custom_call_target="tpu_custom_call" | custom-call | tf_op jit(solution)/shard_map/large_sum/pallas_call | solution.py:322
  258.6 12.6 %fusion.46 = (f32[2048]{0:T(1024)S(1)}, f32[2048]{0:T(1024)S(1)}, f32[512,2048]{1,0:T(8,128)}) fusion(f32[2048]{0:T(1024)S(1)} %get-tuple-element.51, f32[512,2048]{1,0:T(8,128)} %get-tuple-element.67, f32[2048]{0:T(1024)S(1)} %get-tuple-element.52, bf16[2048,2048]{1,0:T(8,128)(2,1)} %get-tuple-element.13, f32[512,2048]{1,0:T(8,128)} %get-tuple-element.66, ...), kind=kOutput, calls=%fused_computation.108 | convolution fusion | flops 4304400384 | bytes 21020672 | tf_op jit(solution)/shard_map/dot_general | solution.py:25
  271.8 13.3 %small_sum.9 = f32[8,8,128]{2,1,0:T(8,128)} custom-call(f32[8,8,128]{2,1,0:T(8,128)} %pad_bitcast_fusion.2.x_ref), custom_call_target="tpu_custom_call" | custom-call | tf_op jit(solution)/shard_map/small_sum/pallas_call | solution.py:87
  285.2 1.3 multiply_bitcast_fusion.1
  286.5 4.7 multiply_convert_fusion.2
  291.3 8.6 %fusion.44 = f32[2048,2048]{1,0:T(8,128)} fusion(bf16[512,2048]{1,0:T(8,128)(2,1)S(1)} %multiply_convert_fusion.2, f32[512,2048]{1,0:T(8,128)S(1)} %copy-done.1, f32[2048]{0:T(1024)S(1)} %get-tuple-element.55, f32[2048]{0:T(1024)S(1)} %get-tuple-element.56, f32[2048]{0:T(1024)S(1)} %copy-done.8, f32[2048]{0:T(1024)S(1)} %copy-done.2), kind=kOutput, calls=%fused_computation.106 | convolution fusion | flops 4301258752 | bytes 23101440 | tf_op jit(solution)/shard_map/dot_general | solution.py:21
  299.9 10.9 %multiply_reduce_fusion.1 = (f32[2048]{0:T(1024)S(1)}, f32[2048]{0:T(1024)S(1)}, f32[512,2048]{1,0:T(8,128)}) fusion(f32[512,2048]{1,0:T(8,128)} %get-tuple-element.65, f32[2048]{0:T(1024)S(1)} %get-tuple-element.55, f32[2048]{0:T(1024)S(1)} %get-tuple-element.56, bf16[512,2048]{1,0:T(8,128)(2,1)S(1)} %multiply_convert_fusion.2, ...), kind=kOutput, calls=%fused_computation.4 | convolution fusion | flops 4304400384 | bytes 18923520 | tf_op jit(solution)/shard_map/dot_general | solution.py:25
  311.5 13.8 %small_sum.10 = f32[8,8,128]{2,1,0:T(8,128)} custom-call(f32[8,8,128]{2,1,0:T(8,128)} %pad_bitcast_fusion.1.x_ref), custom_call_target="tpu_custom_call" | custom-call | tf_op jit(solution)/shard_map/small_sum/pallas_call | solution.py:87
  325.3 1.3 broadcast_multiply_fusion.6
  326.6 4.7 multiply_convert_fusion.1
  331.4 10.2 %multiply_reduce_fusion = (f32[2048]{0:T(1024)S(1)}, f32[2048]{0:T(1024)S(1)}, f32[512,2048]{1,0:T(8,128)}) fusion(f32[512,2048]{1,0:T(8,128)S(1)} %copy-done.10, f32[2048]{0:T(1024)S(1)} %get-tuple-element.59, f32[2048]{0:T(1024)S(1)} %get-tuple-element.60, bf16[512,2048]{1,0:T(8,128)(2,1)S(1)} %multiply_convert_fusion.1, bf16[2048,2048]{1,0:T(8,128)(2,1)} %param.16, ...), kind=kOutput, calls=%fused_computation.2 | convolution fusion | flops 4304400384 | bytes 18923520 | tf_op jit(solution)/shard_map/dot_general | solution.py:25
  342.2 13.8 %small_sum.11 = f32[8,8,128]{2,1,0:T(8,128)} custom-call(f32[8,8,128]{2,1,0:T(8,128)} %pad_bitcast_fusion.x_ref), custom_call_target="tpu_custom_call" | custom-call | tf_op jit(solution)/shard_map/small_sum/pallas_call | solution.py:87
  356.0 1.3 broadcast_multiply_fusion.4
  357.3 10.9 %fusion.42.refs_0_ = f32[2048,2048]{1,0:T(8,128)} fusion(bf16[512,2048]{1,0:T(8,128)(2,1)S(1)} %multiply_convert_fusion.1, f32[512,2048]{1,0:T(8,128)} %get-tuple-element.63, f32[2048]{0:T(1024)S(1)} %get-tuple-element.59, f32[2048]{0:T(1024)S(1)} %get-tuple-element.60, f32[2048]{0:T(1024)S(1)} %copy-done.9, f32[2048]{0:T(1024)S(1)} %copy-done.4), kind=kOutput, calls=%fused_computation.104 | convolution fusion | flops 4301258752 | bytes 23101440 | tf_op jit(solution)/shard_map/dot_general | solution.py:21
  368.3 8.8 %convolution_bitcast_fusion.refs_1_ = f32[2048,2048]{1,0:T(8,128)} fusion(bf16[512,2048]{1,0:T(8,128)(2,1)S(1)} %copy-done.7, f32[512,2048]{1,0:T(8,128)S(1)} %copy-done.12, f32[512,2048]{1,0:T(8,128)S(1)} %copy-done.11, f32[2048]{0:T(1024)S(1)} %fusion.36, f32[2048]{0:T(1024)S(1)} %get-tuple-element.43, f32[2048]{0:T(1024)S(1)} %get-tuple-element.35, ...), kind=kOutput, calls=%fused_computation | convolution fusion | flops 4302307328 | bytes 27303936 | tf_op jit(solution)/shard_map/dot_general | solution.py:21
  377.1 400.3 %large_sum.3 = (f32[2048,2048]{1,0:T(8,128)}, f32[2048,2048]{1,0:T(8,128)}) custom-call(f32[2048,2048]{1,0:T(8,128)} %fusion.42.refs_0_, f32[2048,2048]{1,0:T(8,128)} %convolution_bitcast_fusion.refs_1_), custom_call_target="tpu_custom_call" | custom-call | tf_op jit(solution)/shard_map/large_sum/pallas_call | solution.py:322
  778.1 13.5 %copy.30 = f32[2048,2048]{1,0:T(8,128)} copy(f32[2048,2048]{1,0:T(8,128)} %get-tuple-element.83) | data formatting | bytes 33554432
  791.6 2.9 copy-done
  794.5 8.5 %copy.31 = f32[2048,2048]{1,0:T(8,128)} copy(f32[2048,2048]{1,0:T(8,128)S(1)} %copy-done) | data formatting | bytes 33554432
  803.0 1.4 slice-done.2
  804.3 1.2 slice-done.3
  805.5 6.2 copy.32
  (61 shorter events, 6.4 us)
Async XLA Ops:
  7.2 10.8 %copy-start.6 = (bf16[512,2048]{1,0:T(8,128)(2,1)S(1)}, bf16[512,2048]{1,0:T(8,128)(2,1)}, u32[]{:S(2)}) copy-start(bf16[512,2048]{1,0:T(8,128)(2,1)} %param.14) | copy-start | bytes 6291460
  7.2 770.8 %all-reduce.5.cloned.1.call-start = ((), (), s32[]{:S(2)}) async-start(), calls=%async_computation | async-start | bytes 33554432 | tf_op jit(solution)/shard_map/psum | solution.py:384
  7.2 10.7 %copy-start.5 = (bf16[2048,2048]{1,0:T(8,128)(2,1)S(1)}, bf16[2048,2048]{1,0:T(8,128)(2,1)}, u32[]{:S(2)}) copy-start(bf16[2048,2048]{1,0:T(8,128)(2,1)} %param.18) | copy-start | bytes 25165828
  17.9 24.9 %copy-start.4 = (f32[2048]{0:T(1024)S(1)}, f32[2048]{0:T(1024)}, u32[]{:S(2)}) copy-start(f32[2048]{0:T(1024)} %param.21) | copy-start | bytes 24580
  17.9 24.9 %copy-start.9 = (f32[2048]{0:T(1024)S(1)}, f32[2048]{0:T(1024)}, u32[]{:S(2)}) copy-start(f32[2048]{0:T(1024)} %param.22) | copy-start | bytes 24580
  42.8 11.3 %copy-start.13 = (f32[512,2048]{1,0:T(8,128)S(1)}, f32[512,2048]{1,0:T(8,128)}, u32[]{:S(2)}) copy-start(f32[512,2048]{1,0:T(8,128)} %get-tuple-element.62) | copy-start | bytes 12582916
  54.1 24.5 %copy-start.2 = (f32[2048]{0:T(1024)S(1)}, f32[2048]{0:T(1024)}, u32[]{:S(2)}) copy-start(f32[2048]{0:T(1024)} %param.23) | copy-start | bytes 24580
  54.1 24.5 %copy-start.8 = (f32[2048]{0:T(1024)S(1)}, f32[2048]{0:T(1024)}, u32[]{:S(2)}) copy-start(f32[2048]{0:T(1024)} %param.24) | copy-start | bytes 24580
  78.6 11.3 %copy-start.14 = (f32[512,2048]{1,0:T(8,128)S(1)}, f32[512,2048]{1,0:T(8,128)}, u32[]{:S(2)}) copy-start(f32[512,2048]{1,0:T(8,128)} %get-tuple-element.64) | copy-start | bytes 12582916
  258.6 12.6 %copy-start.3 = (f32[1,2048]{1,0:T(1,128)S(1)}, f32[1,2048]{1,0:T(1,128)}, u32[]{:S(2)}) copy-start(f32[1,2048]{1,0:T(1,128)} %get-tuple-element.14) | copy-start | bytes 24580
  286.5 4.7 copy-start.1
  326.6 4.7 copy-start.10
  357.3 10.9 %copy-start.7 = (bf16[512,2048]{1,0:T(8,128)(2,1)S(1)}, bf16[512,2048]{1,0:T(8,128)(2,1)}, u32[]{:S(2)}) copy-start(bf16[512,2048]{1,0:T(8,128)(2,1)} %param.13) | copy-start | bytes 6291460
  357.3 10.9 %copy-start.11 = (f32[512,2048]{1,0:T(8,128)S(1)}, f32[512,2048]{1,0:T(8,128)}, u32[]{:S(2)}) copy-start(f32[512,2048]{1,0:T(8,128)} %get-tuple-element.63) | copy-start | bytes 12582916
  357.3 10.9 %copy-start.12 = (f32[512,2048]{1,0:T(8,128)S(1)}, f32[512,2048]{1,0:T(8,128)}, u32[]{:S(2)}) copy-start(f32[512,2048]{1,0:T(8,128)} %get-tuple-element.70) | copy-start | bytes 12582916
  778.0 16.4 %copy-start = (f32[2048,2048]{1,0:T(8,128)S(1)}, f32[2048,2048]{1,0:T(8,128)}, u32[]{:S(2)}) copy-start(f32[2048,2048]{1,0:T(8,128)} %get-tuple-element.84) | copy-start | bytes 50331652
  778.0 24.9 %slice-start = ((s8[16777216]{0:T(1024)(128)(4,1)}), s8[4194304]{0:T(1024)(128)(4,1)S(1)}, s32[]{:S(2)}) async-start(s8[16777216]{0:T(1024)(128)(4,1)} %bitcast.110), calls=%async_computation.1 | async-start | bytes 8388608
  778.1 24.9 %slice-start.1 = ((s8[16777216]{0:T(1024)(128)(4,1)}), s8[4194304]{0:T(1024)(128)(4,1)S(1)}, s32[]{:S(2)}) async-start(s8[16777216]{0:T(1024)(128)(4,1)} %bitcast.110), calls=%async_computation.2 | async-start | bytes 8388608
  794.5 9.9 %slice-start.2 = ((s8[16777216]{0:T(1024)(128)(4,1)}), s8[4194304]{0:T(1024)(128)(4,1)S(1)}, s32[]{:S(2)}) async-start(s8[16777216]{0:T(1024)(128)(4,1)} %bitcast.110), calls=%async_computation.3 | async-start | bytes 8388608
  794.5 11.1 %slice-start.3 = ((s8[16777216]{0:T(1024)(128)(4,1)}), s8[4194304]{0:T(1024)(128)(4,1)S(1)}, s32[]{:S(2)}) async-start(s8[16777216]{0:T(1024)(128)(4,1)} %bitcast.110), calls=%async_computation.4 | async-start | bytes 8388608
Sparse Core Ops, SparseCore 0:
  300.0 428.3 all-reduce.4

commit v2 on v1

--- a/solution.py
+++ b/solution.py
@@ -342,6 +342,418 @@
     )(*arrays, *extra)
 
 
+PARTS = 8
+MATS = 3
+SLOTS = 12
+TILE = 256
+BACK_LAGS = (0, 1, 3, 5, 6, 7, 8, 9, 11, 13)
+Z_FIRST = (3, 7)
+
+
+def back_kernel(dz_hbm, xt2, xt1, xt0, w_out, w_mid, u2, u1, vec, out2, out1, out0, sums, *scratch):
+    (dy_own, dy_peer, xt_own, xt_peer, w_buf, u_buf, dpre, payload, plane_buf, depth_buf, own_buf) = scratch[:11]
+    (acc, gathered, rx, ry, rz, rl) = scratch[11:17]
+    (in_sem, tile_sem, peer_send, peer_recv, s1, r1, s2, r2, s3, r3, store_sem, send, recv) = scratch[17:]
+    rows_dev, width = dz_hbm.shape
+    tiles = width // TILE
+    row_count = rows_dev * 4 * PLANE
+    part_rows = width // 2 // PARTS
+    count = MATS * PARTS
+    xts, outs, weights, pres = (xt2, xt1, xt0), (out2, out1, out0), (w_out, w_mid), (u2, u1)
+
+    me = lax.axis_index(DATA_AXIS)
+    pos, plane = me % PLANE, me // PLANE
+    core, bx, by, bz0, bz1 = me % 2, (me // 2) % 2, (me // 4) % 2, (me // 8) % 2, (me // 16) % 2
+    other_core = me + 1 - 2 * core
+    mates = [(pos + d) % PLANE for d in range(1, PLANE)]
+    levels = [(plane + d) % DEPTH for d in range(1, DEPTH)]
+    peers = [plane * PLANE + m for m in mates] + [lv * PLANE + pos for lv in levels]
+
+    def rows(off, size):
+        return pl.ds(pl.multiple_of(off, size), size)
+
+    def cols(i, size=TILE):
+        return pl.ds(pl.multiple_of(i * size, size), size)
+
+    barrier = pltpu.get_barrier_semaphore()
+    signal_all(barrier, peers)
+
+    half = width // 2
+
+    def own_xt(w):
+        return pltpu.make_async_copy(xts[w].at[rows(core * half, half)], xt_own.at[w], in_sem.at[w])
+
+    dz_load = pltpu.make_async_copy(dz_hbm, dy_own.at[0], in_sem.at[MATS])
+
+    def peer_xt(w):
+        return pltpu.make_async_remote_copy(
+            xts[w].at[rows((1 - core) * half, half)], xt_peer.at[w], peer_send.at[w], peer_recv.at[w], device_id=(other_core,), device_id_type=MESH
+        )
+
+    def peer_dy(w):
+        src = dz_hbm if w == 0 else dy_own.at[w % 2]
+        return pltpu.make_async_remote_copy(
+            src, dy_peer.at[w % 2], peer_send.at[MATS + w], peer_recv.at[MATS + w], device_id=(other_core,), device_id_type=MESH
+        )
+
+    def w_tile(layer, i):
+        return pltpu.make_async_copy(weights[layer].at[cols(i)], w_buf.at[i % 2], tile_sem.at[0, i % 2])
+
+    def u_tile(layer, i):
+        return pltpu.make_async_copy(pres[layer].at[:, cols(i)], u_buf.at[i % 2], tile_sem.at[1, i % 2])
+
+    dz_load.start()
+    w_tile(0, 0).start()
+    u_tile(0, 0).start()
+    for w in range(MATS):
+        own_xt(w).start()
+    pl.semaphore_wait(barrier, len(peers))
+    peer_dy(0).start()
+    for w in range(MATS):
+        peer_xt(w).start()
+    dz_load.wait()
+
+    def vec_row(layer, which, i):
+        return vec[layer * 4 + which : layer * 4 + which + 1, cols(i)]
+
+    BLOCK = 64
+
+    def row_loop(body, carry):
+        return lax.fori_loop(0, rows_dev // BLOCK, lambda r, c: body(rows(r * BLOCK, BLOCK), c), carry)
+
+    def chain(layer):
+        def tile(i, carry):
+            w_tile(layer, i).wait()
+            u_tile(layer, i).wait()
+
+            @pl.when(i + 1 < tiles)
+            def _():
+                w_tile(layer, i + 1).start()
+                u_tile(layer, i + 1).start()
+
+            dpre[:, cols(i)] = contract_cols(dy_own[layer], w_buf[i % 2])
+            gain, bias, mean, inv = (vec_row(layer, j, i) for j in range(4))
+
+            def block(at, sums2):
+                n = (u_buf[i % 2, at] - mean) * inv
+                g = jnp.where(n * gain + bias > 0.0, dpre[at, cols(i)], 0.0)
+                dpre[at, cols(i)] = g
+                gn = g * n
+                return tuple(
+                    s + jnp.sum(v.reshape(BLOCK // 8, 8, TILE), axis=0) for s, v in zip(sums2, (gn, g))
+                )
+
+            zero = jnp.zeros((8, TILE), jnp.float32)
+            sn, sg = row_loop(block, (zero, zero))
+            payload[layer, i, 0:1] = jnp.sum(sn, axis=0, keepdims=True)
+            payload[layer, i, 1:2] = jnp.sum(sg, axis=0, keepdims=True)
+            return carry
+
+        lax.fori_loop(0, tiles, tile, 0)
+
+    def du(layer):
+        u_tile(layer, 0).start()
+
+        def tile(i, carry):
+            u_tile(layer, i).wait()
+
+            @pl.when(i + 1 < tiles)
+            def _():
+                u_tile(layer, i + 1).start()
+
+            gain, mean, inv = vec_row(layer, 0, i), vec_row(layer, 2, i), vec_row(layer, 3, i)
+            mean_gn = sums[layer, i, 0:1] / row_count
+            mean_g = sums[layer, i, 1:2] / row_count
+            scale = gain * inv
+
+            def block(at, c):
+                n = (u_buf[i % 2, at] - mean) * inv
+                dy_own[1 - layer, at, cols(i)] = ((dpre[at, cols(i)] - mean_g - n * mean_gn) * scale).astype(jnp.bfloat16)
+                return c
+
+            row_loop(block, 0)
+            return carry
+
+        lax.fori_loop(0, tiles, tile, 0)
+
+    def plane_copy(src, dst, send_sem, recv_sem, mate):
+        return pltpu.make_async_remote_copy(src, dst, send_sem, recv_sem, device_id=(plane * PLANE + mate,), device_id_type=MESH)
+
+    def first(layer, m, slot):
+        return plane_copy(payload.at[layer, m], plane_buf.at[layer, slot], s1.at[layer, m], r1.at[layer, slot], m)
+
+    def second(layer, lv, slot):
+        return pltpu.make_async_remote_copy(
+            own_buf.at[layer, 0], depth_buf.at[layer, slot], s2.at[layer, lv], r2.at[layer, slot], device_id=(lv * PLANE + pos,), device_id_type=MESH
+        )
+
+    def third(layer, m, slot):
+        return plane_copy(own_buf.at[layer, 1], sums.at[layer, slot], s3.at[layer, m], r3.at[layer, slot], m)
+
+    def small_begin(layer):
+        for m in mates:
+            first(layer, m, pos).start()
+        plane_buf[layer, pos] = payload[layer, pos]
+
+    def small_middle(layer):
+        for m in mates:
+            first(layer, m, m).wait_recv()
+        total = plane_buf[layer, 0]
+        for i in range(1, PLANE):
+            total = total + plane_buf[layer, i]
+        own_buf[layer, 0] = total
+        depth_buf[layer, plane] = total
+        for lv in levels:
+            second(layer, lv, plane).start()
+
+    def small_last(layer):
+        for lv in levels:
+            second(layer, lv, lv).wait_recv()
+        total = depth_buf[layer, 0]
+        for i in range(1, DEPTH):
+            total = total + depth_buf[layer, i]
+        own_buf[layer, 1] = total
+        sums[layer, pos] = total
+        for m in mates:
+            third(layer, m, pos).start()
+
+    def small_end(layer):
+        for m in mates:
+            third(layer, m, m).wait_recv()
+            first(layer, m, pos).wait_send()
+            third(layer, m, pos).wait_send()
+        for lv in levels:
+            second(layer, lv, plane).wait_send()
+
+    xy = ((2 + 2 * core, core * by + (1 - core) * bx), (4 - 2 * core, core * bx + (1 - core) * by))
+    zz = ((8, bz0), (16, bz1))
+
+    def steps_of(k):
+        part = k % PARTS
+        zf = 0
+        for z in Z_FIRST:
+            same = part - z
+            zf = zf + (1 - lax.min(same * same, 1))
+        pairs = []
+        for a, b in zip(xy + zz, zz + xy):
+            stride = zf * b[0] + (1 - zf) * a[0]
+            bit = zf * b[1] + (1 - zf) * a[1]
+            pairs.append((me + stride * (1 - 2 * bit), bit))
+        offs, size = [0], part_rows
+        for _, bit in pairs[:3]:
+            size = size // 2
+            offs.append(offs[-1] + bit * size)
+        return pairs, offs
+
+    landing = (rx, ry, rz, rl)
+
+    def remote(src, dst, stage, k, mate):
+        return pltpu.make_async_remote_copy(src, dst, send.at[stage, k], recv.at[stage, k], device_id=(mate,), device_id_type=MESH)
+
+    def reduce_copy(i, k, pairs, offs):
+        size = part_rows >> (i + 1)
+        if i == 3:
+            size = part_rows >> 3
+            off = offs[3]
+        else:
+            off = offs[i] + (1 - pairs[i][1]) * size
+        return remote(acc.at[k % SLOTS, rows(off, size)], landing[i].at[k % SLOTS], i, k, pairs[i][0])
+
+    def gather_copy(i, k, pairs, offs):
+        block = gathered.at[k % SLOTS, rows(offs[i + 1], part_rows >> (i + 1))]
+        return remote(block, block, 6 - i, k, pairs[i][0])
+
+    def out_rows(k, side):
+        return pl.ds(pl.multiple_of(side * half + (k % PARTS) * part_rows, part_rows), part_rows)
+
+    def last_copy(w, k, side):
+        return remote(gathered.at[k % SLOTS], outs[w].at[out_rows(k, side)], 7, k, other_core)
+
+    def store_copy(w, k):
+        return pltpu.make_async_copy(gathered.at[k % SLOTS], outs[w].at[out_rows(k, core)], store_sem.at[k])
+
+    def add_rows(dst, k, off, size, buf):
+        step = min(size, 16)
+        j = k % SLOTS
+
+        def body(i, carry):
+            at = rows(off + i * step, step)
+            dst[j, at] = acc[j, at] + buf[j, rows(i * step, step)]
+            return carry
+
+        lax.fori_loop(0, size // step, body, 0)
+
+    def for_mat(k, what):
+        for w in range(MATS):
+            pl.when(k // PARTS == w)(functools.partial(what, w))
+
+    def form(k):
+        w, j = k // PARTS, k % SLOTS
+        at = rows((k % PARTS) * part_rows, part_rows)
+        step = min(512, width)
+
+        def col(c, carry):
+            cs = cols(c, step)
+            acc[j, :, cs] = jnp.dot(xt_own[w, at], dy_own[w % 2, :, cs], preferred_element_type=jnp.float32) + jnp.dot(
+                xt_peer[w, at], dy_peer[w % 2, :, cs], preferred_element_type=jnp.float32
+            )
+            return carry
+
+        lax.fori_loop(0, width // step, col, 0)
+
+    def stage(i, k):
+        pairs, offs = steps_of(k)
+        if i == 0:
+
+            @pl.when(k == 2 * PARTS)
+            def _():
+                peer_dy(2).wait_recv()
+
+            form(k)
+        elif i == 1:
+            reduce_copy(0, k, pairs, offs).start()
+        elif i < 5:
+            reduce_copy(i - 2, k, pairs, offs).wait_recv()
+            add_rows(acc, k, offs[i - 1], part_rows >> (i - 1), landing[i - 2])
+            reduce_copy(i - 1, k, pairs, offs).start()
+        elif i == 5:
+            reduce_copy(3, k, pairs, offs).wait_recv()
+            add_rows(gathered, k, offs[3], part_rows >> 3, rl)
+            gather_copy(2, k, pairs, offs).start()
+        elif i < 8:
+            gather_copy(8 - i, k, pairs, offs).wait_recv()
+            gather_copy(7 - i, k, pairs, offs).start()
+            if i == 6:
+                for n in range(4):
+                    reduce_copy(n, k, pairs, offs).wait_send()
+        elif i == 8:
+            gather_copy(0, k, pairs, offs).wait_recv()
+
+            def emit(w):
+                last_copy(w, k, core).start()
+                store_copy(w, k).start()
+
+            for_mat(k, emit)
+        else:
+
+            def close(w):
+                last_copy(w, k, 1 - core).wait_recv()
+                store_copy(w, k).wait()
+                last_copy(w, k, core).wait_send()
+
+            for_mat(k, close)
+            for n in range(3):
+                gather_copy(n, k, pairs, offs).wait_send()
+
+    def chunk_loop(first_k, last_k, i):
+        def body(k, carry):
+            stage(i, k)
+            return carry
+
+        lax.fori_loop(first_k, last_k, body, 0)
+
+    ready = {0: SLOTS, 1: 2}
+
+    def slot(t, carry):
+        for i in ORDER:
+            k = t - BACK_LAGS[i]
+
+            @pl.when((k >= ready.get(i, 0)) & (k < count))
+            def _():
+                stage(i, k)
+
+        return carry
+
+    chain(0)
+    w_tile(1, 0).start()
+    small_begin(0)
+    for w in range(MATS):
+        own_xt(w).wait()
+        peer_xt(w).wait_recv()
+    peer_dy(0).wait_recv()
+    chunk_loop(0, PARTS // 2, 0)
+    small_middle(0)
+    chunk_loop(PARTS // 2, PARTS, 0)
+    small_last(0)
+    chunk_loop(0, 2, 1)
+    small_end(0)
+    du(0)
+    peer_dy(1).start()
+    u_tile(1, 0).start()
+    chain(1)
+    small_begin(1)
+    peer_dy(1).wait_recv()
+    chunk_loop(PARTS, PARTS + 2, 0)
+    small_middle(1)
+    chunk_loop(PARTS + 2, SLOTS, 0)
+    small_last(1)
+    slot(3, 0)
+    small_end(1)
+    peer_dy(0).wait_send()
+    du(1)
+    peer_dy(2).start()
+    lax.fori_loop(4, count + BACK_LAGS[-1], slot, 0)
+    for w in range(MATS):
+        peer_xt(w).wait_send()
+    peer_dy(1).wait_send()
+    peer_dy(2).wait_send()
+
+
+def backward(grad_z, xt2, xt1, xt0, w_out, w_mid, u2, u1, vec):
+    rows_dev, width = grad_z.shape
+    tiles = width // TILE
+    part_rows = width // 2 // PARTS
+    count = MATS * PARTS
+    any_spec = pl.BlockSpec(memory_space=pl.ANY)
+    vmem_spec = pl.BlockSpec(memory_space=pltpu.VMEM)
+    mat = jax.ShapeDtypeStruct((width, width), jnp.float32)
+
+    def slots(n):
+        return pltpu.VMEM((SLOTS, n, width), jnp.float32)
+
+    dma = pltpu.SemaphoreType.DMA
+    return pl.pallas_call(
+        back_kernel,
+        name="backward",
+        out_shape=[mat, mat, mat, jax.ShapeDtypeStruct((2, tiles, 2, TILE), jnp.float32)],
+        in_specs=[any_spec] * 8 + [vmem_spec],
+        out_specs=[any_spec] * 3 + [vmem_spec],
+        scratch_shapes=[
+            pltpu.VMEM((2, rows_dev, width), jnp.bfloat16),
+            pltpu.VMEM((2, rows_dev, width), jnp.bfloat16),
+            pltpu.VMEM((MATS, width // 2, rows_dev), jnp.bfloat16),
+            pltpu.VMEM((MATS, width // 2, rows_dev), jnp.bfloat16),
+            pltpu.VMEM((2, TILE, width), jnp.bfloat16),
+            pltpu.VMEM((2, rows_dev, TILE), jnp.float32),
+            pltpu.VMEM((rows_dev, width), jnp.float32),
+            pltpu.VMEM((2, tiles, 2, TILE), jnp.float32),
+            pltpu.VMEM((2, PLANE, 2, TILE), jnp.float32),
+            pltpu.VMEM((2, DEPTH, 2, TILE), jnp.float32),
+            pltpu.VMEM((2, 2, 2, TILE), jnp.float32),
+            slots(part_rows),
+            slots(part_rows),
+            slots(part_rows // 2),
+            slots(part_rows // 4),
+            slots(part_rows // 8),
+            slots(part_rows // 8),
+            dma((MATS + 1,)),
+            dma((2, 2)),
+            dma((2 * MATS,)),
+            dma((2 * MATS,)),
+            dma((2, PLANE)),
+            dma((2, PLANE)),
+            dma((2, DEPTH)),
+            dma((2, DEPTH)),
+            dma((2, PLANE)),
+            dma((2, PLANE)),
+            dma((count,)),
+            dma((8, count)),
+            dma((8, count)),
+        ],
+        compiler_params=pltpu.CompilerParams(collective_id=2, has_side_effects=True, vmem_limit_bytes=VMEM_BYTES),
+    )(grad_z, xt2, xt1, xt0, w_out, w_mid, u2, u1, vec)
+
+
 def solution(mesh):
     shards = mesh.shape[DATA_AXIS]
     row_part = P(DATA_AXIS, None)
@@ -355,23 +767,19 @@
             stat_means = small_sum(stat_sums) / row_count
             inv_a = lax.rsqrt(stat_means[1] - stat_means[0] * stat_means[0] + NORM_EPS)
             inv_b = lax.rsqrt(stat_means[3] - stat_means[2] * stat_means[2] + NORM_EPS)
-            return (pre_a - stat_means[0]) * inv_a, inv_a, (pre_b - stat_means[2]) * inv_b
+            return (pre_a - stat_means[0]) * inv_a, (pre_b - stat_means[2]) * inv_b, stat_means[0], inv_a
 
         def hidden_pair(in_a, in_b, weight_a, weight_b, gain_vec, bias_vec):
-            normed_a, inv_a, normed_b = norm_pair(jnp.dot(in_a, weight_a, preferred_element_type=jnp.float32), jnp.dot(in_b, weight_b, preferred_element_type=jnp.float32))
-            pre_act = normed_a * gain_vec + bias_vec
-            act_a = jnp.maximum(pre_act, 0.0).astype(jnp.bfloat16)
+            pre_a = jnp.dot(in_a, weight_a, preferred_element_type=jnp.float32)
+            normed_a, normed_b, mean_a, inv_a = norm_pair(pre_a, jnp.dot(in_b, weight_b, preferred_element_type=jnp.float32))
+            act_a = jnp.maximum(normed_a * gain_vec + bias_vec, 0.0).astype(jnp.bfloat16)
             act_b = jnp.maximum(normed_b * gain_vec + bias_vec, 0.0).astype(jnp.bfloat16)
-            return act_a, act_b, normed_a, inv_a, pre_act > 0.0
-
-        def affine_back(grad_pre, normed, inv_std, gain_vec):
-            stat_sums = small_sum(jnp.stack([jnp.sum(grad_pre * normed, axis=0), jnp.sum(grad_pre, axis=0)]))
-            grad_u = (grad_pre - stat_sums[1] / row_count - normed * (stat_sums[0] / row_count)) * (gain_vec * inv_std)
-            return grad_u.astype(jnp.bfloat16), stat_sums[0], stat_sums[1]
-
-        act_1, teach_1, normed_1, inv_1, mask_1 = hidden_pair(feat_a, feat_b, w_in, t_in, gain_1, bias_1)
-        act_2, teach_2, normed_2, inv_2, mask_2 = hidden_pair(act_1, teach_1, w_mid, t_mid, gain_2, bias_2)
-        zh_a, inv_z, zh_b = norm_pair(jnp.dot(act_2, w_out, preferred_element_type=jnp.float32), jnp.dot(teach_2, t_out, preferred_element_type=jnp.float32))
+            return act_a, act_b, pre_a, [gain_vec, bias_vec, mean_a, inv_a]
+
+        act_1, teach_1, pre_1, vec_1 = hidden_pair(feat_a, feat_b, w_in, t_in, gain_1, bias_1)
+        act_2, teach_2, pre_2, vec_2 = hidden_pair(act_1, teach_1, w_mid, t_mid, gain_2, bias_2)
+        pre_z = jnp.dot(act_2, w_out, preferred_element_type=jnp.float32)
+        zh_a, zh_b, _, inv_z = norm_pair(pre_z, jnp.dot(teach_2, t_out, preferred_element_type=jnp.float32))
         emb_a = zh_a.astype(jnp.bfloat16)
         emb_b = zh_b.astype(jnp.bfloat16)
         corr_part = contract_rows(emb_a, emb_b)
@@ -381,14 +789,10 @@
         stat_sums = small_sum(jnp.stack([jnp.sum(grad_emb, axis=0), jnp.sum(grad_emb * zh_a, axis=0), loss_row]))
         loss_value = jnp.sum(stat_sums[2]) * 0.5
         grad_z = ((grad_emb - stat_sums[0] / row_count - zh_a * (stat_sums[1] / row_count)) * inv_z).astype(jnp.bfloat16)
-        grad_w_out = lax.psum(contract_rows(act_2, grad_z), DATA_AXIS)
-        grad_pre_2 = jnp.where(mask_2, contract_cols(grad_z, w_out), 0.0)
-        grad_u_2, grad_gain_2, grad_bias_2 = affine_back(grad_pre_2, normed_2, inv_2, gain_2)
-        part_mid = contract_rows(act_1, grad_u_2)
-        grad_pre_1 = jnp.where(mask_1, contract_cols(grad_u_2, w_mid), 0.0)
-        grad_u_1, grad_gain_1, grad_bias_1 = affine_back(grad_pre_1, normed_1, inv_1, gain_1)
-        part_in = contract_rows(feat_a, grad_u_1)
-        grad_w_mid, grad_w_in = large_sum([part_mid, part_in], 8, (3, 7), PlainFinish, [], 2)
-        return (loss_value, grad_emb, grad_w_in, grad_w_mid, grad_w_out, grad_gain_1, grad_bias_1, grad_gain_2, grad_bias_2)
+        grad_w_out, grad_w_mid, grad_w_in, sums = backward(
+            grad_z, act_2.T, act_1.T, feat_a.T, w_out, w_mid, pre_2, pre_1, jnp.stack(vec_2 + vec_1)
+        )
+        sums = jnp.transpose(sums, (0, 2, 1, 3)).reshape(2, 2, -1)
+        return (loss_value, grad_emb, grad_w_in, grad_w_mid, grad_w_out, sums[1, 0], sums[1, 1], sums[0, 0], sums[0, 1])
 
     return jax.shard_map(local_step, mesh=mesh, in_specs=(row_part, row_part) + (replicated,) * 11, out_specs=(replicated, row_part) + (replicated,) * 7, check_vma=False)

time: 825 us -> 831 us (level)
  matrix products: 135 us -> 89.9 us
  Pallas kernels: 614 us -> 643 us
  local copies, waits for them, and re-layouts: 37.5 us -> 64 us
  between operations: 17 us -> 3.86 us
    pallas_call x0 -> x1, Pallas kernels: none -> 455 us  [backward(): pl.pallas_call(back_kernel, name='backward', out_shape=[mat, mat, mat, ja...]
    pallas_call x2 -> x1, Pallas kernels: 529 us -> 130 us  [large_sum(): pl.pallas_call(functools.partial(large_sum_kernel, mats, chunks, z_first,...]
    dot_general x4 -> x1, matrix products: 42.5 us -> 14.2 us  [contract_rows(): lax.dot_general(left_op, right_op, (((0,), (0,)), ((), ())), preferred_el...]
    pallas_call x6 -> x4, Pallas kernels: 84.9 us -> 57.3 us  [small_sum(): pl.pallas_call(small_sum_kernel, name='small_sum', out_shape=jax.ShapeDty...]
    dot_general x0 -> x4, local copies, waits for them, and re-layouts: none -> 21.7 us  [the longest x2 11 us: hidden_pair(): jnp.dot(in_b, weight_b, preferred_element_type=jnp.float32)]
    dot_general x3 -> x1, matrix products: 33.7 us -> 12.6 us  [contract_cols(): lax.dot_general(left_op, right_op, (((1,), (1,)), ((), ())), preferred_el...]
    unnamed x43 -> x32, local copies, waits for them, and re-layouts: 33.7 us -> 37.6 us
  transfers between devices with their start and end apart: 1 -> 0, of which waited for: 0 -> 0; matrix products, arithmetic and copies ran while one was open for 6% -> 0% of each run, Pallas kernels for 52% -> 0%
where the time goes in v2:
time: 831 us; the launch traced here: 819 us
  Pallas kernels  643 us (77%)
  matrix products  89.9 us (11%)
  local copies, waits for them, and re-layouts  64 us (8%)
  other arithmetic  17.8 us (2%)
    pallas_call x1, Pallas kernels, backward(): pl.pallas_call(back_kernel, name='backward', out_shape=[mat, mat, mat, ja...  455 us
    pallas_call x1, Pallas kernels, large_sum(): pl.pallas_call(functools.partial(large_sum_kernel, mats, chunks, z_first,...  130 us
    pallas_call x4, Pallas kernels, small_sum(): pl.pallas_call(small_sum_kernel, name='small_sum', out_shape=jax.ShapeDty...  57.3 us
    unnamed x32, local copies, waits for them, and re-layouts  37.6 us
    dot_general x2, matrix products, hidden_pair(): jnp.dot(in_b, weight_b, preferred_element_type=jnp.float32)  21 us
    dot_general x2, matrix products, hidden_pair(): pre_a = jnp.dot(in_a, weight_a, preferred_element_type=jnp.float32)  20 us

profile of v2, /device:TPU:0, one launch (start us, length us, event | category | flops | bytes accessed | tf_op | source)
XLA Modules:
  0.0 818.7 jit_solution(14311096926499514473)
XLA Ops:
  1.4 3.9 copy.26
  5.4 9.4 %fusion.37 = (f32[2048]{0:T(1024)S(1)}, f32[2048]{0:T(1024)S(1)}, f32[512,2048]{1,0:T(8,128)}) fusion(bf16[512,2048]{1,0:T(8,128)(2,1)S(1)} %copy-done.9, bf16[2048,2048]{1,0:T(8,128)(2,1)} %param.18), kind=kOutput, calls=%fused_computation.74 | convolution fusion | flops 4298108928 | bytes 14696448 | tf_op jit(solution)/shard_map/dot_general | solution.py:774
  14.8 5.5 copy.22
  20.3 9.4 %fusion.36 = (f32[2048]{0:T(1024)S(1)}, f32[2048]{0:T(1024)S(1)}, f32[512,2048]{1,0:T(8,128)}) fusion(bf16[512,2048]{1,0:T(8,128)(2,1)S(1)} %copy-done.3, bf16[2048,2048]{1,0:T(8,128)(2,1)} %param.15), kind=kOutput, calls=%fused_computation.73 | convolution fusion | flops 4298108928 | bytes 14696448 | tf_op jit(solution)/shard_map/dot_general | solution.py:773
  30.4 17.1 %small_sum.4 = f32[8,8,128]{2,1,0:T(8,128)} custom-call(f32[8,8,128]{2,1,0:T(8,128)} %reshape.115.x_ref), custom_call_target="tpu_custom_call" | custom-call | tf_op jit(solution)/shard_map/small_sum/pallas_call | solution.py:87
  47.5 0.8 broadcast_multiply_fusion.2
  48.3 11.6 %fusion.35 = (f32[2048]{0:T(1024)S(1)}, f32[2048]{0:T(1024)S(1)}, f32[512,2048]{1,0:T(8,128)}) fusion(bf16[2048,2048]{1,0:T(8,128)(2,1)} %param.19, f32[512,2048]{0,1:T(8,128)} %copy.22, f32[2048]{0:T(1024)S(1)} %copy-done.4, f32[2048]{0:T(1024)S(1)} %copy-done.5, f32[2048]{0:T(1024)S(1)} %get-tuple-element.55, f32[2048]{0:T(1024)S(1)} %get-tuple-element.51), kind=kOutput, calls=%fused_computation.72 | convolution fusion | flops 4304400384 | bytes 16826368 | tf_op jit(solution)/shard_map/dot_general | solution.py:774
  59.9 5.3 copy.23
  65.3 4.2 fusion.50.xt1
  69.5 10.5 %fusion.34 = (f32[2048]{0:T(1024)S(1)}, f32[2048]{0:T(1024)S(1)}, f32[512,2048]{1,0:T(8,128)}) fusion(bf16[2048,2048]{1,0:T(8,128)(2,1)} %w_mid.1, f32[512,2048]{0,1:T(8,128)S(1)} %copy-done.2, f32[2048]{0:T(1024)S(1)} %bitcast.79, f32[2048]{0:T(1024)S(1)} %get-tuple-element.52, f32[2048]{0:T(1024)S(1)} %copy-done.4, f32[2048]{0:T(1024)S(1)} %copy-done.5), kind=kOutput, calls=%fused_computation.71 | convolution fusion | flops 4304400384 | bytes 16826368 | tf_op jit(solution)/shard_map/dot_general | solution.py:773
  80.7 13.4 %small_sum.5 = f32[8,8,128]{2,1,0:T(8,128)} custom-call(f32[8,8,128]{2,1,0:T(8,128)} %reshape.116.x_ref), custom_call_target="tpu_custom_call" | custom-call | tf_op jit(solution)/shard_map/small_sum/pallas_call | solution.py:87
  94.1 0.8 broadcast_multiply_fusion.1
  95.6 5.3 copy.25
  101.0 3.9 fusion.51.xt2
  104.9 10.5 %fusion.32 = (f32[2048]{0:T(1024)S(1)}, f32[2048]{0:T(1024)S(1)}, f32[512,2048]{1,0:T(8,128)}) fusion(bf16[2048,2048]{1,0:T(8,128)(2,1)} %w_out.1, f32[512,2048]{0,1:T(8,128)S(1)} %copy-done.1, f32[2048]{0:T(1024)S(1)} %bitcast.81, f32[2048]{0:T(1024)S(1)} %get-tuple-element.47, f32[2048]{0:T(1024)S(1)} %copy-done.6, f32[2048]{0:T(1024)S(1)} %copy-done.7), kind=kOutput, calls=%fused_computation.69 | convolution fusion | flops 4304400384 | bytes 16826368 | tf_op jit(solution)/shard_map/dot_general | solution.py:781
  115.4 5.5 copy.24
  121.0 11.6 %fusion.33 = (f32[2048]{0:T(1024)S(1)}, f32[2048]{0:T(1024)S(1)}, f32[512,2048]{1,0:T(8,128)}) fusion(bf16[2048,2048]{1,0:T(8,128)(2,1)} %param.20, f32[512,2048]{0,1:T(8,128)} %copy.24, f32[2048]{0:T(1024)S(1)} %copy-done.6, f32[2048]{0:T(1024)S(1)} %copy-done.7, f32[2048]{0:T(1024)S(1)} %get-tuple-element.50, f32[2048]{0:T(1024)S(1)} %get-tuple-element.46), kind=kOutput, calls=%fused_computation.70 | convolution fusion | flops 4304400384 | bytes 16826368 | tf_op jit(solution)/shard_map/dot_general | solution.py:782
  133.3 13.4 %small_sum.6 = f32[8,8,128]{2,1,0:T(8,128)} custom-call(f32[8,8,128]{2,1,0:T(8,128)} %reshape.117.x_ref), custom_call_target="tpu_custom_call" | custom-call | tf_op jit(solution)/shard_map/small_sum/pallas_call | solution.py:87
  147.5 14.2 %fusion.1.refs_0_ = f32[2048,2048]{1,0:T(8,128)} fusion(f32[512,2048]{1,0:T(8,128)} %get-tuple-element.61, f32[2048]{0:T(1024)S(1)} %get-tuple-element.43, f32[2048]{0:T(1024)S(1)} %get-tuple-element.44, f32[512,2048]{1,0:T(8,128)} %get-tuple-element.60, f32[2048]{0:T(1024)S(1)} %get-tuple-element.45, f32[2048]{0:T(1024)S(1)} %get-tuple-element.42), kind=kOutput, calls=%fused_computation.16 | convolution fusion | flops 4301258752 | bytes 25198592 | tf_op jit(solution)/shard_map/dot_general | solution.py:21
  161.7 130.4 %large_sum.1 = (bf16[2048,2048]{1,0:T(8,128)(2,1)}, f32[1,2048]{1,0:T(1,128)}) custom-call(f32[2048,2048]{1,0:T(8,128)} %fusion.1.refs_0_, f32[1]{0:T(128)} %bitcast.74.refs_1_), custom_call_target="tpu_custom_call" | custom-call | tf_op jit(solution)/shard_map/large_sum/pallas_call | solution.py:322
  292.1 12.6 %fusion.31 = (f32[2048]{0:T(1024)S(1)}, f32[2048]{0:T(1024)S(1)}, f32[512,2048]{1,0:T(8,128)}) fusion(f32[2048]{0:T(1024)S(1)} %get-tuple-element.43, f32[512,2048]{1,0:T(8,128)} %get-tuple-element.61, f32[2048]{0:T(1024)S(1)} %get-tuple-element.44, bf16[2048,2048]{1,0:T(8,128)(2,1)} %get-tuple-element.15, f32[512,2048]{1,0:T(8,128)} %get-tuple-element.60, ...), kind=kOutput, calls=%fused_computation.68 | convolution fusion | flops 4304400384 | bytes 21020672 | tf_op jit(solution)/shard_map/dot_general | solution.py:25
  305.4 13.3 %small_sum.7 = f32[8,8,128]{2,1,0:T(8,128)} custom-call(f32[8,8,128]{2,1,0:T(8,128)} %pad_bitcast_fusion.x_ref), custom_call_target="tpu_custom_call" | custom-call | tf_op jit(solution)/shard_map/small_sum/pallas_call | solution.py:87
  318.7 1.3 multiply_bitcast_fusion.1
  320.7 5.9 multiply_convert_fusion.dz_hbm
  326.6 455.5 %backward.1 = (f32[2048,2048]{1,0:T(8,128)}, f32[2048,2048]{1,0:T(8,128)}, f32[2048,2048]{1,0:T(8,128)}, f32[2,8,2,256]{3,2,1,0:T(2,128)}) custom-call(bf16[512,2048]{1,0:T(8,128)(2,1)} %multiply_convert_fusion.dz_hbm, bf16[2048,512]{1,0:T(8,128)(2,1)} %fusion.51.xt2, bf16[2048,512]{1,0:T(8,128)(2,1)} %fusion.50.xt1, bf16[2048,512]{1,0:T(8,128)(2,1)} %bitcast.77, ...), custom_call_target="tpu_custom_call" | custom-call | tf_op jit(solution)/shard_map/backward/pallas_call | solution.py:715
  782.1 1.4 fusion.38
  783.5 13.5 %copy.31 = f32[2048,2048]{1,0:T(8,128)} copy(f32[2048,2048]{1,0:T(8,128)} %get-tuple-element.74) | data formatting | bytes 33554432
  797.0 2.9 copy-done
  799.9 8.5 %copy.32 = f32[2048,2048]{1,0:T(8,128)} copy(f32[2048,2048]{1,0:T(8,128)S(1)} %copy-done) | data formatting | bytes 33554432
  808.4 1.4 slice-done.2
  809.8 1.2 slice-done.3
  811.0 6.2 copy.33
  (42 shorter events, 4.3 us)
Async XLA Ops:
  0.6 4.7 copy-start.9
  14.8 5.5 copy-start.3
  20.3 28.0 %copy-start.4 = (f32[2048]{0:T(1024)S(1)}, f32[2048]{0:T(1024)}, u32[]{:S(2)}) copy-start(f32[2048]{0:T(1024)} %param.22) | copy-start | bytes 24580
  20.3 28.0 %copy-start.5 = (f32[2048]{0:T(1024)S(1)}, f32[2048]{0:T(1024)}, u32[]{:S(2)}) copy-start(f32[2048]{0:T(1024)} %param.21) | copy-start | bytes 24580
  65.3 4.2 copy-start.2
  69.4 25.5 %copy-start.6 = (f32[2048]{0:T(1024)S(1)}, f32[2048]{0:T(1024)}, u32[]{:S(2)}) copy-start(f32[2048]{0:T(1024)} %param.24) | copy-start | bytes 24580
  69.4 25.5 %copy-start.7 = (f32[2048]{0:T(1024)S(1)}, f32[2048]{0:T(1024)}, u32[]{:S(2)}) copy-start(f32[2048]{0:T(1024)} %param.23) | copy-start | bytes 24580
  101.0 3.9 copy-start.1
  292.1 12.6 %copy-start.8 = (f32[1,2048]{1,0:T(1,128)S(1)}, f32[1,2048]{1,0:T(1,128)}, u32[]{:S(2)}) copy-start(f32[1,2048]{1,0:T(1,128)} %get-tuple-element.16) | copy-start | bytes 24580
  783.5 16.4 %copy-start = (f32[2048,2048]{1,0:T(8,128)S(1)}, f32[2048,2048]{1,0:T(8,128)}, u32[]{:S(2)}) copy-start(f32[2048,2048]{1,0:T(8,128)} %get-tuple-element.75) | copy-start | bytes 50331652
  783.5 24.9 %slice-start = ((s8[16777216]{0:T(1024)(128)(4,1)}), s8[4194304]{0:T(1024)(128)(4,1)S(1)}, s32[]{:S(2)}) async-start(s8[16777216]{0:T(1024)(128)(4,1)} %bitcast.75), calls=%async_computation | async-start | bytes 8388608
  783.5 24.9 %slice-start.1 = ((s8[16777216]{0:T(1024)(128)(4,1)}), s8[4194304]{0:T(1024)(128)(4,1)S(1)}, s32[]{:S(2)}) async-start(s8[16777216]{0:T(1024)(128)(4,1)} %bitcast.75), calls=%async_computation.1 | async-start | bytes 8388608
  799.9 9.9 %slice-start.2 = ((s8[16777216]{0:T(1024)(128)(4,1)}), s8[4194304]{0:T(1024)(128)(4,1)S(1)}, s32[]{:S(2)}) async-start(s8[16777216]{0:T(1024)(128)(4,1)} %bitcast.75), calls=%async_computation.2 | async-start | bytes 8388608
  799.9 11.1 %slice-start.3 = ((s8[16777216]{0:T(1024)(128)(4,1)}), s8[4194304]{0:T(1024)(128)(4,1)S(1)}, s32[]{:S(2)}) async-start(s8[16777216]{0:T(1024)(128)(4,1)} %bitcast.75), calls=%async_computation.3 | async-start | bytes 8388608

commit v3 on v2

--- a/solution.py
+++ b/solution.py
@@ -11,6 +11,7 @@
 DATA_AXIS = "data"
 MESH = pl.DeviceIdType.MESH
 VMEM_BYTES = 62 * 1024 * 1024
+BACK_VMEM = 67_043_328
 LANES = 128
 PLANE = 8
 DEPTH = 4
@@ -346,20 +347,25 @@
 MATS = 3
 SLOTS = 12
 TILE = 256
-BACK_LAGS = (0, 1, 3, 5, 6, 7, 8, 9, 11, 13)
-Z_FIRST = (3, 7)
-
-
-def back_kernel(dz_hbm, xt2, xt1, xt0, w_out, w_mid, u2, u1, vec, out2, out1, out0, sums, *scratch):
-    (dy_own, dy_peer, xt_own, xt_peer, w_buf, u_buf, dpre, payload, plane_buf, depth_buf, own_buf) = scratch[:11]
-    (acc, gathered, rx, ry, rz, rl) = scratch[11:17]
-    (in_sem, tile_sem, peer_send, peer_recv, s1, r1, s2, r2, s3, r3, store_sem, send, recv) = scratch[17:]
+WIDE = 512
+BACK_LAGS = (0, 0, 2, 4, 5, 6, 7, 8, 10, 12)
+Z_FIRST = (2, 7, 12, 17, 21)
+LAYER_SLOTS = 6
+
+
+def back_kernel(dz_hbm, x2, x1, x0, w_out, w_mid, u2, u1, vec, out2, out1, out0, sums, *scratch):
+    (dy, xs, w_buf, u_buf, dpre, payload, plane_buf, depth_buf, own_buf) = scratch[:9]
+    (acc, gathered, rx, ry, rz, rl) = scratch[9:15]
+    (in_sem, tile_sem, peer_send, peer_recv, s1, r1, s2, r2, s3, r3, store_sem, send, recv) = scratch[15:]
     rows_dev, width = dz_hbm.shape
-    tiles = width // TILE
+    wide = w_buf.shape[1]
+    tiles = width // wide
+    per_slot = tiles // 2
     row_count = rows_dev * 4 * PLANE
-    part_rows = width // 2 // PARTS
+    half = width // 2
+    part_rows = half // PARTS
     count = MATS * PARTS
-    xts, outs, weights, pres = (xt2, xt1, xt0), (out2, out1, out0), (w_out, w_mid), (u2, u1)
+    mats_in, outs, weights, pres = (x2, x1, x0), (out2, out1, out0), (w_out, w_mid), (u2, u1)
 
     me = lax.axis_index(DATA_AXIS)
     pos, plane = me % PLANE, me // PLANE
@@ -372,103 +378,111 @@
     def rows(off, size):
         return pl.ds(pl.multiple_of(off, size), size)
 
-    def cols(i, size=TILE):
-        return pl.ds(pl.multiple_of(i * size, size), size)
+    mine = rows(core * rows_dev, rows_dev)
+
+    def pick(index, choices, what):
+        for i, c in enumerate(choices):
+            pl.when(index == i)(functools.partial(what, c))
 
     barrier = pltpu.get_barrier_semaphore()
     signal_all(barrier, peers)
 
-    half = width // 2
-
-    def own_xt(w):
-        return pltpu.make_async_copy(xts[w].at[rows(core * half, half)], xt_own.at[w], in_sem.at[w])
-
-    dz_load = pltpu.make_async_copy(dz_hbm, dy_own.at[0], in_sem.at[MATS])
-
-    def peer_xt(w):
+    def own_x(w):
+        return pltpu.make_async_copy(mats_in[w].at[:, rows(core * half, half)], xs.at[w, mine], in_sem.at[w])
+
+    def peer_x(w):
         return pltpu.make_async_remote_copy(
-            xts[w].at[rows((1 - core) * half, half)], xt_peer.at[w], peer_send.at[w], peer_recv.at[w], device_id=(other_core,), device_id_type=MESH
+            mats_in[w].at[:, rows((1 - core) * half, half)], xs.at[w, mine], peer_send.at[w], peer_recv.at[w], device_id=(other_core,), device_id_type=MESH
         )
 
     def peer_dy(w):
-        src = dz_hbm if w == 0 else dy_own.at[w % 2]
-        return pltpu.make_async_remote_copy(
-            src, dy_peer.at[w % 2], peer_send.at[MATS + w], peer_recv.at[MATS + w], device_id=(other_core,), device_id_type=MESH
-        )
-
-    def w_tile(layer, i):
-        return pltpu.make_async_copy(weights[layer].at[cols(i)], w_buf.at[i % 2], tile_sem.at[0, i % 2])
-
-    def u_tile(layer, i):
-        return pltpu.make_async_copy(pres[layer].at[:, cols(i)], u_buf.at[i % 2], tile_sem.at[1, i % 2])
-
+        block = dy.at[w % 2, mine]
+        return pltpu.make_async_remote_copy(block, block, peer_send.at[MATS + w], peer_recv.at[MATS + w], device_id=(other_core,), device_id_type=MESH)
+
+    def x_arrive(w):
+        block = xs.at[w, mine]
+        pltpu.make_async_copy(block, block, in_sem.at[w]).wait()
+        pltpu.make_async_remote_copy(block, block, peer_send.at[w], peer_recv.at[w], device_id=(other_core,), device_id_type=MESH).wait_recv()
+
+    def w_tile(ref, i):
+        return pltpu.make_async_copy(ref.at[rows(i * wide, wide)], w_buf.at[i % 2], tile_sem.at[0, i % 2])
+
+    def u_tile(ref, i):
+        return pltpu.make_async_copy(ref.at[:, rows(i * wide, wide)], u_buf.at[i % 2], tile_sem.at[1, i % 2])
+
+    def start_w(layer, i):
+        pick(layer, weights, lambda ref: w_tile(ref, i).start())
+
+    def start_u(layer, i):
+        pick(layer, pres, lambda ref: u_tile(ref, i).start())
+
+    dz_load = pltpu.make_async_copy(dz_hbm, dy.at[0, mine], in_sem.at[MATS])
     dz_load.start()
-    w_tile(0, 0).start()
-    u_tile(0, 0).start()
     for w in range(MATS):
-        own_xt(w).start()
+        own_x(w).start()
+    w_tile(weights[0], 0).start()
+    u_tile(pres[0], 0).start()
     pl.semaphore_wait(barrier, len(peers))
+    peer_x(0).start()
+    dz_load.wait()
     peer_dy(0).start()
-    for w in range(MATS):
-        peer_xt(w).start()
-    dz_load.wait()
-
-    def vec_row(layer, which, i):
-        return vec[layer * 4 + which : layer * 4 + which + 1, cols(i)]
-
-    BLOCK = 64
+    for w in range(1, MATS):
+        peer_x(w).start()
+
+    BLOCK = 32
 
     def row_loop(body, carry):
-        return lax.fori_loop(0, rows_dev // BLOCK, lambda r, c: body(rows(r * BLOCK, BLOCK), c), carry)
-
-    def chain(layer):
+        return lax.fori_loop(0, rows_dev // BLOCK, lambda r, c: body(r, c), carry)
+
+    def chain_tile(layer, i):
+        w_tile(w_out, i).wait()
+        u_tile(u2, i).wait()
+
+        @pl.when(i + 1 < tiles)
+        def _():
+            start_w(layer, i + 1)
+            start_u(layer, i + 1)
+
+        at_cols = rows(i * wide, wide)
+        dpre[:, at_cols] = contract_cols(dy[layer, mine], w_buf[i % 2])
+        gain, bias, mean, inv = (vec[layer * 4 + j, :, at_cols] for j in range(4))
+
+        def block(r, sums2):
+            at = rows(r * BLOCK, BLOCK)
+            n = (u_buf[i % 2, at] - mean) * inv
+            g = jnp.where(n * gain + bias > 0.0, dpre[at, at_cols], 0.0)
+            dpre[at, at_cols] = g
+            gn = g * n
+            return tuple(s + jnp.sum(v.reshape(BLOCK // 8, 8, wide), axis=0) for s, v in zip(sums2, (gn, g)))
+
+        zero = jnp.zeros((8, wide), jnp.float32)
+        for row, total in enumerate(row_loop(block, (zero, zero))):
+            total = jnp.sum(total, axis=0, keepdims=True)
+            for c in range(wide // TILE):
+                payload[layer, i * (wide // TILE) + c, row : row + 1] = total[:, c * TILE : (c + 1) * TILE]
+
+    def du(layer):
+        start_u(layer, 0)
+
         def tile(i, carry):
-            w_tile(layer, i).wait()
-            u_tile(layer, i).wait()
+            u_tile(u2, i).wait()
 
             @pl.when(i + 1 < tiles)
             def _():
-                w_tile(layer, i + 1).start()
-                u_tile(layer, i + 1).start()
-
-            dpre[:, cols(i)] = contract_cols(dy_own[layer], w_buf[i % 2])
-            gain, bias, mean, inv = (vec_row(layer, j, i) for j in range(4))
-
-            def block(at, sums2):
+                start_u(layer, i + 1)
+
+            at_cols = rows(i * wide, wide)
+            gain, mean, inv = (vec[layer * 4 + j, :, at_cols] for j in (0, 2, 3))
+            total = jnp.concatenate([sums[layer, i * (wide // TILE) + c] for c in range(wide // TILE)], axis=1)
+            mean_gn = total[0:1] / row_count
+            mean_g = total[1:2] / row_count
+            scale = gain * inv
+
+            def block(r, c):
+                at = rows(r * BLOCK, BLOCK)
                 n = (u_buf[i % 2, at] - mean) * inv
-                g = jnp.where(n * gain + bias > 0.0, dpre[at, cols(i)], 0.0)
-                dpre[at, cols(i)] = g
-                gn = g * n
-                return tuple(
-                    s + jnp.sum(v.reshape(BLOCK // 8, 8, TILE), axis=0) for s, v in zip(sums2, (gn, g))
-                )
-
-            zero = jnp.zeros((8, TILE), jnp.float32)
-            sn, sg = row_loop(block, (zero, zero))
-            payload[layer, i, 0:1] = jnp.sum(sn, axis=0, keepdims=True)
-            payload[layer, i, 1:2] = jnp.sum(sg, axis=0, keepdims=True)
-            return carry
-
-        lax.fori_loop(0, tiles, tile, 0)
-
-    def du(layer):
-        u_tile(layer, 0).start()
-
-        def tile(i, carry):
-            u_tile(layer, i).wait()
-
-            @pl.when(i + 1 < tiles)
-            def _():
-                u_tile(layer, i + 1).start()
-
-            gain, mean, inv = vec_row(layer, 0, i), vec_row(layer, 2, i), vec_row(layer, 3, i)
-            mean_gn = sums[layer, i, 0:1] / row_count
-            mean_g = sums[layer, i, 1:2] / row_count
-            scale = gain * inv
-
-            def block(at, c):
-                n = (u_buf[i % 2, at] - mean) * inv
-                dy_own[1 - layer, at, cols(i)] = ((dpre[at, cols(i)] - mean_g - n * mean_gn) * scale).astype(jnp.bfloat16)
+                value = (dpre[at, at_cols] - mean_g - n * mean_gn) * scale
+                dy[1 - layer, rows(core * rows_dev + r * BLOCK, BLOCK), at_cols] = value.astype(jnp.bfloat16)
                 return c
 
             row_loop(block, 0)
@@ -529,10 +543,9 @@
     zz = ((8, bz0), (16, bz1))
 
     def steps_of(k):
-        part = k % PARTS
         zf = 0
         for z in Z_FIRST:
-            same = part - z
+            same = k - z
             zf = zf + (1 - lax.min(same * same, 1))
         pairs = []
         for a, b in zip(xy + zz, zz + xy):
@@ -566,11 +579,11 @@
     def out_rows(k, side):
         return pl.ds(pl.multiple_of(side * half + (k % PARTS) * part_rows, part_rows), part_rows)
 
-    def last_copy(w, k, side):
-        return remote(gathered.at[k % SLOTS], outs[w].at[out_rows(k, side)], 7, k, other_core)
-
-    def store_copy(w, k):
-        return pltpu.make_async_copy(gathered.at[k % SLOTS], outs[w].at[out_rows(k, core)], store_sem.at[k])
+    def last_copy(out, k, side):
+        return remote(gathered.at[k % SLOTS], out.at[out_rows(k, side)], 7, k, other_core)
+
+    def store_copy(out, k):
+        return pltpu.make_async_copy(gathered.at[k % SLOTS], out.at[out_rows(k, core)], store_sem.at[k])
 
     def add_rows(dst, k, off, size, buf):
         step = min(size, 16)
@@ -583,20 +596,20 @@
 
         lax.fori_loop(0, size // step, body, 0)
 
-    def for_mat(k, what):
-        for w in range(MATS):
-            pl.when(k // PARTS == w)(functools.partial(what, w))
-
     def form(k):
         w, j = k // PARTS, k % SLOTS
-        at = rows((k % PARTS) * part_rows, part_rows)
-        step = min(512, width)
+
+        @pl.when(k % PARTS == 0)
+        def _():
+            x_arrive(w)
+            peer_dy(w).wait_recv()
+
+        at = rows((k % PARTS) * part_rows, 2 * part_rows)
+        step = min(1024, width)
 
         def col(c, carry):
-            cs = cols(c, step)
-            acc[j, :, cs] = jnp.dot(xt_own[w, at], dy_own[w % 2, :, cs], preferred_element_type=jnp.float32) + jnp.dot(
-                xt_peer[w, at], dy_peer[w % 2, :, cs], preferred_element_type=jnp.float32
-            )
+            cs = rows(c * step, step)
+            acc[pl.ds(j, 2), :, cs] = contract_rows(xs[w, :, at], dy[w % 2, :, cs]).reshape(2, part_rows, step)
             return carry
 
         lax.fori_loop(0, width // step, col, 0)
@@ -604,12 +617,7 @@
     def stage(i, k):
         pairs, offs = steps_of(k)
         if i == 0:
-
-            @pl.when(k == 2 * PARTS)
-            def _():
-                peer_dy(2).wait_recv()
-
-            form(k)
+            pl.when(k % 2 == 0)(lambda: form(k))
         elif i == 1:
             reduce_copy(0, k, pairs, offs).start()
         elif i < 5:
@@ -629,77 +637,70 @@
         elif i == 8:
             gather_copy(0, k, pairs, offs).wait_recv()
 
-            def emit(w):
-                last_copy(w, k, core).start()
-                store_copy(w, k).start()
-
-            for_mat(k, emit)
+            def emit(out):
+                last_copy(out, k, core).start()
+                store_copy(out, k).start()
+
+            pick(k // PARTS, outs, emit)
         else:
 
-            def close(w):
-                last_copy(w, k, 1 - core).wait_recv()
-                store_copy(w, k).wait()
-                last_copy(w, k, core).wait_send()
-
-            for_mat(k, close)
+            def close(out):
+                last_copy(out, k, 1 - core).wait_recv()
+                store_copy(out, k).wait()
+                last_copy(out, k, core).wait_send()
+
+            pick(k // PARTS, outs, close)
             for n in range(3):
                 gather_copy(n, k, pairs, offs).wait_send()
 
-    def chunk_loop(first_k, last_k, i):
-        def body(k, carry):
-            stage(i, k)
-            return carry
-
-        lax.fori_loop(first_k, last_k, body, 0)
-
-    ready = {0: SLOTS, 1: 2}
+    def layer_work(t):
+        layer = t // LAYER_SLOTS
+        at = t - LAYER_SLOTS * layer
+
+        @pl.when(at < 2)
+        def _():
+            def body(i, carry):
+                chain_tile(layer, i)
+                return carry
+
+            lax.fori_loop(at * per_slot, at * per_slot + per_slot, body, 0)
+
+        pl.when(at == 2)(lambda: small_begin(layer))
+        pl.when(at == 3)(lambda: small_middle(layer))
+        pl.when(at == 4)(lambda: small_last(layer))
+
+        @pl.when(at == 5)
+        def _():
+            small_end(layer)
+            pl.when(layer == 1)(lambda: peer_dy(0).wait_send())
+            du(layer)
+            peer_dy(layer + 1).start()
+
+            @pl.when(layer == 0)
+            def _():
+                w_tile(weights[1], 0).start()
+                u_tile(pres[1], 0).start()
 
     def slot(t, carry):
         for i in ORDER:
             k = t - BACK_LAGS[i]
 
-            @pl.when((k >= ready.get(i, 0)) & (k < count))
+            @pl.when((k >= 0) & (k < count))
             def _():
                 stage(i, k)
 
+            if i == 1:
+                pl.when(t < 2 * LAYER_SLOTS)(lambda: layer_work(t))
         return carry
 
-    chain(0)
-    w_tile(1, 0).start()
-    small_begin(0)
+    lax.fori_loop(0, count + BACK_LAGS[-1], slot, 0)
     for w in range(MATS):
-        own_xt(w).wait()
-        peer_xt(w).wait_recv()
-    peer_dy(0).wait_recv()
-    chunk_loop(0, PARTS // 2, 0)
-    small_middle(0)
-    chunk_loop(PARTS // 2, PARTS, 0)
-    small_last(0)
-    chunk_loop(0, 2, 1)
-    small_end(0)
-    du(0)
-    peer_dy(1).start()
-    u_tile(1, 0).start()
-    chain(1)
-    small_begin(1)
-    peer_dy(1).wait_recv()
-    chunk_loop(PARTS, PARTS + 2, 0)
-    small_middle(1)
-    chunk_loop(PARTS + 2, SLOTS, 0)
-    small_last(1)
-    slot(3, 0)
-    small_end(1)
-    peer_dy(0).wait_send()
-    du(1)
-    peer_dy(2).start()
-    lax.fori_loop(4, count + BACK_LAGS[-1], slot, 0)
-    for w in range(MATS):
-        peer_xt(w).wait_send()
+        peer_x(w).wait_send()
     peer_dy(1).wait_send()
     peer_dy(2).wait_send()
 
 
-def backward(grad_z, xt2, xt1, xt0, w_out, w_mid, u2, u1, vec):
+def backward(grad_z, x2, x1, x0, w_out, w_mid, u2, u1, vec):
     rows_dev, width = grad_z.shape
     tiles = width // TILE
     part_rows = width // 2 // PARTS
@@ -719,12 +720,10 @@
         in_specs=[any_spec] * 8 + [vmem_spec],
         out_specs=[any_spec] * 3 + [vmem_spec],
         scratch_shapes=[
-            pltpu.VMEM((2, rows_dev, width), jnp.bfloat16),
-            pltpu.VMEM((2, rows_dev, width), jnp.bfloat16),
-            pltpu.VMEM((MATS, width // 2, rows_dev), jnp.bfloat16),
-            pltpu.VMEM((MATS, width // 2, rows_dev), jnp.bfloat16),
-            pltpu.VMEM((2, TILE, width), jnp.bfloat16),
-            pltpu.VMEM((2, rows_dev, TILE), jnp.float32),
+            pltpu.VMEM((2, 2 * rows_dev, width), jnp.bfloat16),
+            pltpu.VMEM((MATS, 2 * rows_dev, width // 2), jnp.bfloat16),
+            pltpu.VMEM((2, WIDE, width), jnp.bfloat16),
+            pltpu.VMEM((2, rows_dev, WIDE), jnp.float32),
             pltpu.VMEM((rows_dev, width), jnp.float32),
             pltpu.VMEM((2, tiles, 2, TILE), jnp.float32),
             pltpu.VMEM((2, PLANE, 2, TILE), jnp.float32),
@@ -750,8 +749,8 @@
             dma((8, count)),
             dma((8, count)),
         ],
-        compiler_params=pltpu.CompilerParams(collective_id=2, has_side_effects=True, vmem_limit_bytes=VMEM_BYTES),
-    )(grad_z, xt2, xt1, xt0, w_out, w_mid, u2, u1, vec)
+        compiler_params=pltpu.CompilerParams(collective_id=2, has_side_effects=True, vmem_limit_bytes=BACK_VMEM),
+    )(grad_z, x2, x1, x0, w_out, w_mid, u2, u1, vec)
 
 
 def solution(mesh):
@@ -790,7 +789,7 @@
         loss_value = jnp.sum(stat_sums[2]) * 0.5
         grad_z = ((grad_emb - stat_sums[0] / row_count - zh_a * (stat_sums[1] / row_count)) * inv_z).astype(jnp.bfloat16)
         grad_w_out, grad_w_mid, grad_w_in, sums = backward(
-            grad_z, act_2.T, act_1.T, feat_a.T, w_out, w_mid, pre_2, pre_1, jnp.stack(vec_2 + vec_1)
+            grad_z, act_2, act_1, feat_a, w_out, w_mid, pre_2, pre_1, jnp.stack(vec_2 + vec_1)[:, None, :]
         )
         sums = jnp.transpose(sums, (0, 2, 1, 3)).reshape(2, 2, -1)
         return (loss_value, grad_emb, grad_w_in, grad_w_mid, grad_w_out, sums[1, 0], sums[1, 1], sums[0, 0], sums[0, 1])

time: 831 us -> 715 us (0.86); the launches traced: 819 us -> 713 us
  Pallas kernels: 643 us -> 575 us
  local copies, waits for them, and re-layouts: 64 us -> 38.5 us
    pallas_call x1, Pallas kernels: 455 us -> 389 us  [backward(): pl.pallas_call(back_kernel, name='backward', out_shape=[mat, mat, mat, ja...]
    dot_general x4 -> x0, local copies, waits for them, and re-layouts: 21.7 us -> none  [the longest x2 11 us: hidden_pair(): jnp.dot(in_b, weight_b, preferred_element_type=jnp.float32)]
    unnamed x32 -> x37, local copies, waits for them, and re-layouts: 37.6 us -> 33.7 us
where the time goes in v3:
time: 715 us; the launch traced here: 713 us
  Pallas kernels  575 us (80%)
  matrix products  82.4 us (12%)
  local copies, waits for them, and re-layouts  38.5 us (5%)
  other arithmetic  13.5 us (2%)
    pallas_call x1, Pallas kernels, backward(): pl.pallas_call(back_kernel, name='backward', out_shape=[mat, mat, mat, ja...  389 us
    pallas_call x1, Pallas kernels, large_sum(): pl.pallas_call(functools.partial(large_sum_kernel, mats, chunks, z_first,...  129 us
    pallas_call x4, Pallas kernels, small_sum(): pl.pallas_call(small_sum_kernel, name='small_sum', out_shape=jax.ShapeDty...  57.3 us
    unnamed x37, local copies, waits for them, and re-layouts  33.7 us
    dot_general x2, matrix products, hidden_pair(): jnp.dot(in_b, weight_b, preferred_element_type=jnp.float32)  22 us

profile of v3, /device:TPU:0, one launch (start us, length us, event | category | flops | bytes accessed | tf_op | source)
XLA Modules:
  0.0 713.0 jit_solution(8116428779803392656)
XLA Ops:
  1.3 10.7 %fusion.37 = (f32[2048]{0:T(1024)S(1)}, f32[2048]{0:T(1024)S(1)}, f32[512,2048]{1,0:T(8,128)}) fusion(bf16[512,2048]{1,0:T(8,128)(2,1)} %param.14, bf16[2048,2048]{1,0:T(8,128)(2,1)} %param.18), kind=kOutput, calls=%fused_computation.74 | convolution fusion | flops 4298108928 | bytes 14696448 | tf_op jit(solution)/shard_map/dot_general | solution.py:773
  12.0 6.0 fusion.36
  18.1 0.6 reshape.115.x_ref
  18.7 17.1 %small_sum.4 = f32[8,8,128]{2,1,0:T(8,128)} custom-call(f32[8,8,128]{2,1,0:T(8,128)} %reshape.115.x_ref), custom_call_target="tpu_custom_call" | custom-call | tf_op jit(solution)/shard_map/small_sum/pallas_call | solution.py:88
  35.8 0.8 broadcast_multiply_fusion.2
  36.7 11.4 %fusion.35 = (f32[2048]{0:T(1024)S(1)}, f32[2048]{0:T(1024)S(1)}, f32[512,2048]{1,0:T(8,128)}) fusion(bf16[2048,2048]{1,0:T(8,128)(2,1)} %param.19, f32[512,2048]{1,0:T(8,128)} %get-tuple-element.56, f32[2048]{0:T(1024)S(1)} %copy-done.5, f32[2048]{0:T(1024)S(1)} %copy-done.6, f32[2048]{0:T(1024)S(1)} %get-tuple-element.55, f32[2048]{0:T(1024)S(1)} %get-tuple-element.51), kind=kOutput, calls=%fused_computation.72 | convolution fusion | flops 4304400384 | bytes 16826368 | tf_op jit(solution)/shard_map/dot_general | solution.py:773
  48.0 0.8 maximum_convert_fusion.2.x1
  48.9 6.1 fusion.34
  55.1 0.6 reshape.116.x_ref
  55.7 13.4 %small_sum.5 = f32[8,8,128]{2,1,0:T(8,128)} custom-call(f32[8,8,128]{2,1,0:T(8,128)} %reshape.116.x_ref), custom_call_target="tpu_custom_call" | custom-call | tf_op jit(solution)/shard_map/small_sum/pallas_call | solution.py:88
  69.2 0.8 broadcast_multiply_fusion.1
  70.0 11.2 %fusion.33 = (f32[2048]{0:T(1024)S(1)}, f32[2048]{0:T(1024)S(1)}, f32[512,2048]{1,0:T(8,128)}) fusion(bf16[2048,2048]{1,0:T(8,128)(2,1)} %param.20, f32[512,2048]{1,0:T(8,128)} %get-tuple-element.58, f32[2048]{0:T(1024)S(1)} %copy-done.7, f32[2048]{0:T(1024)S(1)} %copy-done.8, f32[2048]{0:T(1024)S(1)} %get-tuple-element.50, f32[2048]{0:T(1024)S(1)} %get-tuple-element.46), kind=kOutput, calls=%fused_computation.70 | convolution fusion | flops 4304400384 | bytes 16826368 | tf_op jit(solution)/shard_map/dot_general | solution.py:781
  81.2 0.7 broadcast_in_dim.14.vec
  81.9 3.0 maximum_convert_fusion.x2
  84.9 10.2 %fusion.32 = (f32[2048]{0:T(1024)S(1)}, f32[2048]{0:T(1024)S(1)}, f32[512,2048]{1,0:T(8,128)}) fusion(bf16[512,2048]{1,0:T(8,128)(2,1)S(1)} %maximum_convert_fusion.x2, bf16[2048,2048]{1,0:T(8,128)(2,1)} %w_out.1), kind=kOutput, calls=%fused_computation.69 | convolution fusion | flops 4298108928 | bytes 14696448 | tf_op jit(solution)/shard_map/dot_general | solution.py:780
  95.1 0.6 reshape.117.x_ref
  95.7 13.4 %small_sum.6 = f32[8,8,128]{2,1,0:T(8,128)} custom-call(f32[8,8,128]{2,1,0:T(8,128)} %reshape.117.x_ref), custom_call_target="tpu_custom_call" | custom-call | tf_op jit(solution)/shard_map/small_sum/pallas_call | solution.py:88
  109.2 0.8 broadcast_multiply_fusion
  110.0 14.2 %fusion.1.refs_0_ = f32[2048,2048]{1,0:T(8,128)} fusion(f32[512,2048]{1,0:T(8,128)} %get-tuple-element.61, f32[2048]{0:T(1024)S(1)} %get-tuple-element.43, f32[2048]{0:T(1024)S(1)} %get-tuple-element.44, f32[512,2048]{1,0:T(8,128)} %get-tuple-element.60, f32[2048]{0:T(1024)S(1)} %get-tuple-element.45, f32[2048]{0:T(1024)S(1)} %get-tuple-element.42), kind=kOutput, calls=%fused_computation.16 | convolution fusion | flops 4301258752 | bytes 25198592 | tf_op jit(solution)/shard_map/dot_general | solution.py:22
  124.2 129.4 %large_sum.1 = (bf16[2048,2048]{1,0:T(8,128)(2,1)}, f32[1,2048]{1,0:T(1,128)}) custom-call(f32[2048,2048]{1,0:T(8,128)} %fusion.1.refs_0_, f32[1]{0:T(128)} %bitcast.69.refs_1_), custom_call_target="tpu_custom_call" | custom-call | tf_op jit(solution)/shard_map/large_sum/pallas_call | solution.py:323
  253.6 12.6 %fusion.31 = (f32[2048]{0:T(1024)S(1)}, f32[2048]{0:T(1024)S(1)}, f32[512,2048]{1,0:T(8,128)}) fusion(f32[2048]{0:T(1024)S(1)} %get-tuple-element.43, f32[512,2048]{1,0:T(8,128)} %get-tuple-element.61, f32[2048]{0:T(1024)S(1)} %get-tuple-element.44, bf16[2048,2048]{1,0:T(8,128)(2,1)} %get-tuple-element.15, f32[512,2048]{1,0:T(8,128)} %get-tuple-element.60, ...), kind=kOutput, calls=%fused_computation.68 | convolution fusion | flops 4304400384 | bytes 21020672 | tf_op jit(solution)/shard_map/dot_general | solution.py:26
  266.9 13.3 %small_sum.7 = f32[8,8,128]{2,1,0:T(8,128)} custom-call(f32[8,8,128]{2,1,0:T(8,128)} %pad_bitcast_fusion.x_ref), custom_call_target="tpu_custom_call" | custom-call | tf_op jit(solution)/shard_map/small_sum/pallas_call | solution.py:88
  280.2 1.3 multiply_bitcast_fusion.1
  282.2 5.9 multiply_convert_fusion.dz_hbm
  288.1 388.7 %backward.1 = (f32[2048,2048]{1,0:T(8,128)}, f32[2048,2048]{1,0:T(8,128)}, f32[2048,2048]{1,0:T(8,128)}, f32[2,8,2,256]{3,2,1,0:T(2,128)}) custom-call(bf16[512,2048]{1,0:T(8,128)(2,1)} %multiply_convert_fusion.dz_hbm, bf16[512,2048]{1,0:T(8,128)(2,1)} %copy-done.3, bf16[512,2048]{1,0:T(8,128)(2,1)} %copy-done.2, bf16[512,2048]{1,0:T(8,128)(2,1)} %x0.1, ...), custom_call_target="tpu_custom_call" | custom-call | tf_op jit(solution)/shard_map/backward/pallas_call | solution.py:716
  676.8 1.4 fusion.38
  678.3 13.5 %copy.26 = f32[2048,2048]{1,0:T(8,128)} copy(f32[2048,2048]{1,0:T(8,128)} %get-tuple-element.74) | data formatting | bytes 33554432
  691.8 2.9 copy-done
  694.7 8.5 %copy.27 = f32[2048,2048]{1,0:T(8,128)} copy(f32[2048,2048]{1,0:T(8,128)S(1)} %copy-done) | data formatting | bytes 33554432
  703.2 1.4 slice-done.2
  704.6 1.2 slice-done.3
  705.8 6.2 copy.28
  (45 shorter events, 1.0 us)
Async XLA Ops:
  1.3 10.7 %copy-start.4 = (bf16[512,2048]{1,0:T(8,128)(2,1)S(1)}, bf16[512,2048]{1,0:T(8,128)(2,1)}, u32[]{:S(2)}) copy-start(bf16[512,2048]{1,0:T(8,128)(2,1)} %x0.1) | copy-start | bytes 6291460
  1.3 10.7 %copy-start.10 = (bf16[2048,2048]{1,0:T(8,128)(2,1)S(1)}, bf16[2048,2048]{1,0:T(8,128)(2,1)}, u32[]{:S(2)}) copy-start(bf16[2048,2048]{1,0:T(8,128)(2,1)} %param.15) | copy-start | bytes 25165828
  12.0 24.6 %copy-start.5 = (f32[2048]{0:T(1024)S(1)}, f32[2048]{0:T(1024)}, u32[]{:S(2)}) copy-start(f32[2048]{0:T(1024)} %param.22) | copy-start | bytes 24580
  12.0 24.6 %copy-start.6 = (f32[2048]{0:T(1024)S(1)}, f32[2048]{0:T(1024)}, u32[]{:S(2)}) copy-start(f32[2048]{0:T(1024)} %param.21) | copy-start | bytes 24580
  36.6 12.2 %slice-start.4 = ((s8[8388608]{0:T(1024)(128)(4,1)}), s8[4194304]{0:T(1024)(128)(4,1)S(1)}, s32[]{:S(2)}) async-start(s8[8388608]{0:T(1024)(128)(4,1)} %bitcast.72), calls=%async_computation.4 | async-start | bytes 8388608
  36.6 11.4 %copy-start.1 = (f32[512,2048]{1,0:T(8,128)S(1)}, f32[512,2048]{1,0:T(8,128)}, u32[]{:S(2)}) copy-start(f32[512,2048]{1,0:T(8,128)} %get-tuple-element.57.u1) | copy-start | bytes 12582916
  36.6 12.2 %slice-start.5 = ((s8[8388608]{0:T(1024)(128)(4,1)}), s8[4194304]{0:T(1024)(128)(4,1)S(1)}, s32[]{:S(2)}) async-start(s8[8388608]{0:T(1024)(128)(4,1)} %bitcast.72), calls=%async_computation.5 | async-start | bytes 8388608
  48.9 6.2 copy-start.2
  48.9 21.1 %copy-start.7 = (f32[2048]{0:T(1024)S(1)}, f32[2048]{0:T(1024)}, u32[]{:S(2)}) copy-start(f32[2048]{0:T(1024)} %param.24) | copy-start | bytes 24580
  48.9 21.1 %copy-start.8 = (f32[2048]{0:T(1024)S(1)}, f32[2048]{0:T(1024)}, u32[]{:S(2)}) copy-start(f32[2048]{0:T(1024)} %param.23) | copy-start | bytes 24580
  84.9 10.2 %copy-start.3 = (bf16[512,2048]{1,0:T(8,128)(2,1)}, bf16[512,2048]{1,0:T(8,128)(2,1)S(1)}, u32[]{:S(2)}) copy-start(bf16[512,2048]{1,0:T(8,128)(2,1)S(1)} %maximum_convert_fusion.x2) | copy-start | bytes 6291460
  253.6 12.6 %copy-start.9 = (f32[1,2048]{1,0:T(1,128)S(1)}, f32[1,2048]{1,0:T(1,128)}, u32[]{:S(2)}) copy-start(f32[1,2048]{1,0:T(1,128)} %get-tuple-element.16) | copy-start | bytes 24580
  678.2 16.4 %copy-start = (f32[2048,2048]{1,0:T(8,128)S(1)}, f32[2048,2048]{1,0:T(8,128)}, u32[]{:S(2)}) copy-start(f32[2048,2048]{1,0:T(8,128)} %get-tuple-element.75) | copy-start | bytes 50331652
  678.3 24.9 %slice-start = ((s8[16777216]{0:T(1024)(128)(4,1)}), s8[4194304]{0:T(1024)(128)(4,1)S(1)}, s32[]{:S(2)}) async-start(s8[16777216]{0:T(1024)(128)(4,1)} %bitcast.70), calls=%async_computation | async-start | bytes 8388608
  678.3 24.9 %slice-start.1 = ((s8[16777216]{0:T(1024)(128)(4,1)}), s8[4194304]{0:T(1024)(128)(4,1)S(1)}, s32[]{:S(2)}) async-start(s8[16777216]{0:T(1024)(128)(4,1)} %bitcast.70), calls=%async_computation.1 | async-start | bytes 8388608
  694.7 9.9 %slice-start.2 = ((s8[16777216]{0:T(1024)(128)(4,1)}), s8[4194304]{0:T(1024)(128)(4,1)S(1)}, s32[]{:S(2)}) async-start(s8[16777216]{0:T(1024)(128)(4,1)} %bitcast.70), calls=%async_computation.2 | async-start | bytes 8388608
  694.7 11.1 %slice-start.3 = ((s8[16777216]{0:T(1024)(128)(4,1)}), s8[4194304]{0:T(1024)(128)(4,1)S(1)}, s32[]{:S(2)}) async-start(s8[16777216]{0:T(1024)(128)(4,1)} %bitcast.70), calls=%async_computation.3 | async-start | bytes 8388608

commit v4 on v0

v4 whole, which is shorter than its diff:
```python
import functools

import jax
import jax.numpy as jnp
from jax import lax
from jax.experimental import pallas as pl
from jax.experimental.pallas import tpu as pltpu
from jax.sharding import PartitionSpec as P

NORM_EPS = 1e-5
DATA_AXIS = "data"
MESH = pl.DeviceIdType.MESH
VMEM_BYTES = 67_043_328
PLANE = 8
DEPTH = 4
TILE = 256
WIDE = 512
BLOCK = 32
SUM_ROWS = 4
PARTS = 8
MATS = 3
SLOTS = 12
JOBS = 6
W_BUFS = 3
LAYER_SLOTS = 6
LAGS = (0, 0, 2, 4, 5, 6, 7, 8, 10, 12)
ORDER = (0, 1, 5, 4, 6, 3, 7, 2, 8, 9)
FRONT_Z_FIRST = (2, 6)
BACK_Z_FIRST = (2, 6, 10, 14, 18, 22)


def contract_rows(left_op, right_op):
    return lax.dot_general(left_op, right_op, (((0,), (0,)), ((), ())), preferred_element_type=jnp.float32)


def contract_cols(left_op, right_op):
    return lax.dot_general(left_op, right_op, (((1,), (1,)), ((), ())), preferred_element_type=jnp.float32)


def rows(off, size):
    return pl.ds(pl.multiple_of(off, size), size)


def pick(index, choices, what):
    for i, c in enumerate(choices):
        pl.when(index == i)(functools.partial(what, c))


def loop(lo, hi, body):
    def step(i, carry):
        body(i)
        return carry

    lax.fori_loop(lo, hi, step, 0)


def remote_copy(src, dst, send, recv, mate):
    return pltpu.make_async_remote_copy(src, dst, send, recv, device_id=(mate,), device_id_type=MESH)


class Place:
    def __init__(self):
        me = lax.axis_index(DATA_AXIS)
        self.me = me
        self.pos, self.plane = me % PLANE, me // PLANE
        self.core, self.bx, self.by, self.bz0, self.bz1 = me % 2, (me // 2) % 2, (me // 4) % 2, (me // 8) % 2, (me // 16) % 2
        self.other_core = me + 1 - 2 * self.core
        self.mates = [(self.pos + d) % PLANE for d in range(1, PLANE)]
        self.levels = [(self.plane + d) % DEPTH for d in range(1, DEPTH)]

    def peers(self):
        return [self.plane * PLANE + m for m in self.mates] + [lv * PLANE + self.pos for lv in self.levels]

    def arrive(self):
        sem = pltpu.get_barrier_semaphore()
        for peer in self.peers():
            pl.semaphore_signal(sem, inc=1, device_id=(peer,), device_id_type=MESH)

    def all_here(self):
        pl.semaphore_wait(pltpu.get_barrier_semaphore(), PLANE + DEPTH - 2)


class SmallSum:
    def __init__(self, place, payload, total, plane_buf, depth_buf, own_buf, sems):
        self.p, self.payload, self.total = place, payload, total
        self.plane_buf, self.depth_buf, self.own_buf, self.sems = plane_buf, depth_buf, own_buf, sems

    def first(self, j, m, slot):
        s, r = self.sems[0], self.sems[1]
        return remote_copy(self.payload.at[j, m], self.plane_buf.at[j, slot], s.at[j, m], r.at[j, slot], self.p.plane * PLANE + m)

    def second(self, j, lv, slot):
        s, r = self.sems[2], self.sems[3]
        return remote_copy(self.own_buf.at[j, 0], self.depth_buf.at[j, slot], s.at[j, lv], r.at[j, slot], lv * PLANE + self.p.pos)

    def third(self, j, m, slot):
        s, r = self.sems[4], self.sems[5]
        return remote_copy(self.own_buf.at[j, 1], self.total.at[j, slot], s.at[j, m], r.at[j, slot], self.p.plane * PLANE + m)

    def begin(self, j):
        for m in self.p.mates:
            self.first(j, m, self.p.pos).start()
        self.plane_buf[j, self.p.pos] = self.payload[j, self.p.pos]

    def middle(self, j):
        for m in self.p.mates:
            self.first(j, m, m).wait_recv()
        total = self.plane_buf[j, 0]
        for i in range(1, PLANE):
            total = total + self.plane_buf[j, i]
        self.own_buf[j, 0] = total
        self.depth_buf[j, self.p.plane] = total
        for lv in self.p.levels:
            self.second(j, lv, self.p.plane).start()

    def last(self, j):
        for lv in self.p.levels:
            self.second(j, lv, lv).wait_recv()
        total = self.depth_buf[j, 0]
        for i in range(1, DEPTH):
            total = total + self.depth_buf[j, i]
        self.own_buf[j, 1] = total
        self.total[j, self.p.pos] = total
        for m in self.p.mates:
            self.third(j, m, self.p.pos).start()

    def end(self, j):
        for m in self.p.mates:
            self.third(j, m, m).wait_recv()
            self.first(j, m, self.p.pos).wait_send()
            self.third(j, m, self.p.pos).wait_send()
        for lv in self.p.levels:
            self.second(j, lv, self.p.plane).wait_send()


def small_scratch(count):
    def buf(*lead):
        return pltpu.VMEM((count, *lead, SUM_ROWS, TILE), jnp.float32)

    bufs = [buf(PLANE), buf(PLANE), buf(PLANE), buf(DEPTH), buf(2)]
    return bufs + [pltpu.SemaphoreType.DMA((count, n)) for n in (PLANE, PLANE, DEPTH, DEPTH, PLANE, PLANE)]


SMALL_REFS = 11


def small_sum(place, refs):
    payload, total, plane_buf, depth_buf, own_buf = refs[:5]
    return SmallSum(place, payload, total, plane_buf, depth_buf, own_buf, refs[5:])


class ChunkSum:
    def __init__(self, place, z_first, slots, acc, gathered, landing, send, recv, finish):
        self.p, self.z_first, self.slots = place, z_first, slots
        self.acc, self.gathered, self.landing, self.send, self.recv, self.finish = acc, gathered, landing, send, recv, finish
        self.size = acc.shape[1]
        core, bx, by = place.core, place.bx, place.by
        self.xy = ((2 + 2 * core, core * by + (1 - core) * bx), (4 - 2 * core, core * bx + (1 - core) * by))
        self.zz = ((8, place.bz0), (16, place.bz1))
        self.is_mid = place.bz0 + place.bz1 - 2 * place.bz0 * place.bz1
        self.z_mate = place.me + 8 * (1 - 2 * place.bz0)
        self.mid_mate = place.me + 8 * (1 - 2 * place.bz1)

    def steps(self, k):
        zf = 0
        for z in self.z_first:
            same = k - z
            zf = zf + (1 - lax.min(same * same, 1))
        pairs = []
        for a, b in zip(self.xy + self.zz, self.zz + self.xy):
            stride = zf * b[0] + (1 - zf) * a[0]
            bit = zf * b[1] + (1 - zf) * a[1]
            pairs.append((self.p.me + stride * (1 - 2 * bit), bit))
        offs, size = [0], self.size
        for _, bit in pairs[:3]:
            size = size // 2
            offs.append(offs[-1] + bit * size)
        return zf, pairs, offs

    def copy(self, src, dst, stage, k, mate):
        return remote_copy(src, dst, self.send.at[stage, k], self.recv.at[stage, k], mate)

    def down(self, stage, k, off, size, mate):
        j = k % self.slots
        return self.copy(self.acc.at[j, rows(off, size)], self.landing[stage].at[j, pl.ds(0, size)], stage, k, mate)

    def up(self, stage, k, off, size, mate):
        block = self.gathered.at[k % self.slots, rows(off, size)]
        return self.copy(block, block, stage, k, mate)

    def add(self, k, off, size, buf):
        step = min(size, 16)
        j = k % self.slots

        def body(i):
            at = rows(off + i * step, step)
            self.acc[j, at] = self.acc[j, at] + buf[j, rows(i * step, step)]

        loop(0, size // step, body)

    def close(self, k, off, size):
        step = min(size, 16)

        def body(i):
            self.finish(k, off + i * step, step, self.landing[3], i * step)

        loop(0, size // step, body)

    def stage(self, i, k):
        zf, pairs, offs = self.steps(k)
        s2, s4, s8 = self.size // 2, self.size // 4, self.size // 8
        l1, l2, l3, l4 = self.landing
        keep = self.is_mid
        z_first = zf == 1
        mid = (zf == 0) & (keep == 1)
        end = (zf == 0) & (keep == 0)

        half_copy = lambda: self.down(0, k, offs[0] + (1 - pairs[0][1]) * s2, s2, pairs[0][0])
        quarter_copy = lambda: self.down(1, k, offs[1] + (1 - pairs[1][1]) * s4, s4, pairs[1][0])
        eighth_copy = lambda: self.down(2, k, offs[2] + (1 - pairs[2][1]) * s8, s8, pairs[2][0])
        whole_copy = lambda: self.down(3, k, offs[3], s8, pairs[3][0])
        inward = lambda: self.down(2, k, offs[2], s4, self.z_mate)
        across = lambda: self.down(3, k, offs[2], s4, self.mid_mate)
        back8 = lambda: self.up(4, k, offs[3], s8, pairs[2][0])
        outward = lambda: self.up(4, k, offs[2], s4, self.z_mate)
        back4 = lambda: self.up(5, k, offs[2], s4, pairs[1][0])
        back2 = lambda: self.up(6, k, offs[1], s2, pairs[0][0])

        if i == 1:
            half_copy().start()
        elif i == 2:
            half_copy().wait_recv()
            self.add(k, offs[1], s2, l1)
            quarter_copy().start()
        elif i == 3:
            quarter_copy().wait_recv()
            self.add(k, offs[2], s4, l2)
            pl.when(z_first)(lambda: eighth_copy().start())
            pl.when(end)(lambda: inward().start())
        elif i == 4:

            @pl.when(z_first)
            def _():
                eighth_copy().wait_recv()
                self.add(k, offs[3], s8, l3)
                whole_copy().start()

            @pl.when(mid)
            def _():
                inward().wait_recv()
                self.add(k, offs[2], s4, l3)
                across().start()

        elif i == 5:

            @pl.when(z_first)
            def _():
                whole_copy().wait_recv()
                self.close(k, offs[3], s8)
                back8().start()

            @pl.when(mid)
            def _():
                across().wait_recv()
                self.close(k, offs[2], s4)
                outward().start()

        elif i == 6:
            pl.when(z_first)(lambda: back8().wait_recv())
            pl.when(end)(lambda: outward().wait_recv())
            back4().start()
            half_copy().wait_send()
            quarter_copy().wait_send()

            @pl.when(z_first)
            def _():
                eighth_copy().wait_send()
                whole_copy().wait_send()

            pl.when(end)(lambda: inward().wait_send())
            pl.when(mid)(lambda: across().wait_send())
        elif i == 7:
            back4().wait_recv()
            back2().start()
        elif i == 8:
            back2().wait_recv()
        else:
            pl.when(z_first)(lambda: back8().wait_send())
            pl.when(mid)(lambda: outward().wait_send())
            back4().wait_send()
            back2().wait_send()


def run_slots(count, stage, between):
    def slot(t):
        for i in ORDER:
            k = t - LAGS[i]

            @pl.when((k >= 0) & (k < count))
            def _():
                stage(i, k)

            if i == 1:
                between(t)

    loop(0, count + LAGS[-1], slot)


def chunk_scratch(slots, part_rows, width, count, dtype):
    def buf(n, kind=jnp.float32):
        return pltpu.VMEM((slots, n, width), kind)

    dma = pltpu.SemaphoreType.DMA
    return [buf(part_rows), buf(part_rows, dtype), buf(part_rows // 2), buf(part_rows // 4), buf(part_rows // 4), buf(part_rows // 4)] + [
        dma((8, count)),
        dma((8, count)),
    ]


CHUNK_REFS = 8


def fold(value):
    return jnp.sum(value.reshape(value.shape[0] // 8, 8, value.shape[1]), axis=0)


def front_kernel(feat_a, feat_b, w_in, t_in, w_mid, t_mid, w_out, t_out, affine, off_weight, pre1, pre2, act1, act2, dz, grad_emb, vec, loss, *scratch):
    (x_buf, u_buf, w_buf, stats, ea, eb, g_peer) = scratch[:7]
    (x_sem, w_sem, keep_sem, ge_sem, e_send, e_recv) = scratch[7:13]
    small_refs = scratch[13 : 13 + SMALL_REFS]
    acc, gathered, l1, l2, l3, l4, send, recv = scratch[13 + SMALL_REFS :]
    rows_dev, width = feat_a.shape
    wide = w_buf.shape[2]
    tiles = width // wide
    half = width // 2
    part_rows = half // PARTS
    row_count = rows_dev * DEPTH * PLANE
    weights, feats = (w_in, t_in, w_mid, t_mid, w_out, t_out), (feat_a, feat_b)
    place = Place()
    core = place.core
    mine = rows(core * rows_dev, rows_dev)
    place.arrive()
    small = small_sum(place, small_refs)
    payload, total = small.payload, small.total

    def feat(v):
        return pltpu.make_async_copy(feats[v], x_buf.at[v], x_sem.at[v])

    def w_tile(ref, g):
        return pltpu.make_async_copy(ref.at[:, rows((g % tiles) * wide, wide)], w_buf.at[g % W_BUFS], w_sem.at[g % W_BUFS])

    def start_w(g):
        pick(g // tiles, weights, lambda ref: w_tile(ref, g).start())

    feat(0).start()
    w_tile(weights[0], 0).start()
    feat(1).start()
    for g in range(1, W_BUFS - 1):
        start_w(g)
    feat(0).wait()
    payload[...] = jnp.zeros_like(payload)

    def keep_pre(ref):
        return pltpu.make_async_copy(u_buf.at[0], ref, keep_sem.at[0])

    def keep_act(ref):
        return pltpu.make_async_copy(x_buf.at[0], ref, keep_sem.at[1])

    def row_loop(body, carry):
        return lax.fori_loop(0, rows_dev // BLOCK, lambda r, c: body(rows(r * BLOCK, BLOCK), c), carry)

    def put_sums(j, i, row, value):
        value = jnp.sum(value, axis=0, keepdims=True)
        for c in range(value.shape[1] // TILE):
            payload[j, i + c, row : row + 1] = value[:, c * TILE : (c + 1) * TILE]

    def product(g):
        job, i = g // tiles, g % tiles
        view = job % 2
        w_tile(w_in, g).wait()
        pl.when(g + W_BUFS - 1 < JOBS * tiles)(lambda: start_w(g + W_BUFS - 1))
        at_cols = rows(i * wide, wide)
        u_buf[view, :, at_cols] = jnp.dot(x_buf[view], w_buf[g % W_BUFS], preferred_element_type=jnp.float32)

        def block(at, sums):
            u = u_buf[view, at, at_cols]
            return sums[0] + fold(u), sums[1] + fold(u * u)

        zero = jnp.zeros((8, wide), jnp.float32)
        for row, value in enumerate(row_loop(block, (zero, zero))):
            put_sums(job, i * (wide // TILE), row, value)

    def begin(job):
        small.begin(job)

        @pl.when(job % 2 == 0)
        def _():
            pick(job // 2, (pre1, pre2), lambda ref: keep_pre(ref).start())

    def norm(job):
        layer, view = job // 2, job % 2
        small.end(job)
        for c in range(PLANE):
            at = slice(c * TILE, (c + 1) * TILE)
            means = total[job, c] / row_count
            stats[job, 0, :, at] = means[0:1]
            stats[job, 1, :, at] = lax.rsqrt(means[1:2] - means[0:1] * means[0:1] + NORM_EPS)

        @pl.when((view == 0) & (layer == 1))
        def _():
            keep_act(act1).wait()

        @pl.when((view == 0) & (layer == 2))
        def _():
            keep_act(act2).wait()

        def hidden(i):
            at_cols = rows(i * wide, wide)
            mean, inv = stats[job, 0, :, at_cols], stats[job, 1, :, at_cols]
            gain, bias = affine[layer * 2, :, at_cols], affine[layer * 2 + 1, :, at_cols]

            def block(at, c):
                n = (u_buf[view, at, at_cols] - mean) * inv
                x_buf[view, at, at_cols] = jnp.maximum(n * gain + bias, 0.0).astype(jnp.bfloat16)
                return c

            row_loop(block, 0)

        def student(i):
            at_cols = rows(i * wide, wide)
            mean, inv = stats[job, 0, :, at_cols], stats[job, 1, :, at_cols]

            def block(at, c):
                n = (u_buf[0, at, at_cols] - mean) * inv
                u_buf[0, at, at_cols] = n
                x_buf[0, at, at_cols] = n.astype(jnp.bfloat16)
                return c

            row_loop(block, 0)

        def student_own(i):
            def block(r, c):
                ea[rows(core * rows_dev + r * BLOCK, BLOCK), rows(i * wide, wide)] = x_buf[0, rows(r * BLOCK, BLOCK), rows(core * half + i * wide, wide)]
                return c

            lax.fori_loop(0, rows_dev // BLOCK, block, 0)

        def teacher(i):
            at_cols = rows(i * wide, wide)
            mean, inv = stats[job, 0, :, at_cols], stats[job, 1, :, at_cols]

            def block(r, c):
                n = (u_buf[1, rows(r * BLOCK, BLOCK), at_cols] - mean) * inv
                eb[rows(core * rows_dev + r * BLOCK, BLOCK), at_cols] = n.astype(jnp.bfloat16)
                return c

            lax.fori_loop(0, rows_dev // BLOCK, block, 0)

        @pl.when(layer < 2)
        def _():
            loop(0, tiles, hidden)

            @pl.when(view == 0)
            def _():
                pick(layer, (act1, act2), lambda ref: keep_act(ref).start())
                keep_pre(pre1).wait()

        @pl.when((layer == 2) & (view == 0))
        def _():
            loop(0, tiles, student)
            ea_copy().start()
            loop(0, tiles // 2, student_own)

        @pl.when((layer == 2) & (view == 1))
        def _():
            loop(0, tiles, teacher)
            eb_copy().start()

    ea_copy = lambda: remote_copy(x_buf.at[0, :, rows((1 - core) * half, half)], ea.at[mine], e_send.at[0], e_recv.at[0], place.other_core)
    eb_copy = lambda: remote_copy(eb.at[mine], eb.at[mine], e_send.at[1], e_recv.at[1], place.other_core)

    def step(g):
        job, i = g // tiles, g % tiles
        view = job % 2
        pl.when(g == tiles)(lambda: feat(1).wait())
        product(g)
        pl.when(g == tiles - 1)(lambda: place.all_here())

        @pl.when((view == 0) & (i == 0) & (job > 0))
        def _():
            small.last(job - 1)

        @pl.when((view == 1) & (i == tiles // 2 - 1))
        def _():
            small.middle(job - 1)

        @pl.when(i == tiles - 1)
        def _():
            begin(job)

            @pl.when(view == 1)
            def _():
                small.last(job - 1)
                small.middle(job)

            pl.when(job > 0)(lambda: norm(job - 1))

    loop(0, JOBS * tiles, step)
    small.last(JOBS - 1)
    norm(JOBS - 1)
    for j, source in enumerate((affine.at[2], affine.at[3], stats.at[2, 0], stats.at[2, 1], affine.at[0], affine.at[1], stats.at[0, 0], stats.at[0, 1])):
        vec[j] = source[...]

    loss[...] = jnp.zeros_like(loss)

    def finish(k, off, size, buf, buf_off):
        at = rows(off, size)
        corr = (acc[k, at] + buf[k, rows(buf_off, size)]) / row_count
        row = core * half + k * part_rows + off
        diag = (row + lax.broadcasted_iota(jnp.int32, (size, width), 0)) == lax.broadcasted_iota(jnp.int32, (size, width), 1)
        weight = off_weight[0]
        miss = 1.0 - corr
        loss[...] += jnp.sum(jnp.where(diag, miss * miss, weight * (corr * corr)), axis=0, keepdims=True)
        gathered[k, at] = jnp.where(diag, -2.0 * miss, 2.0 * weight * corr).astype(jnp.bfloat16)

    chunks = ChunkSum(place, FRONT_Z_FIRST, PARTS, acc, gathered, (l1, l2, l3, l4), send, recv, finish)

    def form(k):
        @pl.when(k == 0)
        def _():
            ea_copy().wait_recv()
            eb_copy().wait_recv()

        at = rows(k * part_rows, 2 * part_rows)
        size = min(1024, width)

        def col(c):
            cs = rows(c * size, size)
            acc[pl.ds(k, 2), :, cs] = contract_rows(ea[:, at], eb[:, cs]).reshape(2, part_rows, size)

        loop(0, width // size, col)

    def swap(k):
        return chunks.copy(gathered.at[k], g_peer.at[k], 7, k, place.other_core)

    def ge_cols(k, side):
        return rows(side * half + k * part_rows, 2 * part_rows)

    def ge_copy(k, side):
        at = ge_cols(k, side)
        return pltpu.make_async_copy(u_buf.at[1, :, at], grad_emb.at[:, at], ge_sem.at[k // 2, side])

    def embed(k, side, g_rows):
        at_cols = ge_cols(k, side)
        grad = contract_cols(eb[mine], g_rows.reshape(2 * part_rows, width)) / row_count
        u_buf[1, :, at_cols] = grad
        ge_copy(k, side).start()

        def block(at, sums):
            g = u_buf[1, at, at_cols]
            return sums[0] + fold(g * u_buf[0, at, at_cols]), sums[1] + fold(g)

        zero = jnp.zeros((8, 2 * part_rows), jnp.float32)
        for row, value in enumerate(row_loop(block, (zero, zero))):
            payload[JOBS, (side * half + k * part_rows) // TILE, row : row + 1] = jnp.sum(value, axis=0, keepdims=True)

    def stage(i, k):
        if i == 0:
            pl.when(k % 2 == 0)(lambda: form(k))
            return
        chunks.stage(i, k)
        if i == 8:
            swap(k).start()

            @pl.when(k % 2 == 1)
            def _():
                embed(k - 1, core, gathered[pl.ds(k - 1, 2)])

        if i == 9:
            swap(k).wait_recv()
            swap(k).wait_send()

            @pl.when(k % 2 == 1)
            def _():
                embed(k - 1, 1 - core, g_peer[pl.ds(k - 1, 2)])

    run_slots(PARTS, stage, lambda t: None)
    for c in range(PLANE):
        payload[JOBS, c, 2:3] = loss[:, c * TILE : (c + 1) * TILE]
    small.begin(JOBS)
    ea_copy().wait_send()
    eb_copy().wait_send()
    small.middle(JOBS)
    for k in range(0, PARTS, 2):
        for side in range(2):
            ge_copy(k, side).wait()
    small.last(JOBS)
    small.end(JOBS)

    def dz_tile(i):
        at_cols = rows(i * wide, wide)
        sums = jnp.concatenate([total[JOBS, i * (wide // TILE) + c] for c in range(wide // TILE)], axis=1) / row_count
        mean_gn, mean_g = sums[0:1], sums[1:2]
        inv = stats[JOBS - 2, 1, :, at_cols]

        def block(at, c):
            value = (u_buf[1, at, at_cols] - mean_g - u_buf[0, at, at_cols] * mean_gn) * inv
            x_buf[0, at, at_cols] = value.astype(jnp.bfloat16)
            return c

        row_loop(block, 0)

    loop(0, tiles, dz_tile)
    keep_act(dz).start()
    for c in range(PLANE):
        loss[:, c * TILE : (c + 1) * TILE] = total[JOBS, c, 2:3]
    keep_act(dz).wait()


def front(feat_a, feat_b, weights, affine, off_weight):
    rows_dev, width = feat_a.shape
    half = width // 2
    part_rows = half // PARTS
    any_spec = pl.BlockSpec(memory_space=pl.ANY)
    vmem_spec = pl.BlockSpec(memory_space=pltpu.VMEM)
    wide_f32 = jax.ShapeDtypeStruct((rows_dev, width), jnp.float32)
    wide_bf16 = jax.ShapeDtypeStruct((rows_dev, width), jnp.bfloat16)
    dma = pltpu.SemaphoreType.DMA
    return pl.pallas_call(
        front_kernel,
        name="front",
        out_shape=[wide_f32, wide_f32, wide_bf16, wide_bf16, wide_bf16, wide_f32]
        + [jax.ShapeDtypeStruct((8, 1, width), jnp.float32), jax.ShapeDtypeStruct((1, width), jnp.float32)],
        in_specs=[any_spec] * 8 + [vmem_spec, pl.BlockSpec(memory_space=pltpu.SMEM)],
        out_specs=[any_spec] * 6 + [vmem_spec] * 2,
        scratch_shapes=[
            pltpu.VMEM((2, rows_dev, width), jnp.bfloat16),
            pltpu.VMEM((2, rows_dev, width), jnp.float32),
            pltpu.VMEM((W_BUFS, width, WIDE), jnp.bfloat16),
            pltpu.VMEM((JOBS, 2, 1, width), jnp.float32),
            pltpu.VMEM((2 * rows_dev, half), jnp.bfloat16),
            pltpu.VMEM((2 * rows_dev, width), jnp.bfloat16),
            pltpu.VMEM((PARTS, part_rows, width), jnp.bfloat16),
            dma((2,)),
            dma((W_BUFS,)),
            dma((2,)),
            dma((PARTS // 2, 2)),
            dma((2,)),
            dma((2,)),
        ]
        + small_scratch(JOBS + 1)
        + chunk_scratch(PARTS, part_rows, width, PARTS, jnp.bfloat16),
        compiler_params=pltpu.CompilerParams(collective_id=0, has_side_effects=True, vmem_limit_bytes=VMEM_BYTES),
    )(feat_a, feat_b, *weights, affine, off_weight)


def back_kernel(dz_hbm, x2, x1, x0, w_out, w_mid, u2, u1, vec, out2, out1, out0, sums_out, *scratch):
    (dy, xs, w_buf, u_buf, dpre) = scratch[:5]
    (in_sem, tile_sem, peer_send, peer_recv, store_sem) = scratch[5:10]
    small_refs = scratch[10 : 10 + SMALL_REFS]
    acc, gathered, l1, l2, l3, l4, send, recv = scratch[10 + SMALL_REFS :]
    rows_dev, width = dz_hbm.shape
    wide = w_buf.shape[1]
    tiles = width // wide
    per_slot = tiles // 2
    row_count = rows_dev * DEPTH * PLANE
    half = width // 2
    part_rows = half // PARTS
    count = MATS * PARTS
    mats_in, outs, weights, pres = (x2, x1, x0), (out2, out1, out0), (w_out, w_mid), (u2, u1)
    place = Place()
    core, other_core = place.core, place.other_core
    mine = rows(core * rows_dev, rows_dev)
    place.arrive()
    small = small_sum(place, small_refs)
    payload, sums = small.payload, small.total

    def own_x(w):
        return pltpu.make_async_copy(mats_in[w].at[:, rows(core * half, half)], xs.at[w % 2, mine], in_sem.at[w])

    def peer_x(w):
        return remote_copy(mats_in[w].at[:, rows((1 - core) * half, half)], xs.at[w % 2, mine], peer_send.at[w], peer_recv.at[w], other_core)

    def peer_dy(w):
        block = dy.at[w % 2, mine]
        return remote_copy(block, block, peer_send.at[MATS + w], peer_recv.at[MATS + w], other_core)

    def x_arrive(w):
        block = xs.at[w % 2, mine]
        pltpu.make_async_copy(block, block, in_sem.at[w]).wait()
        remote_copy(block, block, peer_send.at[w], peer_recv.at[w], other_core).wait_recv()

    def w_tile(ref, i):
        return pltpu.make_async_copy(ref.at[rows(i * wide, wide)], w_buf.at[i % 2], tile_sem.at[0, i % 2])

    def u_tile(ref, i):
        return pltpu.make_async_copy(ref.at[:, rows(i * wide, wide)], u_buf.at[i % 2], tile_sem.at[1, i % 2])

    def start_w(layer, i):
        pick(layer, weights, lambda ref: w_tile(ref, i).start())

    def start_u(layer, i):
        pick(layer, pres, lambda ref: u_tile(ref, i).start())

    dz_load = pltpu.make_async_copy(dz_hbm, dy.at[0, mine], in_sem.at[MATS])
    dz_load.start()
    for w in range(2):
        own_x(w).start()
    w_tile(weights[0], 0).start()
    u_tile(pres[0], 0).start()
    payload[...] = jnp.zeros_like(payload)
    place.all_here()
    peer_x(0).start()
    dz_load.wait()
    peer_dy(0).start()
    peer_x(1).start()

    def row_loop(body, carry):
        return lax.fori_loop(0, rows_dev // BLOCK, body, carry)

    def chain_tile(layer, i):
        w_tile(w_out, i).wait()
        u_tile(u2, i).wait()

        @pl.when(i + 1 < tiles)
        def _():
            start_w(layer, i + 1)
            start_u(layer, i + 1)

        at_cols = rows(i * wide, wide)
        dpre[:, at_cols] = contract_cols(dy[layer, mine], w_buf[i % 2])
        gain, bias, mean, inv = (vec[layer * 4 + j, :, at_cols] for j in range(4))

        def block(r, carry):
            at = rows(r * BLOCK, BLOCK)
            n = (u_buf[i % 2, at] - mean) * inv
            g = jnp.where(n * gain + bias > 0.0, dpre[at, at_cols], 0.0)
            dpre[at, at_cols] = g
            return carry[0] + fold(g * n), carry[1] + fold(g)

        zero = jnp.zeros((8, wide), jnp.float32)
        for row, value in enumerate(row_loop(block, (zero, zero))):
            value = jnp.sum(value, axis=0, keepdims=True)
            for c in range(wide // TILE):
                payload[layer, i * (wide // TILE) + c, row : row + 1] = value[:, c * TILE : (c + 1) * TILE]

    def du(layer):
        start_u(layer, 0)

        def tile(i):
            u_tile(u2, i).wait()
            pl.when(i + 1 < tiles)(lambda: start_u(layer, i + 1))
            at_cols = rows(i * wide, wide)
            gain, mean, inv = (vec[layer * 4 + j, :, at_cols] for j in (0, 2, 3))
            means = jnp.concatenate([sums[layer, i * (wide // TILE) + c] for c in range(wide // TILE)], axis=1) / row_count
            mean_gn, mean_g = means[0:1], means[1:2]
            scale = gain * inv

            def block(r, c):
                at = rows(r * BLOCK, BLOCK)
                n = (u_buf[i % 2, at] - mean) * inv
                value = (dpre[at, at_cols] - mean_g - n * mean_gn) * scale
                dy[1 - layer, rows(core * rows_dev + r * BLOCK, BLOCK), at_cols] = value.astype(jnp.bfloat16)
                return c

            row_loop(block, 0)

        loop(0, tiles, tile)

    def finish(k, off, size, buf, buf_off):
        j = k % SLOTS
        gathered[j, rows(off, size)] = acc[j, rows(off, size)] + buf[j, rows(buf_off, size)]

    chunks = ChunkSum(place, BACK_Z_FIRST, SLOTS, acc, gathered, (l1, l2, l3, l4), send, recv, finish)

    def form(k):
        w, j = k // PARTS, k % SLOTS

        @pl.when(k % PARTS == 0)
        def _():
            x_arrive(w)
            peer_dy(w).wait_recv()

        at = rows((k % PARTS) * part_rows, 2 * part_rows)
        size = min(1024, width)

        def col(c):
            cs = rows(c * size, size)
            acc[pl.ds(j, 2), :, cs] = contract_rows(xs[w % 2, :, at], dy[w % 2, :, cs]).reshape(2, part_rows, size)

        loop(0, width // size, col)

    def out_rows(k, side):
        return pl.ds(pl.multiple_of(side * half + (k % PARTS) * part_rows, part_rows), part_rows)

    def last_copy(out, k, side):
        return chunks.copy(gathered.at[k % SLOTS], out.at[out_rows(k, side)], 7, k, other_core)

    def store_copy(out, k):
        return pltpu.make_async_copy(gathered.at[k % SLOTS], out.at[out_rows(k, core)], store_sem.at[k])

    def stage(i, k):
        if i == 0:
            pl.when(k % 2 == 0)(lambda: form(k))
            return
        chunks.stage(i, k)
        if i == 8:

            def emit(out):
                last_copy(out, k, core).start()
                store_copy(out, k).start()

            pick(k // PARTS, outs, emit)
        if i == 9:

            def close(out):
                last_copy(out, k, 1 - core).wait_recv()
                store_copy(out, k).wait()
                last_copy(out, k, core).wait_send()

            pick(k // PARTS, outs, close)

    def layer_work(t):
        layer = t // LAYER_SLOTS
        at = t - LAYER_SLOTS * layer
        pl.when(at < 2)(lambda: loop(at * per_slot, at * per_slot + per_slot, lambda i: chain_tile(layer, i)))
        pl.when(at == 2)(lambda: small.begin(layer))
        pl.when(at == 3)(lambda: small.middle(layer))
        pl.when(at == 4)(lambda: small.last(layer))

        @pl.when(at == 5)
        def _():
            small.end(layer)
            pl.when(layer == 1)(lambda: peer_dy(0).wait_send())
            du(layer)
            peer_dy(layer + 1).start()

            @pl.when(layer == 0)
            def _():
                w_tile(weights[1], 0).start()
                u_tile(pres[1], 0).start()

            @pl.when(layer == 1)
            def _():
                peer_x(0).wait_send()
                own_x(2).start()
                peer_x(2).start()

    run_slots(count, stage, lambda t: pl.when(t < 2 * LAYER_SLOTS)(lambda: layer_work(t)))
    for w in (1, 2):
        peer_x(w).wait_send()
        peer_dy(w).wait_send()
    sums_out[...] = sums[...]


def backward(grad_z, x2, x1, x0, w_out, w_mid, u2, u1, vec):
    rows_dev, width = grad_z.shape
    part_rows = width // 2 // PARTS
    count = MATS * PARTS
    any_spec = pl.BlockSpec(memory_space=pl.ANY)
    vmem_spec = pl.BlockSpec(memory_space=pltpu.VMEM)
    mat = jax.ShapeDtypeStruct((width, width), jnp.float32)
    dma = pltpu.SemaphoreType.DMA
    return pl.pallas_call(
        back_kernel,
        name="backward",
        out_shape=[mat, mat, mat, jax.ShapeDtypeStruct((2, PLANE, SUM_ROWS, TILE), jnp.float32)],
        in_specs=[any_spec] * 8 + [vmem_spec],
        out_specs=[any_spec] * 3 + [vmem_spec],
        scratch_shapes=[
            pltpu.VMEM((2, 2 * rows_dev, width), jnp.bfloat16),
            pltpu.VMEM((2, 2 * rows_dev, width // 2), jnp.bfloat16),
            pltpu.VMEM((2, WIDE, width), jnp.bfloat16),
            pltpu.VMEM((2, rows_dev, WIDE), jnp.float32),
            pltpu.VMEM((rows_dev, width), jnp.float32),
            dma((MATS + 1,)),
            dma((2, 2)),
            dma((2 * MATS,)),
            dma((2 * MATS,)),
            dma((count,)),
        ]
        + small_scratch(2)
        + chunk_scratch(SLOTS, part_rows, width, count, jnp.float32),
        compiler_params=pltpu.CompilerParams(collective_id=1, has_side_effects=True, vmem_limit_bytes=VMEM_BYTES),
    )(grad_z, x2, x1, x0, w_out, w_mid, u2, u1, vec)


def solution(mesh):
    row_part = P(DATA_AXIS, None)
    replicated = P()

    def local_step(feat_a, feat_b, w_in, w_mid, w_out, t_in, t_mid, t_out, gain_1, bias_1, gain_2, bias_2, off_weight):
        affine = jnp.stack([gain_1, bias_1, gain_2, bias_2])[:, None, :]
        pre_1, pre_2, act_1, act_2, grad_z, grad_emb, vec, loss_cols = front(
            feat_a, feat_b, (w_in, t_in, w_mid, t_mid, w_out, t_out), affine, off_weight.reshape(1)
        )
        loss_value = jnp.sum(loss_cols) * 0.5
        grad_w_out, grad_w_mid, grad_w_in, sums = backward(grad_z, act_2, act_1, feat_a, w_out, w_mid, pre_2, pre_1, vec)
        sums = jnp.transpose(sums[:, :, :2], (0, 2, 1, 3)).reshape(2, 2, -1)
        return (loss_value, grad_emb, grad_w_in, grad_w_mid, grad_w_out, sums[1, 0], sums[1, 1], sums[0, 0], sums[0, 1])

    return jax.shard_map(local_step, mesh=mesh, in_specs=(row_part, row_part) + (replicated,) * 11, out_specs=(replicated, row_part) + (replicated,) * 7, check_vma=False)
```

time: 1450 us -> 642 us (0.44)
  waiting for transfers between devices: 989 us -> 0 us
  Pallas kernels: 0 us -> 594 us
  blocking collectives: 243 us -> 0 us
  matrix products: 136 us -> 0 us
  other arithmetic: 19.8 us -> 2.1 us
    psum x2 -> x0, waiting for transfers between devices: 989 us -> none  [the longest x1 712 us: local_step(): weight_grads = lax.psum((grad_w_in, grad_w_mid, grad_w_out), DATA_AXIS)]
    pallas_call x0 -> x2, Pallas kernels: none -> 594 us  [the longest x1 383 us: backward(): pl.pallas_call(back_kernel, name='backward', out_shape=[mat, mat, mat, ja...]
    psum x6 -> x0, blocking collectives: 243 us -> none  [the longest x3 122 us: norm_pair(): stat_means = lax.psum(stat_sums, DATA_AXIS) / row_count]
    dot_general x13 -> x0, matrix products: 136 us -> none  [the longest x4 43.6 us: contract_rows(): lax.dot_general(left_op, right_op, (((0,), (0,)), ((), ())), preferred_el...]
    unnamed x25 -> x14, local copies, waits for them, and re-layouts: 40.2 us -> 38.4 us
  transfers between devices with their start and end apart: 2 -> 0, of which waited for: 2 -> 0; matrix products, arithmetic and copies ran while one was open for 1% -> 0% of each run, Pallas kernels for 0% -> 0%
where the time goes in v4:
time: 642 us; the launch traced here: 639 us
  Pallas kernels  594 us (93%)
  local copies, waits for them, and re-layouts  40.5 us (6%)
    pallas_call x1, Pallas kernels, backward(): pl.pallas_call(back_kernel, name='backward', out_shape=[mat, mat, mat, ja...  383 us
    pallas_call x1, Pallas kernels, front(): pl.pallas_call(front_kernel, name='front', out_shape=[wide_f32, wide_f32,...  210 us
    unnamed x14, local copies, waits for them, and re-layouts  38.4 us

profile of v4, /device:TPU:0, one launch (start us, length us, event | category | flops | bytes accessed | tf_op | source)
XLA Modules:
  0.0 639.3 jit_solution(12936180321316704534)
XLA Ops:
  0.6 0.8 pad_maximum_fusion
  1.4 0.6 broadcast_in_dim.3.affine
  2.7 210.2 %front.1 = (f32[512,2048]{1,0:T(8,128)}, f32[512,2048]{1,0:T(8,128)}, bf16[512,2048]{1,0:T(8,128)(2,1)}, bf16[512,2048]{1,0:T(8,128)(2,1)}, bf16[512,2048]{1,0:T...) custom-call(bf16[512,2048]{1,0:T(8,128)(2,1)} %x0.1, bf16[512,2048]{1,0:T(8,128)(2,1)} %feat_b.1, ...), custom_call_target="tpu_custom_call" | custom-call | tf_op jit(solution)/shard_map/front/pallas_call | solution.py:629
  213.0 383.3 %backward.1 = (f32[2048,2048]{1,0:T(8,128)}, f32[2048,2048]{1,0:T(8,128)}, f32[2048,2048]{1,0:T(8,128)}, f32[2,8,4,256]{3,2,1,0:T(4,128)}) custom-call(bf16[512,2048]{1,0:T(8,128)(2,1)} %get-tuple-element.23.dz_hbm, bf16[512,2048]{1,0:T(8,128)(2,1)} %get-tuple-element.24.x2, bf16[512,2048]{1,0:T(8,128)(2,1)} %get-tuple-element.25.x1, bf16[512,2048]{1,0:T(8,128)(2,1)} %x0.1, ...), custom_call_target="tpu_custom_call" | custom-call | tf_op jit(solution)/shard_map/backward/pallas_call | solution.py:864
  596.3 0.9 slice.15
  597.2 0.6 fusion
  597.8 1.3 reduce_sum.9
  599.8 4.7 copy.27
  604.5 0.0 copy-start
  604.5 0.0 slice-start
  604.5 0.0 slice-start.1
  604.5 0.0 slice-start.2
  604.5 13.5 %copy.28 = f32[2048,2048]{1,0:T(8,128)} copy(f32[2048,2048]{1,0:T(8,128)} %get-tuple-element.48) | data formatting | bytes 33554432
  618.0 2.9 copy-done
  620.9 0.0 slice-start.3
  620.9 8.5 %copy.29 = f32[2048,2048]{1,0:T(8,128)} copy(f32[2048,2048]{1,0:T(8,128)S(1)} %copy-done) | data formatting | bytes 33554432
  629.4 0.0 slice-done
  629.4 0.0 slice-done.1
  629.4 1.1 slice-done.2
  630.5 1.4 slice-done.3
  632.0 6.2 copy.30
  (1 shorter events, 0.0 us)
Async XLA Ops:
  604.5 16.4 %copy-start = (f32[2048,2048]{1,0:T(8,128)S(1)}, f32[2048,2048]{1,0:T(8,128)}, u32[]{:S(2)}) copy-start(f32[2048,2048]{1,0:T(8,128)} %get-tuple-element.49) | copy-start | bytes 50331652
  604.5 24.9 %slice-start = ((s8[16777216]{0:T(1024)(128)(4,1)}), s8[4194304]{0:T(1024)(128)(4,1)S(1)}, s32[]{:S(2)}) async-start(s8[16777216]{0:T(1024)(128)(4,1)} %bitcast.13), calls=%async_computation | async-start | bytes 8388608
  604.5 24.9 %slice-start.1 = ((s8[16777216]{0:T(1024)(128)(4,1)}), s8[4194304]{0:T(1024)(128)(4,1)S(1)}, s32[]{:S(2)}) async-start(s8[16777216]{0:T(1024)(128)(4,1)} %bitcast.13), calls=%async_computation.1 | async-start | bytes 8388608
  604.5 26.1 %slice-start.2 = ((s8[16777216]{0:T(1024)(128)(4,1)}), s8[4194304]{0:T(1024)(128)(4,1)S(1)}, s32[]{:S(2)}) async-start(s8[16777216]{0:T(1024)(128)(4,1)} %bitcast.13), calls=%async_computation.2 | async-start | bytes 8388608
  620.9 11.1 %slice-start.3 = ((s8[16777216]{0:T(1024)(128)(4,1)}), s8[4194304]{0:T(1024)(128)(4,1)S(1)}, s32[]{:S(2)}) async-start(s8[16777216]{0:T(1024)(128)(4,1)} %bitcast.13), calls=%async_computation.3 | async-start | bytes 8388608

commit v5 on v4

--- a/solution.py
+++ b/solution.py
@@ -15,18 +15,18 @@
 DEPTH = 4
 TILE = 256
 WIDE = 512
-BLOCK = 32
+BLOCK = 128
 SUM_ROWS = 4
-PARTS = 8
+PARTS = 16
+GROUP = 4
 MATS = 3
-SLOTS = 12
+SLOTS = 16
 JOBS = 6
 W_BUFS = 3
-LAYER_SLOTS = 6
+LAYER_SLOTS = 8
 LAGS = (0, 0, 2, 4, 5, 6, 7, 8, 10, 12)
 ORDER = (0, 1, 5, 4, 6, 3, 7, 2, 8, 9)
-FRONT_Z_FIRST = (2, 6)
-BACK_Z_FIRST = (2, 6, 10, 14, 18, 22)
+Z_FIRST_EVERY, Z_FIRST_AT = 4, 2
 
 
 def contract_rows(left_op, right_op):
@@ -150,8 +150,8 @@
 
 
 class ChunkSum:
-    def __init__(self, place, z_first, slots, acc, gathered, landing, send, recv, finish):
-        self.p, self.z_first, self.slots = place, z_first, slots
+    def __init__(self, place, slots, acc, gathered, landing, send, recv, finish):
+        self.p, self.slots = place, slots
         self.acc, self.gathered, self.landing, self.send, self.recv, self.finish = acc, gathered, landing, send, recv, finish
         self.size = acc.shape[1]
         core, bx, by = place.core, place.bx, place.by
@@ -161,20 +161,19 @@
         self.z_mate = place.me + 8 * (1 - 2 * place.bz0)
         self.mid_mate = place.me + 8 * (1 - 2 * place.bz1)
 
+    def z_first(self, k):
+        off = k % Z_FIRST_EVERY - Z_FIRST_AT
+        return 1 - lax.min(off * off, 1)
+
     def steps(self, k):
-        zf = 0
-        for z in self.z_first:
-            same = k - z
-            zf = zf + (1 - lax.min(same * same, 1))
+        zf = self.z_first(k)
         pairs = []
         for a, b in zip(self.xy + self.zz, self.zz + self.xy):
             stride = zf * b[0] + (1 - zf) * a[0]
             bit = zf * b[1] + (1 - zf) * a[1]
             pairs.append((self.p.me + stride * (1 - 2 * bit), bit))
-        offs, size = [0], self.size
-        for _, bit in pairs[:3]:
-            size = size // 2
-            offs.append(offs[-1] + bit * size)
+        s2, s4 = self.size // 2, self.size // 4
+        offs = (0, pairs[0][1] * s2, pairs[0][1] * s2 + pairs[1][1] * s4)
         return zf, pairs, offs
 
     def copy(self, src, dst, stage, k, mate):
@@ -182,7 +181,7 @@
 
     def down(self, stage, k, off, size, mate):
         j = k % self.slots
-        return self.copy(self.acc.at[j, rows(off, size)], self.landing[stage].at[j, pl.ds(0, size)], stage, k, mate)
+        return self.copy(self.acc.at[j, rows(off, size)], self.landing[stage].at[j], stage, k, mate)
 
     def up(self, stage, k, off, size, mate):
         block = self.gathered.at[k % self.slots, rows(off, size)]
@@ -198,30 +197,18 @@
 
         loop(0, size // step, body)
 
-    def close(self, k, off, size):
-        step = min(size, 16)
-
-        def body(i):
-            self.finish(k, off + i * step, step, self.landing[3], i * step)
-
-        loop(0, size // step, body)
-
     def stage(self, i, k):
         zf, pairs, offs = self.steps(k)
-        s2, s4, s8 = self.size // 2, self.size // 4, self.size // 8
+        s2, s4 = self.size // 2, self.size // 4
         l1, l2, l3, l4 = self.landing
-        keep = self.is_mid
         z_first = zf == 1
-        mid = (zf == 0) & (keep == 1)
-        end = (zf == 0) & (keep == 0)
+        mid = (zf == 0) & (self.is_mid == 1)
+        end = (zf == 0) & (self.is_mid == 0)
 
         half_copy = lambda: self.down(0, k, offs[0] + (1 - pairs[0][1]) * s2, s2, pairs[0][0])
         quarter_copy = lambda: self.down(1, k, offs[1] + (1 - pairs[1][1]) * s4, s4, pairs[1][0])
-        eighth_copy = lambda: self.down(2, k, offs[2] + (1 - pairs[2][1]) * s8, s8, pairs[2][0])
-        whole_copy = lambda: self.down(3, k, offs[3], s8, pairs[3][0])
-        inward = lambda: self.down(2, k, offs[2], s4, self.z_mate)
-        across = lambda: self.down(3, k, offs[2], s4, self.mid_mate)
-        back8 = lambda: self.up(4, k, offs[3], s8, pairs[2][0])
+        inward = lambda: self.down(2, k, offs[2], s4, zf * pairs[2][0] + (1 - zf) * self.z_mate)
+        across = lambda: self.down(3, k, offs[2], s4, zf * pairs[3][0] + (1 - zf) * self.mid_mate)
         outward = lambda: self.up(4, k, offs[2], s4, self.z_mate)
         back4 = lambda: self.up(5, k, offs[2], s4, pairs[1][0])
         back2 = lambda: self.up(6, k, offs[1], s2, pairs[0][0])
@@ -235,57 +222,37 @@
         elif i == 3:
             quarter_copy().wait_recv()
             self.add(k, offs[2], s4, l2)
-            pl.when(z_first)(lambda: eighth_copy().start())
-            pl.when(end)(lambda: inward().start())
+            pl.when(z_first | end)(lambda: inward().start())
         elif i == 4:
 
-            @pl.when(z_first)
-            def _():
-                eighth_copy().wait_recv()
-                self.add(k, offs[3], s8, l3)
-                whole_copy().start()
-
-            @pl.when(mid)
+            @pl.when(z_first | mid)
             def _():
                 inward().wait_recv()
+                pl.when(z_first)(lambda: inward().wait_send())
                 self.add(k, offs[2], s4, l3)
                 across().start()
 
         elif i == 5:
 
-            @pl.when(z_first)
-            def _():
-                whole_copy().wait_recv()
-                self.close(k, offs[3], s8)
-                back8().start()
-
-            @pl.when(mid)
+            @pl.when(z_first | mid)
             def _():
                 across().wait_recv()
-                self.close(k, offs[2], s4)
-                outward().start()
+                self.finish(k, offs[2], s4, l4)
+                pl.when(mid)(lambda: outward().start())
 
         elif i == 6:
-            pl.when(z_first)(lambda: back8().wait_recv())
             pl.when(end)(lambda: outward().wait_recv())
             back4().start()
             half_copy().wait_send()
             quarter_copy().wait_send()
-
-            @pl.when(z_first)
-            def _():
-                eighth_copy().wait_send()
-                whole_copy().wait_send()
-
             pl.when(end)(lambda: inward().wait_send())
-            pl.when(mid)(lambda: across().wait_send())
+            pl.when(z_first | mid)(lambda: across().wait_send())
         elif i == 7:
             back4().wait_recv()
             back2().start()
         elif i == 8:
             back2().wait_recv()
         else:
-            pl.when(z_first)(lambda: back8().wait_send())
             pl.when(mid)(lambda: outward().wait_send())
             back4().wait_send()
             back2().wait_send()
@@ -324,11 +291,11 @@
     return jnp.sum(value.reshape(value.shape[0] // 8, 8, value.shape[1]), axis=0)
 
 
-def front_kernel(feat_a, feat_b, w_in, t_in, w_mid, t_mid, w_out, t_out, affine, off_weight, pre1, pre2, act1, act2, dz, grad_emb, vec, loss, *scratch):
-    (x_buf, u_buf, w_buf, stats, ea, eb, g_peer) = scratch[:7]
-    (x_sem, w_sem, keep_sem, ge_sem, e_send, e_recv) = scratch[7:13]
-    small_refs = scratch[13 : 13 + SMALL_REFS]
-    acc, gathered, l1, l2, l3, l4, send, recv = scratch[13 + SMALL_REFS :]
+def front_kernel(feat_a, feat_b, w_in, t_in, w_mid, t_mid, w_out, t_out, gain1, bias1, gain2, bias2, off_weight, pre1, pre2, act1, act2, dz, grad_emb, vec, *scratch):
+    (x_buf, u_buf, w_buf, stats, affine, loss, ea, eb, g_peer) = scratch[:9]
+    (x_sem, w_sem, keep_sem, ge_sem, e_send, e_recv) = scratch[9:15]
+    small_refs = scratch[15 : 15 + SMALL_REFS]
+    acc, gathered, l1, l2, l3, l4, send, recv = scratch[15 + SMALL_REFS :]
     rows_dev, width = feat_a.shape
     wide = w_buf.shape[2]
     tiles = width // wide
@@ -357,6 +324,8 @@
     feat(1).start()
     for g in range(1, W_BUFS - 1):
         start_w(g)
+    for j, ref in enumerate((gain1, bias1, gain2, bias2)):
+        affine[j] = ref[...]
     feat(0).wait()
     payload[...] = jnp.zeros_like(payload)
 
@@ -513,17 +482,18 @@
 
     loss[...] = jnp.zeros_like(loss)
 
-    def finish(k, off, size, buf, buf_off):
+    def finish(k, off, size, buf):
+        share = 0.5 - 0.25 * chunks.z_first(k).astype(jnp.float32)
         at = rows(off, size)
-        corr = (acc[k, at] + buf[k, rows(buf_off, size)]) / row_count
+        corr = (acc[k, at] + buf[k]) / row_count
         row = core * half + k * part_rows + off
         diag = (row + lax.broadcasted_iota(jnp.int32, (size, width), 0)) == lax.broadcasted_iota(jnp.int32, (size, width), 1)
         weight = off_weight[0]
         miss = 1.0 - corr
-        loss[...] += jnp.sum(jnp.where(diag, miss * miss, weight * (corr * corr)), axis=0, keepdims=True)
+        loss[...] += share * jnp.sum(jnp.where(diag, miss * miss, weight * (corr * corr)), axis=0, keepdims=True)
         gathered[k, at] = jnp.where(diag, -2.0 * miss, 2.0 * weight * corr).astype(jnp.bfloat16)
 
-    chunks = ChunkSum(place, FRONT_Z_FIRST, PARTS, acc, gathered, (l1, l2, l3, l4), send, recv, finish)
+    chunks = ChunkSum(place, PARTS, acc, gathered, (l1, l2, l3, l4), send, recv, finish)
 
     def form(k):
         @pl.when(k == 0)
@@ -531,12 +501,12 @@
             ea_copy().wait_recv()
             eb_copy().wait_recv()
 
-        at = rows(k * part_rows, 2 * part_rows)
+        at = rows(k * part_rows, GROUP * part_rows)
         size = min(1024, width)
 
         def col(c):
             cs = rows(c * size, size)
-            acc[pl.ds(k, 2), :, cs] = contract_rows(ea[:, at], eb[:, cs]).reshape(2, part_rows, size)
+            acc[pl.ds(k, GROUP), :, cs] = contract_rows(ea[:, at], eb[:, cs]).reshape(GROUP, part_rows, size)
 
         loop(0, width // size, col)
 
@@ -544,15 +514,15 @@
         return chunks.copy(gathered.at[k], g_peer.at[k], 7, k, place.other_core)
 
     def ge_cols(k, side):
-        return rows(side * half + k * part_rows, 2 * part_rows)
+        return rows(side * half + k * part_rows, GROUP * part_rows)
 
     def ge_copy(k, side):
         at = ge_cols(k, side)
-        return pltpu.make_async_copy(u_buf.at[1, :, at], grad_emb.at[:, at], ge_sem.at[k // 2, side])
+        return pltpu.make_async_copy(u_buf.at[1, :, at], grad_emb.at[:, at], ge_sem.at[k // GROUP, side])
 
     def embed(k, side, g_rows):
         at_cols = ge_cols(k, side)
-        grad = contract_cols(eb[mine], g_rows.reshape(2 * part_rows, width)) / row_count
+        grad = contract_cols(eb[mine], g_rows.reshape(GROUP * part_rows, width)) / row_count
         u_buf[1, :, at_cols] = grad
         ge_copy(k, side).start()
 
@@ -560,29 +530,29 @@
             g = u_buf[1, at, at_cols]
             return sums[0] + fold(g * u_buf[0, at, at_cols]), sums[1] + fold(g)
 
-        zero = jnp.zeros((8, 2 * part_rows), jnp.float32)
+        zero = jnp.zeros((8, GROUP * part_rows), jnp.float32)
         for row, value in enumerate(row_loop(block, (zero, zero))):
             payload[JOBS, (side * half + k * part_rows) // TILE, row : row + 1] = jnp.sum(value, axis=0, keepdims=True)
 
     def stage(i, k):
         if i == 0:
-            pl.when(k % 2 == 0)(lambda: form(k))
+            pl.when(k % GROUP == 0)(lambda: form(k))
             return
         chunks.stage(i, k)
         if i == 8:
             swap(k).start()
 
-            @pl.when(k % 2 == 1)
+            @pl.when(k % GROUP == GROUP - 1)
             def _():
-                embed(k - 1, core, gathered[pl.ds(k - 1, 2)])
+                embed(k - GROUP + 1, core, gathered[pl.ds(k - GROUP + 1, GROUP)])
 
         if i == 9:
             swap(k).wait_recv()
             swap(k).wait_send()
 
-            @pl.when(k % 2 == 1)
+            @pl.when(k % GROUP == GROUP - 1)
             def _():
-                embed(k - 1, 1 - core, g_peer[pl.ds(k - 1, 2)])
+                embed(k - GROUP + 1, 1 - core, g_peer[pl.ds(k - GROUP + 1, GROUP)])
 
     run_slots(PARTS, stage, lambda t: None)
     for c in range(PLANE):
@@ -591,7 +561,7 @@
     ea_copy().wait_send()
     eb_copy().wait_send()
     small.middle(JOBS)
-    for k in range(0, PARTS, 2):
+    for k in range(0, PARTS, GROUP):
         for side in range(2):
             ge_copy(k, side).wait()
     small.last(JOBS)
@@ -613,7 +583,7 @@
     loop(0, tiles, dz_tile)
     keep_act(dz).start()
     for c in range(PLANE):
-        loss[:, c * TILE : (c + 1) * TILE] = total[JOBS, c, 2:3]
+        vec[8, :, c * TILE : (c + 1) * TILE] = total[JOBS, c, 2:3]
     keep_act(dz).wait()
 
 
@@ -630,28 +600,30 @@
         front_kernel,
         name="front",
         out_shape=[wide_f32, wide_f32, wide_bf16, wide_bf16, wide_bf16, wide_f32]
-        + [jax.ShapeDtypeStruct((8, 1, width), jnp.float32), jax.ShapeDtypeStruct((1, width), jnp.float32)],
-        in_specs=[any_spec] * 8 + [vmem_spec, pl.BlockSpec(memory_space=pltpu.SMEM)],
-        out_specs=[any_spec] * 6 + [vmem_spec] * 2,
+        + [jax.ShapeDtypeStruct((9, 1, width), jnp.float32)],
+        in_specs=[any_spec] * 8 + [vmem_spec] * 4 + [pl.BlockSpec(memory_space=pltpu.SMEM)],
+        out_specs=[any_spec] * 6 + [vmem_spec],
         scratch_shapes=[
             pltpu.VMEM((2, rows_dev, width), jnp.bfloat16),
             pltpu.VMEM((2, rows_dev, width), jnp.float32),
             pltpu.VMEM((W_BUFS, width, WIDE), jnp.bfloat16),
             pltpu.VMEM((JOBS, 2, 1, width), jnp.float32),
+            pltpu.VMEM((4, 1, width), jnp.float32),
+            pltpu.VMEM((1, width), jnp.float32),
             pltpu.VMEM((2 * rows_dev, half), jnp.bfloat16),
             pltpu.VMEM((2 * rows_dev, width), jnp.bfloat16),
             pltpu.VMEM((PARTS, part_rows, width), jnp.bfloat16),
             dma((2,)),
             dma((W_BUFS,)),
             dma((2,)),
-            dma((PARTS // 2, 2)),
+            dma((PARTS // GROUP, 2)),
             dma((2,)),
             dma((2,)),
         ]
         + small_scratch(JOBS + 1)
         + chunk_scratch(PARTS, part_rows, width, PARTS, jnp.bfloat16),
         compiler_params=pltpu.CompilerParams(collective_id=0, has_side_effects=True, vmem_limit_bytes=VMEM_BYTES),
-    )(feat_a, feat_b, *weights, affine, off_weight)
+    )(feat_a, feat_b, *weights, *affine, off_weight)
 
 
 def back_kernel(dz_hbm, x2, x1, x0, w_out, w_mid, u2, u1, vec, out2, out1, out0, sums_out, *scratch):
@@ -662,7 +634,6 @@
     rows_dev, width = dz_hbm.shape
     wide = w_buf.shape[1]
     tiles = width // wide
-    per_slot = tiles // 2
     row_count = rows_dev * DEPTH * PLANE
     half = width // 2
     part_rows = half // PARTS
@@ -767,11 +738,11 @@
 
         loop(0, tiles, tile)
 
-    def finish(k, off, size, buf, buf_off):
+    def finish(k, off, size, buf):
         j = k % SLOTS
-        gathered[j, rows(off, size)] = acc[j, rows(off, size)] + buf[j, rows(buf_off, size)]
-
-    chunks = ChunkSum(place, BACK_Z_FIRST, SLOTS, acc, gathered, (l1, l2, l3, l4), send, recv, finish)
+        gathered[j, rows(off, size)] = acc[j, rows(off, size)] + buf[j]
+
+    chunks = ChunkSum(place, SLOTS, acc, gathered, (l1, l2, l3, l4), send, recv, finish)
 
     def form(k):
         w, j = k // PARTS, k % SLOTS
@@ -781,12 +752,12 @@
             x_arrive(w)
             peer_dy(w).wait_recv()
 
-        at = rows((k % PARTS) * part_rows, 2 * part_rows)
+        at = rows((k % PARTS) * part_rows, GROUP * part_rows)
         size = min(1024, width)
 
         def col(c):
             cs = rows(c * size, size)
-            acc[pl.ds(j, 2), :, cs] = contract_rows(xs[w % 2, :, at], dy[w % 2, :, cs]).reshape(2, part_rows, size)
+            acc[pl.ds(j, GROUP), :, cs] = contract_rows(xs[w % 2, :, at], dy[w % 2, :, cs]).reshape(GROUP, part_rows, size)
 
         loop(0, width // size, col)
 
@@ -801,7 +772,7 @@
 
     def stage(i, k):
         if i == 0:
-            pl.when(k % 2 == 0)(lambda: form(k))
+            pl.when(k % GROUP == 0)(lambda: form(k))
             return
         chunks.stage(i, k)
         if i == 8:
@@ -823,12 +794,12 @@
     def layer_work(t):
         layer = t // LAYER_SLOTS
         at = t - LAYER_SLOTS * layer
-        pl.when(at < 2)(lambda: loop(at * per_slot, at * per_slot + per_slot, lambda i: chain_tile(layer, i)))
-        pl.when(at == 2)(lambda: small.begin(layer))
-        pl.when(at == 3)(lambda: small.middle(layer))
-        pl.when(at == 4)(lambda: small.last(layer))
-
-        @pl.when(at == 5)
+        pl.when(at < tiles)(lambda: chain_tile(layer, at))
+        pl.when(at == tiles)(lambda: small.begin(layer))
+        pl.when(at == tiles + 1)(lambda: small.middle(layer))
+        pl.when(at == tiles + 2)(lambda: small.last(layer))
+
+        @pl.when(at == tiles + 3)
         def _():
             small.end(layer)
             pl.when(layer == 1)(lambda: peer_dy(0).wait_send())
@@ -850,7 +821,10 @@
     for w in (1, 2):
         peer_x(w).wait_send()
         peer_dy(w).wait_send()
-    sums_out[...] = sums[...]
+    for c in range(PLANE):
+        for row in range(4):
+            sums_out[row : row + 1, c * TILE : (c + 1) * TILE] = sums[row // 2, c, row % 2 : row % 2 + 1]
+    sums_out[4:5] = jnp.full((1, width), jnp.sum(vec[8]))
 
 
 def backward(grad_z, x2, x1, x0, w_out, w_mid, u2, u1, vec):
@@ -864,7 +838,7 @@
     return pl.pallas_call(
         back_kernel,
         name="backward",
-        out_shape=[mat, mat, mat, jax.ShapeDtypeStruct((2, PLANE, SUM_ROWS, TILE), jnp.float32)],
+        out_shape=[mat, mat, mat, jax.ShapeDtypeStruct((5, width), jnp.float32)],
         in_specs=[any_spec] * 8 + [vmem_spec],
         out_specs=[any_spec] * 3 + [vmem_spec],
         scratch_shapes=[
@@ -890,13 +864,11 @@
     replicated = P()
 
     def local_step(feat_a, feat_b, w_in, w_mid, w_out, t_in, t_mid, t_out, gain_1, bias_1, gain_2, bias_2, off_weight):
-        affine = jnp.stack([gain_1, bias_1, gain_2, bias_2])[:, None, :]
-        pre_1, pre_2, act_1, act_2, grad_z, grad_emb, vec, loss_cols = front(
+        affine = [v.reshape(1, -1) for v in (gain_1, bias_1, gain_2, bias_2)]
+        pre_1, pre_2, act_1, act_2, grad_z, grad_emb, vec = front(
             feat_a, feat_b, (w_in, t_in, w_mid, t_mid, w_out, t_out), affine, off_weight.reshape(1)
         )
-        loss_value = jnp.sum(loss_cols) * 0.5
         grad_w_out, grad_w_mid, grad_w_in, sums = backward(grad_z, act_2, act_1, feat_a, w_out, w_mid, pre_2, pre_1, vec)
-        sums = jnp.transpose(sums[:, :, :2], (0, 2, 1, 3)).reshape(2, 2, -1)
-        return (loss_value, grad_emb, grad_w_in, grad_w_mid, grad_w_out, sums[1, 0], sums[1, 1], sums[0, 0], sums[0, 1])
+        return (sums[4, 0], grad_emb, grad_w_in, grad_w_mid, grad_w_out, sums[2], sums[3], sums[0], sums[1])
 
     return jax.shard_map(local_step, mesh=mesh, in_specs=(row_part, row_part) + (replicated,) * 11, out_specs=(replicated, row_part) + (replicated,) * 7, check_vma=False)

time: 642 us -> 636 us (level)
  no operation moved by 1% of the time
where the time goes in v5:
time: 636 us
  Pallas kernels  593 us (93%)
  local copies, waits for them, and re-layouts  41.2 us (6%)
    pallas_call x1, Pallas kernels, backward(): pl.pallas_call(back_kernel, name='backward', out_shape=[mat, mat, mat, ja...  388 us
    pallas_call x1, Pallas kernels, front(): pl.pallas_call(front_kernel, name='front', out_shape=[wide_f32, wide_f32,...  205 us
    unnamed x14, local copies, waits for them, and re-layouts  38.4 us

profile of v5, /device:TPU:0, one launch (start us, length us, event | category | flops | bytes accessed | tf_op | source)
XLA Modules:
  0.0 635.6 jit_solution(15172875283720533202)
XLA Ops:
  1.3 204.7 %front.1 = (f32[512,2048]{1,0:T(8,128)}, f32[512,2048]{1,0:T(8,128)}, bf16[512,2048]{1,0:T(8,128)(2,1)}, bf16[512,2048]{1,0:T(8,128)(2,1)}, bf16[512,2048]{1,0:T...) custom-call(bf16[512,2048]{1,0:T(8,128)(2,1)} %x0.1, bf16[512,2048]{1,0:T(8,128)(2,1)} %feat_b.1, ...), custom_call_target="tpu_custom_call" | custom-call | tf_op jit(solution)/shard_map/front/pallas_call | solution.py:599
  206.0 388.5 %backward.1 = (f32[2048,2048]{1,0:T(8,128)}, f32[2048,2048]{1,0:T(8,128)}, f32[2048,2048]{1,0:T(8,128)}, f32[5,2048]{1,0:T(8,128)}) custom-call(bf16[512,2048]{1,0:T(8,128)(2,1)} %get-tuple-element.20.dz_hbm, bf16[512,2048]{1,0:T(8,128)(2,1)} %get-tuple-element.21.x2, bf16[512,2048]{1,0:T(8,128)(2,1)} %get-tuple-element.22.x1, bf16[512,2048]{1,0:T(8,128)(2,1)} %x0.1, ...), custom_call_target="tpu_custom_call" | custom-call | tf_op jit(solution)/shard_map/backward/pallas_call | solution.py:838
  594.5 1.6 fusion
  596.1 1.2 slice.15
  597.3 4.7 copy.27
  602.0 0.0 copy-start
  602.0 0.0 slice-start
  602.0 0.0 slice-start.1
  602.0 0.0 slice-start.2
  602.0 13.5 %copy.28 = f32[2048,2048]{1,0:T(8,128)} copy(f32[2048,2048]{1,0:T(8,128)} %get-tuple-element.46) | data formatting | bytes 33554432
  615.5 2.9 copy-done
  618.4 0.0 slice-start.3
  618.4 8.5 %copy.29 = f32[2048,2048]{1,0:T(8,128)} copy(f32[2048,2048]{1,0:T(8,128)S(1)} %copy-done) | data formatting | bytes 33554432
  626.9 0.0 slice-done
  626.9 0.0 slice-done.1
  626.9 1.1 slice-done.2
  628.0 1.4 slice-done.3
  629.5 6.2 copy.30
  (1 shorter events, 0.0 us)
Async XLA Ops:
  602.0 16.4 %copy-start = (f32[2048,2048]{1,0:T(8,128)S(1)}, f32[2048,2048]{1,0:T(8,128)}, u32[]{:S(2)}) copy-start(f32[2048,2048]{1,0:T(8,128)} %get-tuple-element.47) | copy-start | bytes 50331652
  602.0 24.9 %slice-start = ((s8[16777216]{0:T(1024)(128)(4,1)}), s8[4194304]{0:T(1024)(128)(4,1)S(1)}, s32[]{:S(2)}) async-start(s8[16777216]{0:T(1024)(128)(4,1)} %bitcast.11), calls=%async_computation | async-start | bytes 8388608
  602.0 24.9 %slice-start.1 = ((s8[16777216]{0:T(1024)(128)(4,1)}), s8[4194304]{0:T(1024)(128)(4,1)S(1)}, s32[]{:S(2)}) async-start(s8[16777216]{0:T(1024)(128)(4,1)} %bitcast.11), calls=%async_computation.1 | async-start | bytes 8388608
  602.0 26.1 %slice-start.2 = ((s8[16777216]{0:T(1024)(128)(4,1)}), s8[4194304]{0:T(1024)(128)(4,1)S(1)}, s32[]{:S(2)}) async-start(s8[16777216]{0:T(1024)(128)(4,1)} %bitcast.11), calls=%async_computation.2 | async-start | bytes 8388608
  618.4 11.1 %slice-start.3 = ((s8[16777216]{0:T(1024)(128)(4,1)}), s8[4194304]{0:T(1024)(128)(4,1)S(1)}, s32[]{:S(2)}) async-start(s8[16777216]{0:T(1024)(128)(4,1)} %bitcast.11), calls=%async_computation.3 | async-start | bytes 8388608

commit v6 on v5

--- a/solution.py
+++ b/solution.py
@@ -20,13 +20,13 @@
 PARTS = 16
 GROUP = 4
 MATS = 3
-SLOTS = 16
+ACC_SLOTS = 20
+GATHER_SLOTS = 16
 JOBS = 6
 W_BUFS = 3
 LAYER_SLOTS = 8
-LAGS = (0, 0, 2, 4, 5, 6, 7, 8, 10, 12)
-ORDER = (0, 1, 5, 4, 6, 3, 7, 2, 8, 9)
-Z_FIRST_EVERY, Z_FIRST_AT = 4, 2
+FRONT_PLAN = ((0, 0, 3, 5, 7, 10, 11, 13, 17, 19), (0, 1, 3, 4, 6, 5, 2, 9, 8, 7), (5, 2))
+BACK_PLAN = ((0, 0, 5, 7, 10, 12, 13, 16, 20, 23), (0, 1, 9, 5, 3, 2, 8, 7, 4, 6), (4, 2))
 
 
 def contract_rows(left_op, right_op):
@@ -150,8 +150,8 @@
 
 
 class ChunkSum:
-    def __init__(self, place, slots, acc, gathered, landing, send, recv, finish):
-        self.p, self.slots = place, slots
+    def __init__(self, place, z_first, acc, gathered, landing, send, recv, finish):
+        self.p, self.z_first_plan, self.slots, self.gather_slots = place, z_first, acc.shape[0], gathered.shape[0]
         self.acc, self.gathered, self.landing, self.send, self.recv, self.finish = acc, gathered, landing, send, recv, finish
         self.size = acc.shape[1]
         core, bx, by = place.core, place.bx, place.by
@@ -162,7 +162,8 @@
         self.mid_mate = place.me + 8 * (1 - 2 * place.bz1)
 
     def z_first(self, k):
-        off = k % Z_FIRST_EVERY - Z_FIRST_AT
+        every, at = self.z_first_plan
+        off = k % every - at
         return 1 - lax.min(off * off, 1)
 
     def steps(self, k):
@@ -184,7 +185,7 @@
         return self.copy(self.acc.at[j, rows(off, size)], self.landing[stage].at[j], stage, k, mate)
 
     def up(self, stage, k, off, size, mate):
-        block = self.gathered.at[k % self.slots, rows(off, size)]
+        block = self.gathered.at[k % self.gather_slots, rows(off, size)]
         return self.copy(block, block, stage, k, mate)
 
     def add(self, k, off, size, buf):
@@ -258,10 +259,12 @@
             back2().wait_send()
 
 
-def run_slots(count, stage, between):
+def run_slots(plan, count, stage, between):
+    lags, order, _ = plan
+
     def slot(t):
-        for i in ORDER:
-            k = t - LAGS[i]
+        for i in order:
+            k = t - lags[i]
 
             @pl.when((k >= 0) & (k < count))
             def _():
@@ -270,15 +273,17 @@
             if i == 1:
                 between(t)
 
-    loop(0, count + LAGS[-1], slot)
-
-
-def chunk_scratch(slots, part_rows, width, count, dtype):
-    def buf(n, kind=jnp.float32):
-        return pltpu.VMEM((slots, n, width), kind)
+    loop(0, count + lags[-1], slot)
+
+
+def chunk_scratch(slots, gather_slots, part_rows, width, count, dtype):
+    def buf(n):
+        return pltpu.VMEM((slots, n, width), jnp.float32)
+
+    gathered = pltpu.VMEM((gather_slots, part_rows, width), dtype)
 
     dma = pltpu.SemaphoreType.DMA
-    return [buf(part_rows), buf(part_rows, dtype), buf(part_rows // 2), buf(part_rows // 4), buf(part_rows // 4), buf(part_rows // 4)] + [
+    return [buf(part_rows), gathered, buf(part_rows // 2), buf(part_rows // 4), buf(part_rows // 4), buf(part_rows // 4)] + [
         dma((8, count)),
         dma((8, count)),
     ]
@@ -493,7 +498,7 @@
         loss[...] += share * jnp.sum(jnp.where(diag, miss * miss, weight * (corr * corr)), axis=0, keepdims=True)
         gathered[k, at] = jnp.where(diag, -2.0 * miss, 2.0 * weight * corr).astype(jnp.bfloat16)
 
-    chunks = ChunkSum(place, PARTS, acc, gathered, (l1, l2, l3, l4), send, recv, finish)
+    chunks = ChunkSum(place, FRONT_PLAN[2], acc, gathered, (l1, l2, l3, l4), send, recv, finish)
 
     def form(k):
         @pl.when(k == 0)
@@ -554,7 +559,7 @@
             def _():
                 embed(k - GROUP + 1, 1 - core, g_peer[pl.ds(k - GROUP + 1, GROUP)])
 
-    run_slots(PARTS, stage, lambda t: None)
+    run_slots(FRONT_PLAN, PARTS, stage, lambda t: None)
     for c in range(PLANE):
         payload[JOBS, c, 2:3] = loss[:, c * TILE : (c + 1) * TILE]
     small.begin(JOBS)
@@ -621,7 +626,7 @@
             dma((2,)),
         ]
         + small_scratch(JOBS + 1)
-        + chunk_scratch(PARTS, part_rows, width, PARTS, jnp.bfloat16),
+        + chunk_scratch(PARTS, PARTS, part_rows, width, PARTS, jnp.bfloat16),
         compiler_params=pltpu.CompilerParams(collective_id=0, has_side_effects=True, vmem_limit_bytes=VMEM_BYTES),
     )(feat_a, feat_b, *weights, *affine, off_weight)
 
@@ -739,13 +744,13 @@
         loop(0, tiles, tile)
 
     def finish(k, off, size, buf):
-        j = k % SLOTS
-        gathered[j, rows(off, size)] = acc[j, rows(off, size)] + buf[j]
-
-    chunks = ChunkSum(place, SLOTS, acc, gathered, (l1, l2, l3, l4), send, recv, finish)
+        j = k % ACC_SLOTS
+        gathered[k % GATHER_SLOTS, rows(off, size)] = acc[j, rows(off, size)] + buf[j]
+
+    chunks = ChunkSum(place, BACK_PLAN[2], acc, gathered, (l1, l2, l3, l4), send, recv, finish)
 
     def form(k):
-        w, j = k // PARTS, k % SLOTS
+        w, j = k // PARTS, k % ACC_SLOTS
 
         @pl.when(k % PARTS == 0)
         def _():
@@ -765,10 +770,10 @@
         return pl.ds(pl.multiple_of(side * half + (k % PARTS) * part_rows, part_rows), part_rows)
 
     def last_copy(out, k, side):
-        return chunks.copy(gathered.at[k % SLOTS], out.at[out_rows(k, side)], 7, k, other_core)
+        return chunks.copy(gathered.at[k % GATHER_SLOTS], out.at[out_rows(k, side)], 7, k, other_core)
 
     def store_copy(out, k):
-        return pltpu.make_async_copy(gathered.at[k % SLOTS], out.at[out_rows(k, core)], store_sem.at[k])
+        return pltpu.make_async_copy(gathered.at[k % GATHER_SLOTS], out.at[out_rows(k, core)], store_sem.at[k])
 
     def stage(i, k):
         if i == 0:
@@ -817,7 +822,7 @@
                 own_x(2).start()
                 peer_x(2).start()
 
-    run_slots(count, stage, lambda t: pl.when(t < 2 * LAYER_SLOTS)(lambda: layer_work(t)))
+    run_slots(BACK_PLAN, count, stage, lambda t: pl.when(t < 2 * LAYER_SLOTS)(lambda: layer_work(t)))
     for w in (1, 2):
         peer_x(w).wait_send()
         peer_dy(w).wait_send()
@@ -854,7 +859,7 @@
             dma((count,)),
         ]
         + small_scratch(2)
-        + chunk_scratch(SLOTS, part_rows, width, count, jnp.float32),
+        + chunk_scratch(ACC_SLOTS, GATHER_SLOTS, part_rows, width, count, jnp.float32),
         compiler_params=pltpu.CompilerParams(collective_id=1, has_side_effects=True, vmem_limit_bytes=VMEM_BYTES),
     )(grad_z, x2, x1, x0, w_out, w_mid, u2, u1, vec)
 

time: 636 us -> 607 us (0.954)
  Pallas kernels: 593 us -> 564 us
    pallas_call x1, Pallas kernels: 205 us -> 185 us  [front(): pl.pallas_call(front_kernel, name='front', out_shape=[wide_f32, wide_f32,...]
    pallas_call x1, Pallas kernels: 388 us -> 378 us  [backward(): pl.pallas_call(back_kernel, name='backward', out_shape=[mat, mat, mat, ja...]
where the time goes in v6:
time: 607 us; the launch traced here: 606 us
  Pallas kernels  564 us (93%)
  local copies, waits for them, and re-layouts  41.2 us (7%)
    pallas_call x1, Pallas kernels, backward(): pl.pallas_call(back_kernel, name='backward', out_shape=[mat, mat, mat, ja...  378 us
    pallas_call x1, Pallas kernels, front(): pl.pallas_call(front_kernel, name='front', out_shape=[wide_f32, wide_f32,...  185 us
    unnamed x14, local copies, waits for them, and re-layouts  38.4 us

profile of v6, /device:TPU:0, one launch (start us, length us, event | category | flops | bytes accessed | tf_op | source)
XLA Modules:
  0.0 606.0 jit_solution(233350950935375681)
XLA Ops:
  1.3 185.3 %front.1 = (f32[512,2048]{1,0:T(8,128)}, f32[512,2048]{1,0:T(8,128)}, bf16[512,2048]{1,0:T(8,128)(2,1)}, bf16[512,2048]{1,0:T(8,128)(2,1)}, bf16[512,2048]{1,0:T...) custom-call(bf16[512,2048]{1,0:T(8,128)(2,1)} %x0.1, bf16[512,2048]{1,0:T(8,128)(2,1)} %feat_b.1, ...), custom_call_target="tpu_custom_call" | custom-call | tf_op jit(solution)/shard_map/front/pallas_call | solution.py:604
  186.6 378.2 %backward.1 = (f32[2048,2048]{1,0:T(8,128)}, f32[2048,2048]{1,0:T(8,128)}, f32[2048,2048]{1,0:T(8,128)}, f32[5,2048]{1,0:T(8,128)}) custom-call(bf16[512,2048]{1,0:T(8,128)(2,1)} %get-tuple-element.20.dz_hbm, bf16[512,2048]{1,0:T(8,128)(2,1)} %get-tuple-element.21.x2, bf16[512,2048]{1,0:T(8,128)(2,1)} %get-tuple-element.22.x1, bf16[512,2048]{1,0:T(8,128)(2,1)} %x0.1, ...), custom_call_target="tpu_custom_call" | custom-call | tf_op jit(solution)/shard_map/backward/pallas_call | solution.py:843
  564.8 1.6 fusion
  566.5 1.2 slice.15
  567.6 4.7 copy.27
  572.3 0.0 copy-start
  572.3 0.0 slice-start
  572.3 0.0 slice-start.1
  572.3 0.0 slice-start.2
  572.3 13.5 %copy.28 = f32[2048,2048]{1,0:T(8,128)} copy(f32[2048,2048]{1,0:T(8,128)} %get-tuple-element.46) | data formatting | bytes 33554432
  585.9 2.9 copy-done
  588.8 0.0 slice-start.3
  588.8 8.5 %copy.29 = f32[2048,2048]{1,0:T(8,128)} copy(f32[2048,2048]{1,0:T(8,128)S(1)} %copy-done) | data formatting | bytes 33554432
  597.3 0.0 slice-done
  597.3 0.0 slice-done.1
  597.3 1.1 slice-done.2
  598.4 1.4 slice-done.3
  599.8 6.2 %copy.30 = f32[2048,2048]{1,0:T(8,128)} copy(f32[2048,2048]{1,0:T(8,128)S(1)} %bitcast.12) | data formatting | bytes 33554432
  (1 shorter events, 0.0 us)
Async XLA Ops:
  572.3 16.4 %copy-start = (f32[2048,2048]{1,0:T(8,128)S(1)}, f32[2048,2048]{1,0:T(8,128)}, u32[]{:S(2)}) copy-start(f32[2048,2048]{1,0:T(8,128)} %get-tuple-element.47) | copy-start | bytes 50331652
  572.3 24.9 %slice-start = ((s8[16777216]{0:T(1024)(128)(4,1)}), s8[4194304]{0:T(1024)(128)(4,1)S(1)}, s32[]{:S(2)}) async-start(s8[16777216]{0:T(1024)(128)(4,1)} %bitcast.11), calls=%async_computation | async-start | bytes 8388608
  572.3 24.9 %slice-start.1 = ((s8[16777216]{0:T(1024)(128)(4,1)}), s8[4194304]{0:T(1024)(128)(4,1)S(1)}, s32[]{:S(2)}) async-start(s8[16777216]{0:T(1024)(128)(4,1)} %bitcast.11), calls=%async_computation.1 | async-start | bytes 8388608
  572.3 26.1 %slice-start.2 = ((s8[16777216]{0:T(1024)(128)(4,1)}), s8[4194304]{0:T(1024)(128)(4,1)S(1)}, s32[]{:S(2)}) async-start(s8[16777216]{0:T(1024)(128)(4,1)} %bitcast.11), calls=%async_computation.2 | async-start | bytes 8388608
  588.8 11.1 %slice-start.3 = ((s8[16777216]{0:T(1024)(128)(4,1)}), s8[4194304]{0:T(1024)(128)(4,1)S(1)}, s32[]{:S(2)}) async-start(s8[16777216]{0:T(1024)(128)(4,1)} %bitcast.11), calls=%async_computation.3 | async-start | bytes 8388608

commit v7 on v6

--- a/solution.py
+++ b/solution.py
@@ -24,7 +24,9 @@
 GATHER_SLOTS = 16
 JOBS = 6
 W_BUFS = 3
-LAYER_SLOTS = 8
+LAYER_SLOTS = 15
+COPY_ROWS = 256
+COPY_BUFS = 12
 FRONT_PLAN = ((0, 0, 3, 5, 7, 10, 11, 13, 17, 19), (0, 1, 3, 4, 6, 5, 2, 9, 8, 7), (5, 2))
 BACK_PLAN = ((0, 0, 5, 7, 10, 12, 13, 16, 20, 23), (0, 1, 9, 5, 3, 2, 8, 7, 4, 6), (4, 2))
 
@@ -296,11 +298,11 @@
     return jnp.sum(value.reshape(value.shape[0] // 8, 8, value.shape[1]), axis=0)
 
 
-def front_kernel(feat_a, feat_b, w_in, t_in, w_mid, t_mid, w_out, t_out, gain1, bias1, gain2, bias2, off_weight, pre1, pre2, act1, act2, dz, grad_emb, vec, *scratch):
+def front_kernel(feat_a, feat_b, w_in, t_in, w_mid, t_mid, w_out, t_out, gain1, bias1, gain2, bias2, off_weight, pre1, pre2, xs2, xs1, xs0, dz, grad_emb, vec, *scratch):
     (x_buf, u_buf, w_buf, stats, affine, loss, ea, eb, g_peer) = scratch[:9]
-    (x_sem, w_sem, keep_sem, ge_sem, e_send, e_recv) = scratch[9:15]
-    small_refs = scratch[15 : 15 + SMALL_REFS]
-    acc, gathered, l1, l2, l3, l4, send, recv = scratch[15 + SMALL_REFS :]
+    (x_sem, w_sem, pre_sem, keep_sem, keep_send, keep_recv, ge_sem, e_send, e_recv) = scratch[9:18]
+    small_refs = scratch[18 : 18 + SMALL_REFS]
+    acc, gathered, l1, l2, l3, l4, send, recv = scratch[18 + SMALL_REFS :]
     rows_dev, width = feat_a.shape
     wide = w_buf.shape[2]
     tiles = width // wide
@@ -335,10 +337,29 @@
     payload[...] = jnp.zeros_like(payload)
 
     def keep_pre(ref):
-        return pltpu.make_async_copy(u_buf.at[0], ref, keep_sem.at[0])
-
-    def keep_act(ref):
-        return pltpu.make_async_copy(x_buf.at[0], ref, keep_sem.at[1])
+        return pltpu.make_async_copy(u_buf.at[0], ref, pre_sem.at[0])
+
+    kept = (xs0, xs1, xs2)
+
+    def keep_x(w):
+        here = pltpu.make_async_copy(x_buf.at[0, :, rows(core * half, half)], kept[w].at[mine], keep_sem.at[w])
+        there = remote_copy(x_buf.at[0, :, rows((1 - core) * half, half)], kept[w].at[mine], keep_send.at[w], keep_recv.at[w], place.other_core)
+        return here, there
+
+    def start_x(w):
+        for c in keep_x(w):
+            c.start()
+
+    def free_x(w):
+        here, there = keep_x(w)
+        here.wait()
+        there.wait_send()
+
+    def keep_dz(i):
+        at = (slice(None), rows(i * wide, wide))
+        here = pltpu.make_async_copy(x_buf.at[(0, *at)], dz.at[mine, at[1]], keep_sem.at[3 + i])
+        there = remote_copy(x_buf.at[(0, *at)], dz.at[mine, at[1]], keep_send.at[3 + i], keep_recv.at[3 + i], place.other_core)
+        return here, there
 
     def row_loop(body, carry):
         return lax.fori_loop(0, rows_dev // BLOCK, lambda r, c: body(rows(r * BLOCK, BLOCK), c), carry)
@@ -380,13 +401,7 @@
             stats[job, 0, :, at] = means[0:1]
             stats[job, 1, :, at] = lax.rsqrt(means[1:2] - means[0:1] * means[0:1] + NORM_EPS)
 
-        @pl.when((view == 0) & (layer == 1))
-        def _():
-            keep_act(act1).wait()
-
-        @pl.when((view == 0) & (layer == 2))
-        def _():
-            keep_act(act2).wait()
+        pl.when(view == 0)(lambda: pick(layer, (0, 1, 2), free_x))
 
         def hidden(i):
             at_cols = rows(i * wide, wide)
@@ -436,7 +451,7 @@
 
             @pl.when(view == 0)
             def _():
-                pick(layer, (act1, act2), lambda ref: keep_act(ref).start())
+                pick(layer, (1, 2), start_x)
                 keep_pre(pre1).wait()
 
         @pl.when((layer == 2) & (view == 0))
@@ -458,28 +473,22 @@
         view = job % 2
         pl.when(g == tiles)(lambda: feat(1).wait())
         product(g)
-        pl.when(g == tiles - 1)(lambda: place.all_here())
-
-        @pl.when((view == 0) & (i == 0) & (job > 0))
-        def _():
-            small.last(job - 1)
-
-        @pl.when((view == 1) & (i == tiles // 2 - 1))
-        def _():
-            small.middle(job - 1)
+
+        @pl.when(g == 0)
+        def _():
+            place.all_here()
+            start_x(0)
+
+        pl.when((i == 0) & (job > 0))(lambda: small.middle(job - 1))
+        pl.when((i == tiles - 2) & (job > 0))(lambda: small.last(job - 1))
 
         @pl.when(i == tiles - 1)
         def _():
             begin(job)
-
-            @pl.when(view == 1)
-            def _():
-                small.last(job - 1)
-                small.middle(job)
-
             pl.when(job > 0)(lambda: norm(job - 1))
 
     loop(0, JOBS * tiles, step)
+    small.middle(JOBS - 1)
     small.last(JOBS - 1)
     norm(JOBS - 1)
     for j, source in enumerate((affine.at[2], affine.at[3], stats.at[2, 0], stats.at[2, 1], affine.at[0], affine.at[1], stats.at[0, 0], stats.at[0, 1])):
@@ -584,12 +593,18 @@
             return c
 
         row_loop(block, 0)
+        for c in keep_dz(i):
+            c.start()
 
     loop(0, tiles, dz_tile)
-    keep_act(dz).start()
     for c in range(PLANE):
         vec[8, :, c * TILE : (c + 1) * TILE] = total[JOBS, c, 2:3]
-    keep_act(dz).wait()
+    for w in range(3):
+        keep_x(w)[1].wait_recv()
+    for i in range(tiles):
+        here, there = keep_dz(i)
+        here.wait()
+        there.wait()
 
 
 def front(feat_a, feat_b, weights, affine, off_weight):
@@ -599,15 +614,17 @@
     any_spec = pl.BlockSpec(memory_space=pl.ANY)
     vmem_spec = pl.BlockSpec(memory_space=pltpu.VMEM)
     wide_f32 = jax.ShapeDtypeStruct((rows_dev, width), jnp.float32)
-    wide_bf16 = jax.ShapeDtypeStruct((rows_dev, width), jnp.bfloat16)
+    kept = jax.ShapeDtypeStruct((2 * rows_dev, half), jnp.bfloat16)
+    both_dz = jax.ShapeDtypeStruct((2 * rows_dev, width), jnp.bfloat16)
+    keeps = 3 + width // WIDE
     dma = pltpu.SemaphoreType.DMA
     return pl.pallas_call(
         front_kernel,
         name="front",
-        out_shape=[wide_f32, wide_f32, wide_bf16, wide_bf16, wide_bf16, wide_f32]
+        out_shape=[wide_f32, wide_f32, kept, kept, kept, both_dz, wide_f32]
         + [jax.ShapeDtypeStruct((9, 1, width), jnp.float32)],
         in_specs=[any_spec] * 8 + [vmem_spec] * 4 + [pl.BlockSpec(memory_space=pltpu.SMEM)],
-        out_specs=[any_spec] * 6 + [vmem_spec],
+        out_specs=[any_spec] * 7 + [vmem_spec],
         scratch_shapes=[
             pltpu.VMEM((2, rows_dev, width), jnp.bfloat16),
             pltpu.VMEM((2, rows_dev, width), jnp.float32),
@@ -620,7 +637,10 @@
             pltpu.VMEM((PARTS, part_rows, width), jnp.bfloat16),
             dma((2,)),
             dma((W_BUFS,)),
-            dma((2,)),
+            dma((1,)),
+            dma((keeps,)),
+            dma((keeps,)),
+            dma((keeps,)),
             dma((PARTS // GROUP, 2)),
             dma((2,)),
             dma((2,)),
@@ -636,7 +656,7 @@
     (in_sem, tile_sem, peer_send, peer_recv, store_sem) = scratch[5:10]
     small_refs = scratch[10 : 10 + SMALL_REFS]
     acc, gathered, l1, l2, l3, l4, send, recv = scratch[10 + SMALL_REFS :]
-    rows_dev, width = dz_hbm.shape
+    rows_dev, width = dpre.shape
     wide = w_buf.shape[1]
     tiles = width // wide
     row_count = rows_dev * DEPTH * PLANE
@@ -651,20 +671,12 @@
     small = small_sum(place, small_refs)
     payload, sums = small.payload, small.total
 
-    def own_x(w):
-        return pltpu.make_async_copy(mats_in[w].at[:, rows(core * half, half)], xs.at[w % 2, mine], in_sem.at[w])
-
-    def peer_x(w):
-        return remote_copy(mats_in[w].at[:, rows((1 - core) * half, half)], xs.at[w % 2, mine], peer_send.at[w], peer_recv.at[w], other_core)
+    def load_x(w):
+        return pltpu.make_async_copy(mats_in[w], xs.at[w % 2], in_sem.at[w])
 
     def peer_dy(w):
         block = dy.at[w % 2, mine]
-        return remote_copy(block, block, peer_send.at[MATS + w], peer_recv.at[MATS + w], other_core)
-
-    def x_arrive(w):
-        block = xs.at[w % 2, mine]
-        pltpu.make_async_copy(block, block, in_sem.at[w]).wait()
-        remote_copy(block, block, peer_send.at[w], peer_recv.at[w], other_core).wait_recv()
+        return remote_copy(block, block, peer_send.at[w], peer_recv.at[w], other_core)
 
     def w_tile(ref, i):
         return pltpu.make_async_copy(ref.at[rows(i * wide, wide)], w_buf.at[i % 2], tile_sem.at[0, i % 2])
@@ -678,18 +690,13 @@
     def start_u(layer, i):
         pick(layer, pres, lambda ref: u_tile(ref, i).start())
 
-    dz_load = pltpu.make_async_copy(dz_hbm, dy.at[0, mine], in_sem.at[MATS])
+    dz_load = pltpu.make_async_copy(dz_hbm, dy.at[0], in_sem.at[MATS])
     dz_load.start()
-    for w in range(2):
-        own_x(w).start()
+    load_x(0).start()
     w_tile(weights[0], 0).start()
     u_tile(pres[0], 0).start()
+    load_x(1).start()
     payload[...] = jnp.zeros_like(payload)
-    place.all_here()
-    peer_x(0).start()
-    dz_load.wait()
-    peer_dy(0).start()
-    peer_x(1).start()
 
     def row_loop(body, carry):
         return lax.fori_loop(0, rows_dev // BLOCK, body, carry)
@@ -720,28 +727,23 @@
             for c in range(wide // TILE):
                 payload[layer, i * (wide // TILE) + c, row : row + 1] = value[:, c * TILE : (c + 1) * TILE]
 
-    def du(layer):
-        start_u(layer, 0)
-
-        def tile(i):
-            u_tile(u2, i).wait()
-            pl.when(i + 1 < tiles)(lambda: start_u(layer, i + 1))
-            at_cols = rows(i * wide, wide)
-            gain, mean, inv = (vec[layer * 4 + j, :, at_cols] for j in (0, 2, 3))
-            means = jnp.concatenate([sums[layer, i * (wide // TILE) + c] for c in range(wide // TILE)], axis=1) / row_count
-            mean_gn, mean_g = means[0:1], means[1:2]
-            scale = gain * inv
-
-            def block(r, c):
-                at = rows(r * BLOCK, BLOCK)
-                n = (u_buf[i % 2, at] - mean) * inv
-                value = (dpre[at, at_cols] - mean_g - n * mean_gn) * scale
-                dy[1 - layer, rows(core * rows_dev + r * BLOCK, BLOCK), at_cols] = value.astype(jnp.bfloat16)
-                return c
-
-            row_loop(block, 0)
-
-        loop(0, tiles, tile)
+    def du_tile(layer, i):
+        u_tile(u2, i).wait()
+        pl.when(i + 1 < tiles)(lambda: start_u(layer, i + 1))
+        at_cols = rows(i * wide, wide)
+        gain, mean, inv = (vec[layer * 4 + j, :, at_cols] for j in (0, 2, 3))
+        means = jnp.concatenate([sums[layer, i * (wide // TILE) + c] for c in range(wide // TILE)], axis=1) / row_count
+        mean_gn, mean_g = means[0:1], means[1:2]
+        scale = gain * inv
+
+        def block(r, c):
+            at = rows(r * BLOCK, BLOCK)
+            n = (u_buf[i % 2, at] - mean) * inv
+            value = (dpre[at, at_cols] - mean_g - n * mean_gn) * scale
+            dy[1 - layer, rows(core * rows_dev + r * BLOCK, BLOCK), at_cols] = value.astype(jnp.bfloat16)
+            return c
+
+        row_loop(block, 0)
 
     def finish(k, off, size, buf):
         j = k % ACC_SLOTS
@@ -754,8 +756,8 @@
 
         @pl.when(k % PARTS == 0)
         def _():
-            x_arrive(w)
-            peer_dy(w).wait_recv()
+            pltpu.make_async_copy(xs.at[w % 2], xs.at[w % 2], in_sem.at[w]).wait()
+            pl.when(w > 0)(lambda: peer_dy(w).wait_recv())
 
         at = rows((k % PARTS) * part_rows, GROUP * part_rows)
         size = min(1024, width)
@@ -777,7 +779,7 @@
 
     def stage(i, k):
         if i == 0:
-            pl.when(k % GROUP == 0)(lambda: form(k))
+            pl.when((k % GROUP == 0) & (k > 0))(lambda: form(k))
             return
         chunks.stage(i, k)
         if i == 8:
@@ -799,16 +801,21 @@
     def layer_work(t):
         layer = t // LAYER_SLOTS
         at = t - LAYER_SLOTS * layer
-        pl.when(at < tiles)(lambda: chain_tile(layer, at))
-        pl.when(at == tiles)(lambda: small.begin(layer))
-        pl.when(at == tiles + 1)(lambda: small.middle(layer))
-        pl.when(at == tiles + 2)(lambda: small.last(layer))
-
-        @pl.when(at == tiles + 3)
-        def _():
-            small.end(layer)
-            pl.when(layer == 1)(lambda: peer_dy(0).wait_send())
-            du(layer)
+        first_du = 2 * tiles + 3
+        pl.when((at < 2 * tiles) & (at % 2 == 1))(lambda: chain_tile(layer, at // 2))
+        pl.when(at == 2 * tiles)(lambda: small.begin(layer))
+        pl.when(at == 2 * tiles + 1)(lambda: small.middle(layer))
+
+        @pl.when(at == 2 * tiles + 2)
+        def _():
+            small.last(layer)
+            start_u(layer, 0)
+
+        pl.when(at == first_du)(lambda: small.end(layer))
+        pl.when(at >= first_du)(lambda: du_tile(layer, at - first_du))
+
+        @pl.when(at == LAYER_SLOTS - 1)
+        def _():
             peer_dy(layer + 1).start()
 
             @pl.when(layer == 0)
@@ -816,15 +823,13 @@
                 w_tile(weights[1], 0).start()
                 u_tile(pres[1], 0).start()
 
-            @pl.when(layer == 1)
-            def _():
-                peer_x(0).wait_send()
-                own_x(2).start()
-                peer_x(2).start()
-
+            pl.when(layer == 1)(lambda: load_x(2).start())
+
+    dz_load.wait()
+    form(0)
+    place.all_here()
     run_slots(BACK_PLAN, count, stage, lambda t: pl.when(t < 2 * LAYER_SLOTS)(lambda: layer_work(t)))
     for w in (1, 2):
-        peer_x(w).wait_send()
         peer_dy(w).wait_send()
     for c in range(PLANE):
         for row in range(4):
@@ -833,7 +838,7 @@
 
 
 def backward(grad_z, x2, x1, x0, w_out, w_mid, u2, u1, vec):
-    rows_dev, width = grad_z.shape
+    rows_dev, width = u2.shape
     part_rows = width // 2 // PARTS
     count = MATS * PARTS
     any_spec = pl.BlockSpec(memory_space=pl.ANY)
@@ -854,8 +859,8 @@
             pltpu.VMEM((rows_dev, width), jnp.float32),
             dma((MATS + 1,)),
             dma((2, 2)),
-            dma((2 * MATS,)),
-            dma((2 * MATS,)),
+            dma((MATS,)),
+            dma((MATS,)),
             dma((count,)),
         ]
         + small_scratch(2)
@@ -864,16 +869,58 @@
     )(grad_z, x2, x1, x0, w_out, w_mid, u2, u1, vec)
 
 
+def copy_kernel(*refs):
+    pairs = len(refs[:-3]) // 2
+    ins, outs, (buf, in_sem, out_sem) = refs[:pairs], refs[pairs : 2 * pairs], refs[2 * pairs :]
+    blocks = [(i, r) for i in range(pairs) for r in range(0, ins[i].shape[0], COPY_ROWS)]
+
+    def read(b):
+        i, r = blocks[b]
+        return pltpu.make_async_copy(ins[i].at[pl.ds(r, COPY_ROWS)], buf.at[b % COPY_BUFS], in_sem.at[b % COPY_BUFS])
+
+    def write(b):
+        i, r = blocks[b]
+        return pltpu.make_async_copy(buf.at[b % COPY_BUFS], outs[i].at[pl.ds(r, COPY_ROWS)], out_sem.at[b % COPY_BUFS])
+
+    ahead = COPY_BUFS // 2
+    for b in range(min(ahead, len(blocks))):
+        read(b).start()
+    for b in range(len(blocks)):
+        if b + ahead < len(blocks):
+            if b + ahead >= COPY_BUFS:
+                write(b + ahead - COPY_BUFS).wait()
+            read(b + ahead).start()
+        read(b).wait()
+        write(b).start()
+    for b in range(max(0, len(blocks) - COPY_BUFS), len(blocks)):
+        write(b).wait()
+
+
+def copy_out(*arrays):
+    any_spec = pl.BlockSpec(memory_space=pl.ANY)
+    dma = pltpu.SemaphoreType.DMA
+    return pl.pallas_call(
+        copy_kernel,
+        name="copy_out",
+        out_shape=[jax.ShapeDtypeStruct(a.shape, a.dtype) for a in arrays],
+        in_specs=[any_spec] * len(arrays),
+        out_specs=[any_spec] * len(arrays),
+        scratch_shapes=[pltpu.VMEM((COPY_BUFS, COPY_ROWS, arrays[0].shape[1]), jnp.float32), dma((COPY_BUFS,)), dma((COPY_BUFS,))],
+        compiler_params=pltpu.CompilerParams(vmem_limit_bytes=VMEM_BYTES),
+    )(*arrays)
+
+
 def solution(mesh):
     row_part = P(DATA_AXIS, None)
     replicated = P()
 
     def local_step(feat_a, feat_b, w_in, w_mid, w_out, t_in, t_mid, t_out, gain_1, bias_1, gain_2, bias_2, off_weight):
         affine = [v.reshape(1, -1) for v in (gain_1, bias_1, gain_2, bias_2)]
-        pre_1, pre_2, act_1, act_2, grad_z, grad_emb, vec = front(
+        pre_1, pre_2, xs_2, xs_1, xs_0, grad_z, grad_emb, vec = front(
             feat_a, feat_b, (w_in, t_in, w_mid, t_mid, w_out, t_out), affine, off_weight.reshape(1)
         )
-        grad_w_out, grad_w_mid, grad_w_in, sums = backward(grad_z, act_2, act_1, feat_a, w_out, w_mid, pre_2, pre_1, vec)
+        grad_w_out, grad_w_mid, grad_w_in, sums = backward(grad_z, xs_2, xs_1, xs_0, w_out, w_mid, pre_2, pre_1, vec)
+        grad_emb, grad_w_out, grad_w_mid, grad_w_in = copy_out(grad_emb, grad_w_out, grad_w_mid, grad_w_in)
         return (sums[4, 0], grad_emb, grad_w_in, grad_w_mid, grad_w_out, sums[2], sums[3], sums[0], sums[1])
 
     return jax.shard_map(local_step, mesh=mesh, in_specs=(row_part, row_part) + (replicated,) * 11, out_specs=(replicated, row_part) + (replicated,) * 7, check_vma=False)

time: 607 us -> 589 us (0.970)
  local copies, waits for them, and re-layouts: 41.2 us -> 2.82 us
  Pallas kernels: 564 us -> 585 us
    unnamed x14 -> x0, local copies, waits for them, and re-layouts: 38.4 us -> none
    pallas_call x0 -> x1, Pallas kernels: none -> 36 us  [copy_out(): pl.pallas_call(copy_kernel, name='copy_out', out_shape=[jax.ShapeDtypeStr...]
    pallas_call x1, Pallas kernels: 378 us -> 359 us  [backward(): pl.pallas_call(back_kernel, name='backward', out_shape=[mat, mat, mat, ja...]
where the time goes in v7:
time: 589 us
  Pallas kernels  585 us (99%)
    pallas_call x1, Pallas kernels, backward(): pl.pallas_call(back_kernel, name='backward', out_shape=[mat, mat, mat, ja...  359 us
    pallas_call x1, Pallas kernels, front(): pl.pallas_call(front_kernel, name='front', out_shape=[wide_f32, wide_f32,...  190 us
    pallas_call x1, Pallas kernels, copy_out(): pl.pallas_call(copy_kernel, name='copy_out', out_shape=[jax.ShapeDtypeStr...  36 us

profile of v7, /device:TPU:0, one launch (start us, length us, event | category | flops | bytes accessed | tf_op | source)
XLA Modules:
  0.0 588.8 jit_solution(7169360424184750729)
XLA Ops:
  1.3 190.1 %front.1 = (f32[512,2048]{1,0:T(8,128)}, f32[512,2048]{1,0:T(8,128)}, bf16[1024,1024]{1,0:T(8,128)(2,1)}, bf16[1024,1024]{1,0:T(8,128)(2,1)}, bf16[1024,1024]{1,...) custom-call(bf16[512,2048]{1,0:T(8,128)(2,1)} %feat_a.1, ...), custom_call_target="tpu_custom_call" | custom-call | tf_op jit(solution)/shard_map/front/pallas_call | solution.py:621
  191.4 358.6 %backward.1 = (f32[2048,2048]{1,0:T(8,128)}, f32[2048,2048]{1,0:T(8,128)}, f32[2048,2048]{1,0:T(8,128)}, f32[5,2048]{1,0:T(8,128)}) custom-call(bf16[1024,2048]{1,0:T(8,128)(2,1)} %get-tuple-element.25.dz_hbm, bf16[1024,1024]{1,0:T(8,128)(2,1)} %get-tuple-element.26.x2, bf16[1024,1024]{1,0:T(8,128)(2,1)} %get-tuple-element.27.x1, ...), custom_call_target="tpu_custom_call" | custom-call | tf_op jit(solution)/shard_map/backward/pallas_call | solution.py:848
  550.0 36.0 %copy_out.1 = (f32[512,2048]{1,0:T(8,128)}, f32[2048,2048]{1,0:T(8,128)}, f32[2048,2048]{1,0:T(8,128)}, f32[2048,2048]{1,0:T(8,128)}) custom-call(f32[512,2048]{1,0:T(8,128)} %get-tuple-element.33.refs_0_, f32[2048,2048]{1,0:T(8,128)} %get-tuple-element.34.refs_1_, f32[2048,2048]{1,0:T(8,128)} %get-tuple-element.35.refs_2_, ...), custom_call_target="tpu_custom_call" | custom-call | tf_op jit(solution)/shard_map/copy_out/pallas_call | solution.py:902
  586.0 1.6 fusion
  587.7 1.2 slice.15

commit v8 on v7

--- a/solution.py
+++ b/solution.py
@@ -27,8 +27,18 @@
 LAYER_SLOTS = 15
 COPY_ROWS = 256
 COPY_BUFS = 12
-FRONT_PLAN = ((0, 0, 3, 5, 7, 10, 11, 13, 17, 19), (0, 1, 3, 4, 6, 5, 2, 9, 8, 7), (5, 2))
-BACK_PLAN = ((0, 0, 5, 7, 10, 12, 13, 16, 20, 23), (0, 1, 9, 5, 3, 2, 8, 7, 4, 6), (4, 2))
+FRONT_PLAN = ((0, 0, 3, 5, 7, 9, 12, 13, 16, 17, 18), (0, 6, 3, 4, 9, 10, 8, 5, 2, 7, 1))
+BACK_PLAN = ((0, 0, 3, 5, 7, 8, 9, 11, 14, 17, 19), (0, 4, 8, 7, 10, 1, 2, 3, 5, 6, 9))
+
+
+def front_kind(kind, k):
+    s, l = (k % 5 == 2) & (k > 2), k == 2
+    return {"s": s, "l": l, "x": (k % 5 != 2)}[kind]
+
+
+def back_kind(kind, k):
+    l = ((k % 5 == 2) & (k < 43)) | ((k % 5 == 0) & (k >= 10) & (k < 36))
+    return l if kind == "l" else jnp.logical_not(l)
 
 
 def contract_rows(left_op, right_op):
@@ -152,42 +162,33 @@
 
 
 class ChunkSum:
-    def __init__(self, place, z_first, acc, gathered, landing, send, recv, finish):
-        self.p, self.z_first_plan, self.slots, self.gather_slots = place, z_first, acc.shape[0], gathered.shape[0]
+    def __init__(self, place, kinds, is_kind, acc, gathered, landing, send, recv, finish):
+        self.p, self.kinds, self.is_kind, self.slots, self.gather_slots = place, kinds, is_kind, acc.shape[0], gathered.shape[0]
         self.acc, self.gathered, self.landing, self.send, self.recv, self.finish = acc, gathered, landing, send, recv, finish
         self.size = acc.shape[1]
-        core, bx, by = place.core, place.bx, place.by
-        self.xy = ((2 + 2 * core, core * by + (1 - core) * bx), (4 - 2 * core, core * bx + (1 - core) * by))
-        self.zz = ((8, place.bz0), (16, place.bz1))
+        self.s2, self.s4 = self.size // 2, self.size // 4
+        core, bx, by, me = place.core, place.bx, place.by, place.me
+        first, second = core * by + (1 - core) * bx, core * bx + (1 - core) * by
+        self.xy = ((me + (2 + 2 * core) * (1 - 2 * first), first), (me + (4 - 2 * core) * (1 - 2 * second), second))
+        self.zz = ((me + 8 * (1 - 2 * place.bz0), place.bz0), (me + 16 * (1 - 2 * place.bz1), place.bz1))
         self.is_mid = place.bz0 + place.bz1 - 2 * place.bz0 * place.bz1
-        self.z_mate = place.me + 8 * (1 - 2 * place.bz0)
-        self.mid_mate = place.me + 8 * (1 - 2 * place.bz1)
-
-    def z_first(self, k):
-        every, at = self.z_first_plan
-        off = k % every - at
-        return 1 - lax.min(off * off, 1)
-
-    def steps(self, k):
-        zf = self.z_first(k)
-        pairs = []
-        for a, b in zip(self.xy + self.zz, self.zz + self.xy):
-            stride = zf * b[0] + (1 - zf) * a[0]
-            bit = zf * b[1] + (1 - zf) * a[1]
-            pairs.append((self.p.me + stride * (1 - 2 * bit), bit))
-        s2, s4 = self.size // 2, self.size // 4
-        offs = (0, pairs[0][1] * s2, pairs[0][1] * s2 + pairs[1][1] * s4)
-        return zf, pairs, offs
+        self.mid, self.end = self.is_mid == 1, self.is_mid == 0
+        self.z_mate = self.zz[0][0]
+        self.mid_mate = me + 8 * (1 - 2 * place.bz1)
 
     def copy(self, src, dst, stage, k, mate):
         return remote_copy(src, dst, self.send.at[stage, k], self.recv.at[stage, k], mate)
 
-    def down(self, stage, k, off, size, mate):
+    def span(self, off, size):
+        return pl.ds(pl.multiple_of(off, self.s4), size)
+
+    def down(self, stage, k, off, size, mate, buf=None):
         j = k % self.slots
-        return self.copy(self.acc.at[j, rows(off, size)], self.landing[stage].at[j], stage, k, mate)
+        buf = self.landing[stage] if buf is None else buf
+        return self.copy(self.acc.at[j, self.span(off, size)], buf.at[j, pl.ds(0, size)], stage, k, mate)
 
     def up(self, stage, k, off, size, mate):
-        block = self.gathered.at[k % self.gather_slots, rows(off, size)]
+        block = self.gathered.at[k % self.gather_slots, self.span(off, size)]
         return self.copy(block, block, stage, k, mate)
 
     def add(self, k, off, size, buf):
@@ -195,74 +196,189 @@
         j = k % self.slots
 
         def body(i):
-            at = rows(off + i * step, step)
+            at = pl.ds(pl.multiple_of(off + i * step, step), step)
             self.acc[j, at] = self.acc[j, at] + buf[j, rows(i * step, step)]
 
         loop(0, size // step, body)
 
     def stage(self, i, k):
-        zf, pairs, offs = self.steps(k)
-        s2, s4 = self.size // 2, self.size // 4
-        l1, l2, l3, l4 = self.landing
-        z_first = zf == 1
-        mid = (zf == 0) & (self.is_mid == 1)
-        end = (zf == 0) & (self.is_mid == 0)
-
-        half_copy = lambda: self.down(0, k, offs[0] + (1 - pairs[0][1]) * s2, s2, pairs[0][0])
-        quarter_copy = lambda: self.down(1, k, offs[1] + (1 - pairs[1][1]) * s4, s4, pairs[1][0])
-        inward = lambda: self.down(2, k, offs[2], s4, zf * pairs[2][0] + (1 - zf) * self.z_mate)
-        across = lambda: self.down(3, k, offs[2], s4, zf * pairs[3][0] + (1 - zf) * self.mid_mate)
-        outward = lambda: self.up(4, k, offs[2], s4, self.z_mate)
-        back4 = lambda: self.up(5, k, offs[2], s4, pairs[1][0])
-        back2 = lambda: self.up(6, k, offs[1], s2, pairs[0][0])
-
+        for kind in self.kinds:
+            run = {"x": self.stage_x, "s": self.stage_s, "l": self.stage_l}[kind]
+            pl.when(self.is_kind(kind, k))(functools.partial(run, i, k))
+
+    def stage_x(self, i, k):
+        (m1, b1), (m2, b2), s2, s4 = *self.xy, self.s2, self.s4
+        off1, off2 = b1 * s2, b1 * s2 + b2 * s4
+        half = lambda: self.down(0, k, (1 - b1) * s2, s2, m1)
+        quarter = lambda: self.down(1, k, off1 + (1 - b2) * s4, s4, m2)
+        inward = lambda: self.down(2, k, off2, s4, self.z_mate)
+        across = lambda: self.down(3, k, off2, s4, self.mid_mate)
+        outward = lambda: self.up(4, k, off2, s4, self.z_mate)
+        back4 = lambda: self.up(5, k, off2, s4, m2)
+        back2 = lambda: self.up(6, k, off1, s2, m1)
         if i == 1:
-            half_copy().start()
+            half().start()
         elif i == 2:
-            half_copy().wait_recv()
-            self.add(k, offs[1], s2, l1)
-            quarter_copy().start()
+            half().wait_recv()
+            self.add(k, off1, s2, self.landing[0])
+            quarter().start()
         elif i == 3:
-            quarter_copy().wait_recv()
-            self.add(k, offs[2], s4, l2)
-            pl.when(z_first | end)(lambda: inward().start())
+            quarter().wait_recv()
+            self.add(k, off2, s4, self.landing[1])
+            pl.when(self.end)(lambda: inward().start())
         elif i == 4:
 
-            @pl.when(z_first | mid)
+            @pl.when(self.mid)
             def _():
                 inward().wait_recv()
-                pl.when(z_first)(lambda: inward().wait_send())
-                self.add(k, offs[2], s4, l3)
+                self.add(k, off2, s4, self.landing[2])
                 across().start()
 
         elif i == 5:
 
-            @pl.when(z_first | mid)
+            @pl.when(self.mid)
             def _():
                 across().wait_recv()
-                self.finish(k, offs[2], s4, l4)
-                pl.when(mid)(lambda: outward().start())
+                self.finish(k, off2, s4, self.landing[3])
+                outward().start()
 
         elif i == 6:
-            pl.when(end)(lambda: outward().wait_recv())
+            pl.when(self.end)(lambda: outward().wait_recv())
             back4().start()
-            half_copy().wait_send()
-            quarter_copy().wait_send()
-            pl.when(end)(lambda: inward().wait_send())
-            pl.when(z_first | mid)(lambda: across().wait_send())
+            half().wait_send()
+            quarter().wait_send()
+            pl.when(self.end)(lambda: inward().wait_send())
+            pl.when(self.mid)(lambda: across().wait_send())
         elif i == 7:
             back4().wait_recv()
             back2().start()
         elif i == 8:
             back2().wait_recv()
-        else:
-            pl.when(mid)(lambda: outward().wait_send())
+        elif i == 10:
+            pl.when(self.mid)(lambda: outward().wait_send())
             back4().wait_send()
             back2().wait_send()
 
+    def stage_s(self, i, k):
+        (m1, b1), (m2, b2), s2, s4 = *self.zz, self.s2, self.s4
+        off1, off2 = b1 * s2, b1 * s2 + b2 * s4
+        half = lambda: self.down(0, k, (1 - b1) * s2, s2, m1)
+        quarter = lambda: self.down(1, k, off1 + (1 - b2) * s4, s4, m2)
+        whole_1 = lambda: self.down(2, k, off2, s4, self.xy[0][0])
+        whole_2 = lambda: self.down(3, k, off2, s4, self.xy[1][0])
+        back4 = lambda: self.up(5, k, off2, s4, m2)
+        back2 = lambda: self.up(6, k, off1, s2, m1)
+        if i == 1:
+            half().start()
+        elif i == 2:
+            half().wait_recv()
+            self.add(k, off1, s2, self.landing[0])
+            quarter().start()
+        elif i == 3:
+            quarter().wait_recv()
+            self.add(k, off2, s4, self.landing[1])
+            whole_1().start()
+        elif i == 4:
+            whole_1().wait_recv()
+            whole_1().wait_send()
+            self.add(k, off2, s4, self.landing[2])
+            whole_2().start()
+        elif i == 5:
+            whole_2().wait_recv()
+            self.finish(k, off2, s4, self.landing[3])
+        elif i == 6:
+            back4().start()
+            half().wait_send()
+            quarter().wait_send()
+            whole_2().wait_send()
+        elif i == 7:
+            back4().wait_recv()
+            back2().start()
+        elif i == 8:
+            back2().wait_recv()
+        elif i == 10:
+            back4().wait_send()
+            back2().wait_send()
+
+    def stage_l(self, i, k):
+        s2, s4 = self.s2, self.s4
+        s3 = s2 + s4
+        b0, b1 = self.p.bz0, self.p.bz1
+        own, side, tip, rest = (2 * b1 + b0) * s4, b1 * s2, 3 * b1 * s4, (1 - b1) * s4
+        inward = lambda: self.down(0, k, rest, s3, self.z_mate)
+        across = lambda: self.down(1, k, (1 - b1) * s2, s2, self.mid_mate)
+        outward = lambda: self.down(2, k, tip, s4, self.z_mate)
+        whole_1 = lambda: self.down(3, k, own, s4, self.xy[0][0])
+        whole_2 = lambda: self.down(8, k, own, s4, self.xy[1][0], self.landing[4])
+        tip_back = lambda: self.up(4, k, tip, s4, self.z_mate)
+        side_back = lambda: self.up(5, k, side, s2, self.mid_mate)
+        rest_back = lambda: self.up(6, k, rest, s3, self.z_mate)
+        if i == 1:
+            pl.when(self.end)(lambda: inward().start())
+        elif i == 2:
+
+            @pl.when(self.mid)
+            def _():
+                inward().wait_recv()
+                self.add(k, rest, s3, self.landing[0])
+                across().start()
+
+        elif i == 3:
+
+            @pl.when(self.mid)
+            def _():
+                across().wait_recv()
+                self.add(k, side, s2, self.landing[1])
+                outward().start()
+
+        elif i == 4:
+
+            @pl.when(self.end)
+            def _():
+                outward().wait_recv()
+                self.add(k, own, s4, self.landing[2])
+
+            whole_1().start()
+        elif i == 5:
+            whole_1().wait_recv()
+            whole_1().wait_send()
+            pl.when(self.mid)(lambda: outward().wait_send())
+            self.add(k, own, s4, self.landing[3])
+            whole_2().start()
+        elif i == 6:
+            whole_2().wait_recv()
+            self.finish(k, own, s4, self.landing[4])
+            pl.when(self.end)(lambda: tip_back().start())
+            whole_2().wait_send()
+            pl.when(self.end)(lambda: inward().wait_send())
+            pl.when(self.mid)(lambda: across().wait_send())
+        elif i == 7:
+
+            @pl.when(self.mid)
+            def _():
+                tip_back().wait_recv()
+                side_back().start()
+
+        elif i == 8:
+
+            @pl.when(self.mid)
+            def _():
+                side_back().wait_recv()
+                rest_back().start()
+
+        elif i == 9:
+            pl.when(self.end)(lambda: rest_back().wait_recv())
+        elif i == 10:
+            pl.when(self.end)(lambda: tip_back().wait_send())
+
+            @pl.when(self.mid)
+            def _():
+                side_back().wait_send()
+                rest_back().wait_send()
+
 
 def run_slots(plan, count, stage, between):
-    lags, order, _ = plan
+    lags, order = plan
 
     def slot(t):
         for i in order:
@@ -285,13 +401,8 @@
     gathered = pltpu.VMEM((gather_slots, part_rows, width), dtype)
 
     dma = pltpu.SemaphoreType.DMA
-    return [buf(part_rows), gathered, buf(part_rows // 2), buf(part_rows // 4), buf(part_rows // 4), buf(part_rows // 4)] + [
-        dma((8, count)),
-        dma((8, count)),
-    ]
-
-
-CHUNK_REFS = 8
+    quarter = part_rows // 4
+    return [buf(part_rows), gathered, *(buf(n * quarter) for n in (3, 2, 1, 1, 1)), dma((9, count)), dma((9, count))]
 
 
 def fold(value):
@@ -302,7 +413,7 @@
     (x_buf, u_buf, w_buf, stats, affine, loss, ea, eb, g_peer) = scratch[:9]
     (x_sem, w_sem, pre_sem, keep_sem, keep_send, keep_recv, ge_sem, e_send, e_recv) = scratch[9:18]
     small_refs = scratch[18 : 18 + SMALL_REFS]
-    acc, gathered, l1, l2, l3, l4, send, recv = scratch[18 + SMALL_REFS :]
+    acc, gathered, *landing, send, recv = scratch[18 + SMALL_REFS :]
     rows_dev, width = feat_a.shape
     wide = w_buf.shape[2]
     tiles = width // wide
@@ -497,7 +608,7 @@
     loss[...] = jnp.zeros_like(loss)
 
     def finish(k, off, size, buf):
-        share = 0.5 - 0.25 * chunks.z_first(k).astype(jnp.float32)
+        share = jnp.where(front_kind("x", k), 0.5, 0.25)
         at = rows(off, size)
         corr = (acc[k, at] + buf[k]) / row_count
         row = core * half + k * part_rows + off
@@ -507,7 +618,7 @@
         loss[...] += share * jnp.sum(jnp.where(diag, miss * miss, weight * (corr * corr)), axis=0, keepdims=True)
         gathered[k, at] = jnp.where(diag, -2.0 * miss, 2.0 * weight * corr).astype(jnp.bfloat16)
 
-    chunks = ChunkSum(place, FRONT_PLAN[2], acc, gathered, (l1, l2, l3, l4), send, recv, finish)
+    chunks = ChunkSum(place, "xsl", front_kind, acc, gathered, landing, send, recv, finish)
 
     def form(k):
         @pl.when(k == 0)
@@ -554,13 +665,15 @@
             return
         chunks.stage(i, k)
         if i == 8:
-            swap(k).start()
+            pl.when(jnp.logical_not(front_kind("l", k)))(lambda: swap(k).start())
+        if i == 9:
+            pl.when(front_kind("l", k))(lambda: swap(k).start())
 
             @pl.when(k % GROUP == GROUP - 1)
             def _():
                 embed(k - GROUP + 1, core, gathered[pl.ds(k - GROUP + 1, GROUP)])
 
-        if i == 9:
+        if i == 10:
             swap(k).wait_recv()
             swap(k).wait_send()
 
@@ -655,7 +768,7 @@
     (dy, xs, w_buf, u_buf, dpre) = scratch[:5]
     (in_sem, tile_sem, peer_send, peer_recv, store_sem) = scratch[5:10]
     small_refs = scratch[10 : 10 + SMALL_REFS]
-    acc, gathered, l1, l2, l3, l4, send, recv = scratch[10 + SMALL_REFS :]
+    acc, gathered, *landing, send, recv = scratch[10 + SMALL_REFS :]
     rows_dev, width = dpre.shape
     wide = w_buf.shape[1]
     tiles = width // wide
@@ -749,7 +862,7 @@
         j = k % ACC_SLOTS
         gathered[k % GATHER_SLOTS, rows(off, size)] = acc[j, rows(off, size)] + buf[j]
 
-    chunks = ChunkSum(place, BACK_PLAN[2], acc, gathered, (l1, l2, l3, l4), send, recv, finish)
+    chunks = ChunkSum(place, "xl", back_kind, acc, gathered, landing, send, recv, finish)
 
     def form(k):
         w, j = k // PARTS, k % ACC_SLOTS
@@ -782,14 +895,15 @@
             pl.when((k % GROUP == 0) & (k > 0))(lambda: form(k))
             return
         chunks.stage(i, k)
+        def emit(out):
+            last_copy(out, k, core).start()
+            store_copy(out, k).start()
+
         if i == 8:
-
-            def emit(out):
-                last_copy(out, k, core).start()
-                store_copy(out, k).start()
-
-            pick(k // PARTS, outs, emit)
+            pl.when(back_kind("x", k))(lambda: pick(k // PARTS, outs, emit))
         if i == 9:
+            pl.when(back_kind("l", k))(lambda: pick(k // PARTS, outs, emit))
+        if i == 10:
 
             def close(out):
                 last_copy(out, k, 1 - core).wait_recv()

time: 589 us -> 576 us (0.978)
  Pallas kernels: 585 us -> 572 us
    pallas_call x1, Pallas kernels: 359 us -> 345 us  [backward(): pl.pallas_call(back_kernel, name='backward', out_shape=[mat, mat, mat, ja...]
where the time goes in v8:
time: 576 us
  Pallas kernels  572 us (99%)
    pallas_call x1, Pallas kernels, backward(): pl.pallas_call(back_kernel, name='backward', out_shape=[mat, mat, mat, ja...  345 us
    pallas_call x1, Pallas kernels, front(): pl.pallas_call(front_kernel, name='front', out_shape=[wide_f32, wide_f32,...  191 us
    pallas_call x1, Pallas kernels, copy_out(): pl.pallas_call(copy_kernel, name='copy_out', out_shape=[jax.ShapeDtypeStr...  36 us

profile of v8, /device:TPU:0, one launch (start us, length us, event | category | flops | bytes accessed | tf_op | source)
XLA Modules:
  0.0 576.1 jit_solution(12684296160054690463)
XLA Ops:
  1.3 191.0 %front.1 = (f32[512,2048]{1,0:T(8,128)}, f32[512,2048]{1,0:T(8,128)}, bf16[1024,1024]{1,0:T(8,128)(2,1)}, bf16[1024,1024]{1,0:T(8,128)(2,1)}, bf16[1024,1024]{1,...) custom-call(bf16[512,2048]{1,0:T(8,128)(2,1)} %feat_a.1, ...), custom_call_target="tpu_custom_call" | custom-call | tf_op jit(solution)/shard_map/front/pallas_call | solution.py:734
  192.3 344.9 %backward.1 = (f32[2048,2048]{1,0:T(8,128)}, f32[2048,2048]{1,0:T(8,128)}, f32[2048,2048]{1,0:T(8,128)}, f32[5,2048]{1,0:T(8,128)}) custom-call(bf16[1024,2048]{1,0:T(8,128)(2,1)} %get-tuple-element.25.dz_hbm, bf16[1024,1024]{1,0:T(8,128)(2,1)} %get-tuple-element.26.x2, bf16[1024,1024]{1,0:T(8,128)(2,1)} %get-tuple-element.27.x1, ...), custom_call_target="tpu_custom_call" | custom-call | tf_op jit(solution)/shard_map/backward/pallas_call | solution.py:962
  537.3 36.0 %copy_out.1 = (f32[512,2048]{1,0:T(8,128)}, f32[2048,2048]{1,0:T(8,128)}, f32[2048,2048]{1,0:T(8,128)}, f32[2048,2048]{1,0:T(8,128)}) custom-call(f32[512,2048]{1,0:T(8,128)} %get-tuple-element.33.refs_0_, f32[2048,2048]{1,0:T(8,128)} %get-tuple-element.34.refs_1_, f32[2048,2048]{1,0:T(8,128)} %get-tuple-element.35.refs_2_, ...), custom_call_target="tpu_custom_call" | custom-call | tf_op jit(solution)/shard_map/copy_out/pallas_call | solution.py:1016
  573.3 1.6 fusion
  574.9 1.2 slice.15

commit v9 on v8

--- a/solution.py
+++ b/solution.py
@@ -26,7 +26,7 @@
 W_BUFS = 3
 LAYER_SLOTS = 15
 COPY_ROWS = 256
-COPY_BUFS = 12
+COPY_BUFS = 20
 FRONT_PLAN = ((0, 0, 3, 5, 7, 9, 12, 13, 16, 17, 18), (0, 6, 3, 4, 9, 10, 8, 5, 2, 7, 1))
 BACK_PLAN = ((0, 0, 3, 5, 7, 8, 9, 11, 14, 17, 19), (0, 4, 8, 7, 10, 1, 2, 3, 5, 6, 9))
 
@@ -377,6 +377,11 @@
                 rest_back().wait_send()
 
 
+def form_next(k, form):
+    pl.when(k == 1)(lambda: form(GROUP // 2, GROUP // 2))
+    pl.when((k % GROUP == 0) & (k > 0))(lambda: form(k, GROUP))
+
+
 def run_slots(plan, count, stage, between):
     lags, order = plan
 
@@ -555,6 +560,7 @@
                 return c
 
             lax.fori_loop(0, rows_dev // BLOCK, block, 0)
+            eb_copy(i).start()
 
         @pl.when(layer < 2)
         def _():
@@ -574,10 +580,12 @@
         @pl.when((layer == 2) & (view == 1))
         def _():
             loop(0, tiles, teacher)
-            eb_copy().start()
 
     ea_copy = lambda: remote_copy(x_buf.at[0, :, rows((1 - core) * half, half)], ea.at[mine], e_send.at[0], e_recv.at[0], place.other_core)
-    eb_copy = lambda: remote_copy(eb.at[mine], eb.at[mine], e_send.at[1], e_recv.at[1], place.other_core)
+
+    def eb_copy(i):
+        block = eb.at[mine, rows(i * wide, wide)]
+        return remote_copy(block, block, e_send.at[1 + i], e_recv.at[1 + i], place.other_core)
 
     def step(g):
         job, i = g // tiles, g % tiles
@@ -620,18 +628,18 @@
 
     chunks = ChunkSum(place, "xsl", front_kind, acc, gathered, landing, send, recv, finish)
 
-    def form(k):
-        @pl.when(k == 0)
-        def _():
-            ea_copy().wait_recv()
-            eb_copy().wait_recv()
-
-        at = rows(k * part_rows, GROUP * part_rows)
+    def form(k, group):
+        at = rows(k * part_rows, group * part_rows)
         size = min(1024, width)
 
         def col(c):
+            @pl.when(k == 0)
+            def _():
+                for i in range(size // wide):
+                    eb_copy(c * (size // wide) + i).wait_recv()
+
             cs = rows(c * size, size)
-            acc[pl.ds(k, GROUP), :, cs] = contract_rows(ea[:, at], eb[:, cs]).reshape(GROUP, part_rows, size)
+            acc[pl.ds(k, group), :, cs] = contract_rows(ea[:, at], eb[:, cs]).reshape(group, part_rows, size)
 
         loop(0, width // size, col)
 
@@ -661,7 +669,7 @@
 
     def stage(i, k):
         if i == 0:
-            pl.when(k % GROUP == 0)(lambda: form(k))
+            form_next(k, form)
             return
         chunks.stage(i, k)
         if i == 8:
@@ -681,12 +689,15 @@
             def _():
                 embed(k - GROUP + 1, 1 - core, g_peer[pl.ds(k - GROUP + 1, GROUP)])
 
+    ea_copy().wait_recv()
+    form(0, GROUP // 2)
     run_slots(FRONT_PLAN, PARTS, stage, lambda t: None)
     for c in range(PLANE):
         payload[JOBS, c, 2:3] = loss[:, c * TILE : (c + 1) * TILE]
     small.begin(JOBS)
     ea_copy().wait_send()
-    eb_copy().wait_send()
+    for i in range(tiles):
+        eb_copy(i).wait_send()
     small.middle(JOBS)
     for k in range(0, PARTS, GROUP):
         for side in range(2):
@@ -755,8 +766,8 @@
             dma((keeps,)),
             dma((keeps,)),
             dma((PARTS // GROUP, 2)),
-            dma((2,)),
-            dma((2,)),
+            dma((1 + width // WIDE,)),
+            dma((1 + width // WIDE,)),
         ]
         + small_scratch(JOBS + 1)
         + chunk_scratch(PARTS, PARTS, part_rows, width, PARTS, jnp.bfloat16),
@@ -803,9 +814,14 @@
     def start_u(layer, i):
         pick(layer, pres, lambda ref: u_tile(ref, i).start())
 
-    dz_load = pltpu.make_async_copy(dz_hbm, dy.at[0], in_sem.at[MATS])
-    dz_load.start()
+    size = min(1024, width)
+
+    def load_dz(c):
+        return pltpu.make_async_copy(dz_hbm.at[:, rows(c * size, size)], dy.at[0, :, rows(c * size, size)], in_sem.at[MATS + c])
+
     load_x(0).start()
+    for c in range(width // size):
+        load_dz(c).start()
     w_tile(weights[0], 0).start()
     u_tile(pres[0], 0).start()
     load_x(1).start()
@@ -864,7 +880,7 @@
 
     chunks = ChunkSum(place, "xl", back_kind, acc, gathered, landing, send, recv, finish)
 
-    def form(k):
+    def form(k, group):
         w, j = k // PARTS, k % ACC_SLOTS
 
         @pl.when(k % PARTS == 0)
@@ -872,12 +888,12 @@
             pltpu.make_async_copy(xs.at[w % 2], xs.at[w % 2], in_sem.at[w]).wait()
             pl.when(w > 0)(lambda: peer_dy(w).wait_recv())
 
-        at = rows((k % PARTS) * part_rows, GROUP * part_rows)
-        size = min(1024, width)
+        at = rows((k % PARTS) * part_rows, group * part_rows)
 
         def col(c):
+            pl.when(k == 0)(lambda: load_dz(c).wait())
             cs = rows(c * size, size)
-            acc[pl.ds(j, GROUP), :, cs] = contract_rows(xs[w % 2, :, at], dy[w % 2, :, cs]).reshape(GROUP, part_rows, size)
+            acc[pl.ds(j, group), :, cs] = contract_rows(xs[w % 2, :, at], dy[w % 2, :, cs]).reshape(group, part_rows, size)
 
         loop(0, width // size, col)
 
@@ -892,7 +908,7 @@
 
     def stage(i, k):
         if i == 0:
-            pl.when((k % GROUP == 0) & (k > 0))(lambda: form(k))
+            form_next(k, form)
             return
         chunks.stage(i, k)
         def emit(out):
@@ -939,8 +955,7 @@
 
             pl.when(layer == 1)(lambda: load_x(2).start())
 
-    dz_load.wait()
-    form(0)
+    form(0, GROUP // 2)
     place.all_here()
     run_slots(BACK_PLAN, count, stage, lambda t: pl.when(t < 2 * LAYER_SLOTS)(lambda: layer_work(t)))
     for w in (1, 2):
@@ -971,7 +986,7 @@
             pltpu.VMEM((2, WIDE, width), jnp.bfloat16),
             pltpu.VMEM((2, rows_dev, WIDE), jnp.float32),
             pltpu.VMEM((rows_dev, width), jnp.float32),
-            dma((MATS + 1,)),
+            dma((MATS + 2,)),
             dma((2, 2)),
             dma((MATS,)),
             dma((MATS,)),
@@ -984,8 +999,8 @@
 
 
 def copy_kernel(*refs):
-    pairs = len(refs[:-3]) // 2
-    ins, outs, (buf, in_sem, out_sem) = refs[:pairs], refs[pairs : 2 * pairs], refs[2 * pairs :]
+    pairs = (len(refs) - 3 - 6) // 2
+    ins, small, outs, small_outs, (buf, in_sem, out_sem) = refs[:pairs], refs[pairs], refs[pairs + 1 : 2 * pairs + 1], refs[2 * pairs + 1 : -3], refs[-3:]
     blocks = [(i, r) for i in range(pairs) for r in range(0, ins[i].shape[0], COPY_ROWS)]
 
     def read(b):
@@ -999,6 +1014,9 @@
     ahead = COPY_BUFS // 2
     for b in range(min(ahead, len(blocks))):
         read(b).start()
+    for row in range(4):
+        small_outs[row][...] = small[row : row + 1]
+    small_outs[4][...] = small[4:5, :1]
     for b in range(len(blocks)):
         if b + ahead < len(blocks):
             if b + ahead >= COPY_BUFS:
@@ -1010,18 +1028,21 @@
         write(b).wait()
 
 
-def copy_out(*arrays):
+def copy_out(arrays, small):
     any_spec = pl.BlockSpec(memory_space=pl.ANY)
+    vmem_spec = pl.BlockSpec(memory_space=pltpu.VMEM)
     dma = pltpu.SemaphoreType.DMA
+    width = small.shape[1]
+    row = jax.ShapeDtypeStruct((1, width), jnp.float32)
     return pl.pallas_call(
         copy_kernel,
         name="copy_out",
-        out_shape=[jax.ShapeDtypeStruct(a.shape, a.dtype) for a in arrays],
-        in_specs=[any_spec] * len(arrays),
-        out_specs=[any_spec] * len(arrays),
-        scratch_shapes=[pltpu.VMEM((COPY_BUFS, COPY_ROWS, arrays[0].shape[1]), jnp.float32), dma((COPY_BUFS,)), dma((COPY_BUFS,))],
+        out_shape=[jax.ShapeDtypeStruct(a.shape, a.dtype) for a in arrays] + [row] * 4 + [jax.ShapeDtypeStruct((1, 1), jnp.float32)],
+        in_specs=[any_spec] * len(arrays) + [vmem_spec],
+        out_specs=[any_spec] * len(arrays) + [vmem_spec] * 5,
+        scratch_shapes=[pltpu.VMEM((COPY_BUFS, COPY_ROWS, width), jnp.float32), dma((COPY_BUFS,)), dma((COPY_BUFS,))],
         compiler_params=pltpu.CompilerParams(vmem_limit_bytes=VMEM_BYTES),
-    )(*arrays)
+    )(*arrays, small)
 
 
 def solution(mesh):
@@ -1034,7 +1055,8 @@
             feat_a, feat_b, (w_in, t_in, w_mid, t_mid, w_out, t_out), affine, off_weight.reshape(1)
         )
         grad_w_out, grad_w_mid, grad_w_in, sums = backward(grad_z, xs_2, xs_1, xs_0, w_out, w_mid, pre_2, pre_1, vec)
-        grad_emb, grad_w_out, grad_w_mid, grad_w_in = copy_out(grad_emb, grad_w_out, grad_w_mid, grad_w_in)
-        return (sums[4, 0], grad_emb, grad_w_in, grad_w_mid, grad_w_out, sums[2], sums[3], sums[0], sums[1])
+        (grad_emb, grad_w_out, grad_w_mid, grad_w_in, gain_2, bias_2, gain_1, bias_1, loss) = copy_out((grad_emb, grad_w_out, grad_w_mid, grad_w_in), sums)
+        gain_1, bias_1, gain_2, bias_2 = (v.reshape(-1) for v in (gain_1, bias_1, gain_2, bias_2))
+        return (loss.reshape(()), grad_emb, grad_w_in, grad_w_mid, grad_w_out, gain_1, bias_1, gain_2, bias_2)
 
     return jax.shard_map(local_step, mesh=mesh, in_specs=(row_part, row_part) + (replicated,) * 11, out_specs=(replicated, row_part) + (replicated,) * 7, check_vma=False)

time: 576 us -> 573 us (level)
  no operation moved by 1% of the time
where the time goes in v9:
time: 573 us
  Pallas kernels  571 us (100%)
    pallas_call x1, Pallas kernels, backward(): pl.pallas_call(back_kernel, name='backward', out_shape=[mat, mat, mat, ja...  344 us
    pallas_call x1, Pallas kernels, front(): pl.pallas_call(front_kernel, name='front', out_shape=[wide_f32, wide_f32,...  190 us
    pallas_call x1, Pallas kernels, copy_out(): pl.pallas_call(copy_kernel, name='copy_out', out_shape=[jax.ShapeDtypeStr...  37.7 us

profile of v9, /device:TPU:0, one launch (start us, length us, event | category | flops | bytes accessed | tf_op | source)
XLA Modules:
  0.0 572.6 jit_solution(2796121058873969461)
XLA Ops:
  1.3 189.9 %front.1 = (f32[512,2048]{1,0:T(8,128)}, f32[512,2048]{1,0:T(8,128)}, bf16[1024,1024]{1,0:T(8,128)(2,1)}, bf16[1024,1024]{1,0:T(8,128)(2,1)}, bf16[1024,1024]{1,...) custom-call(bf16[512,2048]{1,0:T(8,128)(2,1)} %feat_a.1, ...), custom_call_target="tpu_custom_call" | custom-call | tf_op jit(solution)/shard_map/front/pallas_call | solution.py:745
  191.2 343.8 %backward.1 = (f32[2048,2048]{1,0:T(8,128)}, f32[2048,2048]{1,0:T(8,128)}, f32[2048,2048]{1,0:T(8,128)}, f32[5,2048]{1,0:T(8,128)}) custom-call(bf16[1024,2048]{1,0:T(8,128)(2,1)} %get-tuple-element.31.dz_hbm, bf16[1024,1024]{1,0:T(8,128)(2,1)} %get-tuple-element.32.x2, bf16[1024,1024]{1,0:T(8,128)(2,1)} %get-tuple-element.33.x1, ...), custom_call_target="tpu_custom_call" | custom-call | tf_op jit(solution)/shard_map/backward/pallas_call | solution.py:977
  534.9 37.7 %copy_out.1 = (f32[512,2048]{1,0:T(8,128)}, f32[2048,2048]{1,0:T(8,128)}, f32[2048,2048]{1,0:T(8,128)}, f32[2048,2048]{1,0:T(8,128)}, f32[1,2048]{1,0:T(1,128)},...) custom-call(f32[512,2048]{1,0:T(8,128)} %get-tuple-element.30.refs_0_, ...), custom_call_target="tpu_custom_call" | custom-call | tf_op jit(solution)/shard_map/copy_out/pallas_call | solution.py:1037

commit v10 on v9

--- a/solution.py
+++ b/solution.py
@@ -16,7 +16,7 @@
 TILE = 256
 WIDE = 512
 BLOCK = 128
-SUM_ROWS = 4
+SUM_ROWS = 2
 PARTS = 16
 GROUP = 4
 MATS = 3
@@ -93,72 +93,59 @@
 
 
 class SmallSum:
-    def __init__(self, place, payload, total, plane_buf, depth_buf, own_buf, sems):
+    def __init__(self, place, payload, total, depth_buf, line_sum, plane_buf, sems):
         self.p, self.payload, self.total = place, payload, total
-        self.plane_buf, self.depth_buf, self.own_buf, self.sems = plane_buf, depth_buf, own_buf, sems
-
-    def first(self, j, m, slot):
+        self.depth_buf, self.line_sum, self.plane_buf, self.sems = depth_buf, line_sum, plane_buf, sems
+
+    def along(self, j, lv, slot):
         s, r = self.sems[0], self.sems[1]
-        return remote_copy(self.payload.at[j, m], self.plane_buf.at[j, slot], s.at[j, m], r.at[j, slot], self.p.plane * PLANE + m)
-
-    def second(self, j, lv, slot):
+        return remote_copy(self.payload.at[j], self.depth_buf.at[j, slot], s.at[j, lv], r.at[j, slot], lv * PLANE + self.p.pos)
+
+    def within(self, j, m, slot):
         s, r = self.sems[2], self.sems[3]
-        return remote_copy(self.own_buf.at[j, 0], self.depth_buf.at[j, slot], s.at[j, lv], r.at[j, slot], lv * PLANE + self.p.pos)
-
-    def third(self, j, m, slot):
-        s, r = self.sems[4], self.sems[5]
-        return remote_copy(self.own_buf.at[j, 1], self.total.at[j, slot], s.at[j, m], r.at[j, slot], self.p.plane * PLANE + m)
+        return remote_copy(self.line_sum.at[j], self.plane_buf.at[j, slot], s.at[j, m], r.at[j, slot], self.p.plane * PLANE + m)
 
     def begin(self, j):
+        for lv in self.p.levels:
+            self.along(j, lv, self.p.plane).start()
+        self.depth_buf[j, self.p.plane] = self.payload[j]
+
+    def middle(self, j):
+        for lv in self.p.levels:
+            self.along(j, lv, lv).wait_recv()
+        total = self.depth_buf[j, 0]
+        for i in range(1, DEPTH):
+            total = total + self.depth_buf[j, i]
+        self.line_sum[j] = total
         for m in self.p.mates:
-            self.first(j, m, self.p.pos).start()
-        self.plane_buf[j, self.p.pos] = self.payload[j, self.p.pos]
-
-    def middle(self, j):
+            self.within(j, m, self.p.pos).start()
+        self.plane_buf[j, self.p.pos] = total
+
+    def end(self, j):
         for m in self.p.mates:
-            self.first(j, m, m).wait_recv()
+            self.within(j, m, m).wait_recv()
         total = self.plane_buf[j, 0]
         for i in range(1, PLANE):
             total = total + self.plane_buf[j, i]
-        self.own_buf[j, 0] = total
-        self.depth_buf[j, self.p.plane] = total
+        self.total[j] = total
         for lv in self.p.levels:
-            self.second(j, lv, self.p.plane).start()
-
-    def last(self, j):
-        for lv in self.p.levels:
-            self.second(j, lv, lv).wait_recv()
-        total = self.depth_buf[j, 0]
-        for i in range(1, DEPTH):
-            total = total + self.depth_buf[j, i]
-        self.own_buf[j, 1] = total
-        self.total[j, self.p.pos] = total
+            self.along(j, lv, self.p.plane).wait_send()
         for m in self.p.mates:
-            self.third(j, m, self.p.pos).start()
-
-    def end(self, j):
-        for m in self.p.mates:
-            self.third(j, m, m).wait_recv()
-            self.first(j, m, self.p.pos).wait_send()
-            self.third(j, m, self.p.pos).wait_send()
-        for lv in self.p.levels:
-            self.second(j, lv, self.p.plane).wait_send()
+            self.within(j, m, self.p.pos).wait_send()
 
 
 def small_scratch(count):
     def buf(*lead):
-        return pltpu.VMEM((count, *lead, SUM_ROWS, TILE), jnp.float32)
-
-    bufs = [buf(PLANE), buf(PLANE), buf(PLANE), buf(DEPTH), buf(2)]
-    return bufs + [pltpu.SemaphoreType.DMA((count, n)) for n in (PLANE, PLANE, DEPTH, DEPTH, PLANE, PLANE)]
-
-
-SMALL_REFS = 11
+        return pltpu.VMEM((count, *lead, PLANE, SUM_ROWS, TILE), jnp.float32)
+
+    return [buf(), buf(), buf(DEPTH), buf(), buf(PLANE)] + [pltpu.SemaphoreType.DMA((count, n)) for n in (DEPTH, DEPTH, PLANE, PLANE)]
+
+
+SMALL_REFS = 9
 
 
 def small_sum(place, refs):
-    payload, total, plane_buf, depth_buf, own_buf = refs[:5]
-    return SmallSum(place, payload, total, plane_buf, depth_buf, own_buf, refs[5:])
+    return SmallSum(place, *refs[:5], refs[5:])
 
 
 class ChunkSum:
@@ -598,8 +585,7 @@
             place.all_here()
             start_x(0)
 
-        pl.when((i == 0) & (job > 0))(lambda: small.middle(job - 1))
-        pl.when((i == tiles - 2) & (job > 0))(lambda: small.last(job - 1))
+        pl.when((i == 1) & (job > 0))(lambda: small.middle(job - 1))
 
         @pl.when(i == tiles - 1)
         def _():
@@ -608,7 +594,6 @@
 
     loop(0, JOBS * tiles, step)
     small.middle(JOBS - 1)
-    small.last(JOBS - 1)
     norm(JOBS - 1)
     for j, source in enumerate((affine.at[2], affine.at[3], stats.at[2, 0], stats.at[2, 1], affine.at[0], affine.at[1], stats.at[0, 0], stats.at[0, 1])):
         vec[j] = source[...]
@@ -692,17 +677,18 @@
     ea_copy().wait_recv()
     form(0, GROUP // 2)
     run_slots(FRONT_PLAN, PARTS, stage, lambda t: None)
+    small.begin(JOBS)
     for c in range(PLANE):
-        payload[JOBS, c, 2:3] = loss[:, c * TILE : (c + 1) * TILE]
-    small.begin(JOBS)
+        payload[JOBS + 1, c, 0:1] = loss[:, c * TILE : (c + 1) * TILE]
+    small.begin(JOBS + 1)
     ea_copy().wait_send()
     for i in range(tiles):
         eb_copy(i).wait_send()
     small.middle(JOBS)
+    small.middle(JOBS + 1)
     for k in range(0, PARTS, GROUP):
         for side in range(2):
             ge_copy(k, side).wait()
-    small.last(JOBS)
     small.end(JOBS)
 
     def dz_tile(i):
@@ -721,8 +707,9 @@
             c.start()
 
     loop(0, tiles, dz_tile)
+    small.end(JOBS + 1)
     for c in range(PLANE):
-        vec[8, :, c * TILE : (c + 1) * TILE] = total[JOBS, c, 2:3]
+        vec[8, :, c * TILE : (c + 1) * TILE] = total[JOBS + 1, c, 0:1]
     for w in range(3):
         keep_x(w)[1].wait_recv()
     for i in range(tiles):
@@ -769,7 +756,7 @@
             dma((1 + width // WIDE,)),
             dma((1 + width // WIDE,)),
         ]
-        + small_scratch(JOBS + 1)
+        + small_scratch(JOBS + 2)
         + chunk_scratch(PARTS, PARTS, part_rows, width, PARTS, jnp.bfloat16),
         compiler_params=pltpu.CompilerParams(collective_id=0, has_side_effects=True, vmem_limit_bytes=VMEM_BYTES),
     )(feat_a, feat_b, *weights, *affine, off_weight)
@@ -936,10 +923,7 @@
         pl.when(at == 2 * tiles)(lambda: small.begin(layer))
         pl.when(at == 2 * tiles + 1)(lambda: small.middle(layer))
 
-        @pl.when(at == 2 * tiles + 2)
-        def _():
-            small.last(layer)
-            start_u(layer, 0)
+        pl.when(at == 2 * tiles + 2)(lambda: start_u(layer, 0))
 
         pl.when(at == first_du)(lambda: small.end(layer))
         pl.when(at >= first_du)(lambda: du_tile(layer, at - first_du))

time: 573 us -> 559 us (0.976)
  Pallas kernels: 571 us -> 558 us
    pallas_call x1, Pallas kernels: 190 us -> 176 us  [front(): pl.pallas_call(front_kernel, name='front', out_shape=[wide_f32, wide_f32,...]
where the time goes in v10:
time: 559 us
  Pallas kernels  558 us (100%)
    pallas_call x1, Pallas kernels, backward(): pl.pallas_call(back_kernel, name='backward', out_shape=[mat, mat, mat, ja...  344 us
    pallas_call x1, Pallas kernels, front(): pl.pallas_call(front_kernel, name='front', out_shape=[wide_f32, wide_f32,...  176 us
    pallas_call x1, Pallas kernels, copy_out(): pl.pallas_call(copy_kernel, name='copy_out', out_shape=[jax.ShapeDtypeStr...  37.7 us

profile of v10, /device:TPU:0, one launch (start us, length us, event | category | flops | bytes accessed | tf_op | source)
XLA Modules:
  0.0 559.0 jit_solution(6700921850975847473)
XLA Ops:
  1.3 176.2 %front.1 = (f32[512,2048]{1,0:T(8,128)}, f32[512,2048]{1,0:T(8,128)}, bf16[1024,1024]{1,0:T(8,128)(2,1)}, bf16[1024,1024]{1,0:T(8,128)(2,1)}, bf16[1024,1024]{1,...) custom-call(bf16[512,2048]{1,0:T(8,128)(2,1)} %feat_a.1, ...), custom_call_target="tpu_custom_call" | custom-call | tf_op jit(solution)/shard_map/front/pallas_call | solution.py:732
  177.5 343.8 %backward.1 = (f32[2048,2048]{1,0:T(8,128)}, f32[2048,2048]{1,0:T(8,128)}, f32[2048,2048]{1,0:T(8,128)}, f32[5,2048]{1,0:T(8,128)}) custom-call(bf16[1024,2048]{1,0:T(8,128)(2,1)} %get-tuple-element.31.dz_hbm, bf16[1024,1024]{1,0:T(8,128)(2,1)} %get-tuple-element.32.x2, bf16[1024,1024]{1,0:T(8,128)(2,1)} %get-tuple-element.33.x1, ...), custom_call_target="tpu_custom_call" | custom-call | tf_op jit(solution)/shard_map/backward/pallas_call | solution.py:961
  521.4 37.7 %copy_out.1 = (f32[512,2048]{1,0:T(8,128)}, f32[2048,2048]{1,0:T(8,128)}, f32[2048,2048]{1,0:T(8,128)}, f32[2048,2048]{1,0:T(8,128)}, f32[1,2048]{1,0:T(1,128)},...) custom-call(f32[512,2048]{1,0:T(8,128)} %get-tuple-element.30.refs_0_, ...), custom_call_target="tpu_custom_call" | custom-call | tf_op jit(solution)/shard_map/copy_out/pallas_call | solution.py:1021

commit v11 on v10

--- a/solution.py
+++ b/solution.py
@@ -585,7 +585,7 @@
             place.all_here()
             start_x(0)
 
-        pl.when((i == 1) & (job > 0))(lambda: small.middle(job - 1))
+        pl.when((i == 0) & (job > 0))(lambda: small.middle(job - 1))
 
         @pl.when(i == tiles - 1)
         def _():
@@ -983,8 +983,9 @@
 
 
 def copy_kernel(*refs):
-    pairs = (len(refs) - 3 - 6) // 2
-    ins, small, outs, small_outs, (buf, in_sem, out_sem) = refs[:pairs], refs[pairs], refs[pairs + 1 : 2 * pairs + 1], refs[2 * pairs + 1 : -3], refs[-3:]
+    pairs = (len(refs) - 5 - 6) // 2
+    ins, small, outs, small_outs = refs[:pairs], refs[pairs], refs[pairs + 1 : 2 * pairs + 1], refs[2 * pairs + 1 : -5]
+    buf, small_buf, in_sem, out_sem, small_sem = refs[-5:]
     blocks = [(i, r) for i in range(pairs) for r in range(0, ins[i].shape[0], COPY_ROWS)]
 
     def read(b):
@@ -998,9 +999,11 @@
     ahead = COPY_BUFS // 2
     for b in range(min(ahead, len(blocks))):
         read(b).start()
-    for row in range(4):
-        small_outs[row][...] = small[row : row + 1]
-    small_outs[4][...] = small[4:5, :1]
+    pltpu.make_async_copy(small, small_buf, small_sem.at[4]).start()
+
+    def small_write(row):
+        return pltpu.make_async_copy(small_buf.at[pl.ds(row, 1)], small_outs[row], small_sem.at[row])
+
     for b in range(len(blocks)):
         if b + ahead < len(blocks):
             if b + ahead >= COPY_BUFS:
@@ -1008,6 +1011,13 @@
             read(b + ahead).start()
         read(b).wait()
         write(b).start()
+        if b == 0:
+            pltpu.make_async_copy(small, small_buf, small_sem.at[4]).wait()
+            small_outs[4][...] = small_buf[4:5, :1]
+            for row in range(4):
+                small_write(row).start()
+    for row in range(4):
+        small_write(row).wait()
     for b in range(max(0, len(blocks) - COPY_BUFS), len(blocks)):
         write(b).wait()
 
@@ -1022,9 +1032,15 @@
         copy_kernel,
         name="copy_out",
         out_shape=[jax.ShapeDtypeStruct(a.shape, a.dtype) for a in arrays] + [row] * 4 + [jax.ShapeDtypeStruct((1, 1), jnp.float32)],
-        in_specs=[any_spec] * len(arrays) + [vmem_spec],
-        out_specs=[any_spec] * len(arrays) + [vmem_spec] * 5,
-        scratch_shapes=[pltpu.VMEM((COPY_BUFS, COPY_ROWS, width), jnp.float32), dma((COPY_BUFS,)), dma((COPY_BUFS,))],
+        in_specs=[any_spec] * (len(arrays) + 1),
+        out_specs=[any_spec] * (len(arrays) + 4) + [vmem_spec],
+        scratch_shapes=[
+            pltpu.VMEM((COPY_BUFS, COPY_ROWS, width), jnp.float32),
+            pltpu.VMEM(small.shape, jnp.float32),
+            dma((COPY_BUFS,)),
+            dma((COPY_BUFS,)),
+            dma((5,)),
+        ],
         compiler_params=pltpu.CompilerParams(vmem_limit_bytes=VMEM_BYTES),
     )(*arrays, small)
 

time: 559 us -> 563 us (level)
  no operation moved by 1% of the time
where the time goes in v11:
time: 563 us
  Pallas kernels  562 us (100%)
    pallas_call x1, Pallas kernels, backward(): pl.pallas_call(back_kernel, name='backward', out_shape=[mat, mat, mat, ja...  344 us
    pallas_call x1, Pallas kernels, front(): pl.pallas_call(front_kernel, name='front', out_shape=[wide_f32, wide_f32,...  181 us
    pallas_call x1, Pallas kernels, copy_out(): pl.pallas_call(copy_kernel, name='copy_out', out_shape=[jax.ShapeDtypeStr...  36.7 us

profile of v11, /device:TPU:0, one launch (start us, length us, event | category | flops | bytes accessed | tf_op | source)
XLA Modules:
  0.0 562.8 jit_solution(4825208094540247146)
XLA Ops:
  1.3 180.9 %front.1 = (f32[512,2048]{1,0:T(8,128)}, f32[512,2048]{1,0:T(8,128)}, bf16[1024,1024]{1,0:T(8,128)(2,1)}, bf16[1024,1024]{1,0:T(8,128)(2,1)}, bf16[1024,1024]{1,...) custom-call(bf16[512,2048]{1,0:T(8,128)(2,1)} %feat_a.1, ...), custom_call_target="tpu_custom_call" | custom-call | tf_op jit(solution)/shard_map/front/pallas_call | solution.py:732
  182.2 343.9 %backward.1 = (f32[2048,2048]{1,0:T(8,128)}, f32[2048,2048]{1,0:T(8,128)}, f32[2048,2048]{1,0:T(8,128)}, f32[5,2048]{1,0:T(8,128)}) custom-call(bf16[1024,2048]{1,0:T(8,128)(2,1)} %get-tuple-element.31.dz_hbm, bf16[1024,1024]{1,0:T(8,128)(2,1)} %get-tuple-element.32.x2, bf16[1024,1024]{1,0:T(8,128)(2,1)} %get-tuple-element.33.x1, ...), custom_call_target="tpu_custom_call" | custom-call | tf_op jit(solution)/shard_map/backward/pallas_call | solution.py:961
  526.1 36.7 %copy_out.1 = (f32[512,2048]{1,0:T(8,128)}, f32[2048,2048]{1,0:T(8,128)}, f32[2048,2048]{1,0:T(8,128)}, f32[2048,2048]{1,0:T(8,128)}, f32[1,2048]{1,0:T(1,128)},...) custom-call(f32[512,2048]{1,0:T(8,128)} %get-tuple-element.30.refs_0_, ...), custom_call_target="tpu_custom_call" | custom-call | tf_op jit(solution)/shard_map/copy_out/pallas_call | solution.py:1031

commit v12 on v11

--- a/solution.py
+++ b/solution.py
@@ -20,13 +20,15 @@
 PARTS = 16
 GROUP = 4
 MATS = 3
-ACC_SLOTS = 20
-GATHER_SLOTS = 16
+ACC_SLOTS = 16
+GATHER_SLOTS = 14
+BACK_VMEM = 49_800_000
+COPY_VMEM = 40 * 1024 * 1024
 JOBS = 6
 W_BUFS = 3
 LAYER_SLOTS = 15
 COPY_ROWS = 256
-COPY_BUFS = 20
+COPY_BUFS = 16
 FRONT_PLAN = ((0, 0, 3, 5, 7, 9, 12, 13, 16, 17, 18), (0, 6, 3, 4, 9, 10, 8, 5, 2, 7, 1))
 BACK_PLAN = ((0, 0, 3, 5, 7, 8, 9, 11, 14, 17, 19), (0, 4, 8, 7, 10, 1, 2, 3, 5, 6, 9))
 
@@ -148,10 +150,29 @@
     return SmallSum(place, *refs[:5], refs[5:])
 
 
+class Homed:
+    def __init__(self, homes, make):
+        self.homes, self.make = homes, make
+
+    def do(self, what):
+        for when, home in self.homes:
+            run = lambda home=home: getattr(self.make(home), what)()
+            run() if when is None else pl.when(when)(run)
+
+    def start(self):
+        self.do("start")
+
+    def wait_recv(self):
+        self.do("wait_recv")
+
+    def wait_send(self):
+        self.do("wait_send")
+
+
 class ChunkSum:
-    def __init__(self, place, kinds, is_kind, acc, gathered, landing, send, recv, finish):
-        self.p, self.kinds, self.is_kind, self.slots, self.gather_slots = place, kinds, is_kind, acc.shape[0], gathered.shape[0]
-        self.acc, self.gathered, self.landing, self.send, self.recv, self.finish = acc, gathered, landing, send, recv, finish
+    def __init__(self, place, kinds, is_kind, acc, homes, landing, send, recv, finish):
+        self.p, self.kinds, self.is_kind, self.slots, self.homes = place, kinds, is_kind, acc.shape[0], homes
+        self.acc, self.landing, self.send, self.recv, self.finish = acc, landing, send, recv, finish
         self.size = acc.shape[1]
         self.s2, self.s4 = self.size // 2, self.size // 4
         core, bx, by, me = place.core, place.bx, place.by, place.me
@@ -175,8 +196,7 @@
         return self.copy(self.acc.at[j, self.span(off, size)], buf.at[j, pl.ds(0, size)], stage, k, mate)
 
     def up(self, stage, k, off, size, mate):
-        block = self.gathered.at[k % self.gather_slots, self.span(off, size)]
-        return self.copy(block, block, stage, k, mate)
+        return Homed(self.homes(k), lambda home: self.copy(home(off, size), home(off, size), stage, k, mate))
 
     def add(self, k, off, size, buf):
         step = min(size, 16)
@@ -585,7 +605,7 @@
             place.all_here()
             start_x(0)
 
-        pl.when((i == 0) & (job > 0))(lambda: small.middle(job - 1))
+        pl.when((i == 1) & (job > 0))(lambda: small.middle(job - 1))
 
         @pl.when(i == tiles - 1)
         def _():
@@ -611,7 +631,10 @@
         loss[...] += share * jnp.sum(jnp.where(diag, miss * miss, weight * (corr * corr)), axis=0, keepdims=True)
         gathered[k, at] = jnp.where(diag, -2.0 * miss, 2.0 * weight * corr).astype(jnp.bfloat16)
 
-    chunks = ChunkSum(place, "xsl", front_kind, acc, gathered, landing, send, recv, finish)
+    def homes(k):
+        return [(None, lambda off, size: gathered.at[k, pl.ds(pl.multiple_of(off, part_rows // 4), size)])]
+
+    chunks = ChunkSum(place, "xsl", front_kind, acc, homes, landing, send, recv, finish)
 
     def form(k, group):
         at = rows(k * part_rows, group * part_rows)
@@ -763,18 +786,23 @@
 
 
 def back_kernel(dz_hbm, x2, x1, x0, w_out, w_mid, u2, u1, vec, out2, out1, out0, sums_out, *scratch):
-    (dy, xs, w_buf, u_buf, dpre) = scratch[:5]
-    (in_sem, tile_sem, peer_send, peer_recv, store_sem) = scratch[5:10]
-    small_refs = scratch[10 : 10 + SMALL_REFS]
-    acc, gathered, *landing, send, recv = scratch[10 + SMALL_REFS :]
-    rows_dev, width = dpre.shape
-    wide = w_buf.shape[1]
+    (dy, xs, w_buf) = scratch[:3]
+    (in_sem, tile_sem, peer_send, peer_recv, store_sem) = scratch[3:8]
+    small_refs = scratch[8 : 8 + SMALL_REFS]
+    acc, gathered, *landing, send, recv = scratch[8 + SMALL_REFS :]
+    rows_dev, width = u2.shape
+    wide = w_buf.shape[0]
     tiles = width // wide
     row_count = rows_dev * DEPTH * PLANE
     half = width // 2
     part_rows = half // PARTS
     count = MATS * PARTS
-    mats_in, outs, weights, pres = (x2, x1, x0), (out2, out1, out0), (w_out, w_mid), (u2, u1)
+    mats_in, outs, weights, pres = (x2, x1, x0), (out2, out1), (w_out, w_mid), (u2, u1)
+    dpre = out0.at[pl.ds(0, rows_dev)]
+
+    def u_buf(i):
+        return out0.at[pl.ds(rows_dev, rows_dev), rows((i % 2) * wide, wide)]
+
     place = Place()
     core, other_core = place.core, place.other_core
     mine = rows(core * rows_dev, rows_dev)
@@ -790,10 +818,10 @@
         return remote_copy(block, block, peer_send.at[w], peer_recv.at[w], other_core)
 
     def w_tile(ref, i):
-        return pltpu.make_async_copy(ref.at[rows(i * wide, wide)], w_buf.at[i % 2], tile_sem.at[0, i % 2])
+        return pltpu.make_async_copy(ref.at[rows(i * wide, wide)], w_buf, tile_sem.at[0, 0])
 
     def u_tile(ref, i):
-        return pltpu.make_async_copy(ref.at[:, rows(i * wide, wide)], u_buf.at[i % 2], tile_sem.at[1, i % 2])
+        return pltpu.make_async_copy(ref.at[:, rows(i * wide, wide)], u_buf(i), tile_sem.at[1, i % 2])
 
     def start_w(layer, i):
         pick(layer, weights, lambda ref: w_tile(ref, i).start())
@@ -821,18 +849,15 @@
         w_tile(w_out, i).wait()
         u_tile(u2, i).wait()
 
-        @pl.when(i + 1 < tiles)
-        def _():
-            start_w(layer, i + 1)
-            start_u(layer, i + 1)
-
+        pl.when(i + 1 < tiles)(lambda: start_u(layer, i + 1))
         at_cols = rows(i * wide, wide)
-        dpre[:, at_cols] = contract_cols(dy[layer, mine], w_buf[i % 2])
+        dpre[:, at_cols] = contract_cols(dy[layer, mine], w_buf[...])
+        pl.when(i + 1 < tiles)(lambda: start_w(layer, i + 1))
         gain, bias, mean, inv = (vec[layer * 4 + j, :, at_cols] for j in range(4))
 
         def block(r, carry):
             at = rows(r * BLOCK, BLOCK)
-            n = (u_buf[i % 2, at] - mean) * inv
+            n = (out0[rows(rows_dev + r * BLOCK, BLOCK), rows((i % 2) * wide, wide)] - mean) * inv
             g = jnp.where(n * gain + bias > 0.0, dpre[at, at_cols], 0.0)
             dpre[at, at_cols] = g
             return carry[0] + fold(g * n), carry[1] + fold(g)
@@ -854,18 +879,38 @@
 
         def block(r, c):
             at = rows(r * BLOCK, BLOCK)
-            n = (u_buf[i % 2, at] - mean) * inv
+            n = (out0[rows(rows_dev + r * BLOCK, BLOCK), rows((i % 2) * wide, wide)] - mean) * inv
             value = (dpre[at, at_cols] - mean_g - n * mean_gn) * scale
             dy[1 - layer, rows(core * rows_dev + r * BLOCK, BLOCK), at_cols] = value.astype(jnp.bfloat16)
             return c
 
         row_loop(block, 0)
 
+    in_last = (MATS - 1) * PARTS
+    quarter = part_rows // 4
+
+    def home_row(k):
+        return core * half + (k % PARTS) * part_rows
+
+    def homes(k):
+        return [
+            (k < in_last, lambda off, size: gathered.at[k % GATHER_SLOTS, pl.ds(pl.multiple_of(off, quarter), size)]),
+            (k >= in_last, lambda off, size: out0.at[pl.ds(pl.multiple_of(home_row(k) + off, quarter), size)]),
+        ]
+
     def finish(k, off, size, buf):
         j = k % ACC_SLOTS
-        gathered[k % GATHER_SLOTS, rows(off, size)] = acc[j, rows(off, size)] + buf[j]
-
-    chunks = ChunkSum(place, "xl", back_kind, acc, gathered, landing, send, recv, finish)
+        value = acc[j, rows(off, size)] + buf[j]
+
+        @pl.when(k < in_last)
+        def _():
+            gathered[k % GATHER_SLOTS, rows(off, size)] = value
+
+        @pl.when(k >= in_last)
+        def _():
+            out0[rows(home_row(k) + off, size)] = value
+
+    chunks = ChunkSum(place, "xl", back_kind, acc, homes, landing, send, recv, finish)
 
     def form(k, group):
         w, j = k // PARTS, k % ACC_SLOTS
@@ -898,14 +943,22 @@
             form_next(k, form)
             return
         chunks.stage(i, k)
+        own_rows = out0.at[pl.ds(pl.multiple_of(home_row(k), part_rows), part_rows)]
+        in_place = chunks.copy(own_rows, own_rows, 7, k, other_core)
+        last = k // PARTS == MATS - 1
+
         def emit(out):
             last_copy(out, k, core).start()
             store_copy(out, k).start()
 
+        def emit_any():
+            pick(k // PARTS, outs, emit)
+            pl.when(last)(lambda: in_place.start())
+
         if i == 8:
-            pl.when(back_kind("x", k))(lambda: pick(k // PARTS, outs, emit))
+            pl.when(back_kind("x", k))(emit_any)
         if i == 9:
-            pl.when(back_kind("l", k))(lambda: pick(k // PARTS, outs, emit))
+            pl.when(back_kind("l", k))(emit_any)
         if i == 10:
 
             def close(out):
@@ -914,6 +967,11 @@
                 last_copy(out, k, core).wait_send()
 
             pick(k // PARTS, outs, close)
+
+            @pl.when(last)
+            def _():
+                in_place.wait_recv()
+                in_place.wait_send()
 
     def layer_work(t):
         layer = t // LAYER_SLOTS
@@ -961,15 +1019,13 @@
     return pl.pallas_call(
         back_kernel,
         name="backward",
-        out_shape=[mat, mat, mat, jax.ShapeDtypeStruct((5, width), jnp.float32)],
+        out_shape=[mat, mat, pltpu.VMEM((width, width), jnp.float32), jax.ShapeDtypeStruct((5, width), jnp.float32)],
         in_specs=[any_spec] * 8 + [vmem_spec],
-        out_specs=[any_spec] * 3 + [vmem_spec],
+        out_specs=[any_spec] * 2 + [vmem_spec] * 2,
         scratch_shapes=[
             pltpu.VMEM((2, 2 * rows_dev, width), jnp.bfloat16),
             pltpu.VMEM((2, 2 * rows_dev, width // 2), jnp.bfloat16),
-            pltpu.VMEM((2, WIDE, width), jnp.bfloat16),
-            pltpu.VMEM((2, rows_dev, WIDE), jnp.float32),
-            pltpu.VMEM((rows_dev, width), jnp.float32),
+            pltpu.VMEM((WIDE, width), jnp.bfloat16),
             dma((MATS + 2,)),
             dma((2, 2)),
             dma((MATS,)),
@@ -978,15 +1034,16 @@
         ]
         + small_scratch(2)
         + chunk_scratch(ACC_SLOTS, GATHER_SLOTS, part_rows, width, count, jnp.float32),
-        compiler_params=pltpu.CompilerParams(collective_id=1, has_side_effects=True, vmem_limit_bytes=VMEM_BYTES),
+        compiler_params=pltpu.CompilerParams(collective_id=1, has_side_effects=True, vmem_limit_bytes=BACK_VMEM),
     )(grad_z, x2, x1, x0, w_out, w_mid, u2, u1, vec)
 
 
 def copy_kernel(*refs):
-    pairs = (len(refs) - 5 - 6) // 2
-    ins, small, outs, small_outs = refs[:pairs], refs[pairs], refs[pairs + 1 : 2 * pairs + 1], refs[2 * pairs + 1 : -5]
-    buf, small_buf, in_sem, out_sem, small_sem = refs[-5:]
-    blocks = [(i, r) for i in range(pairs) for r in range(0, ins[i].shape[0], COPY_ROWS)]
+    pairs = (len(refs) - 6 - 6) // 2
+    ins, small, outs, small_outs = refs[:pairs], refs[pairs], refs[pairs + 1 : 2 * pairs + 1], refs[2 * pairs + 1 : -6]
+    buf, small_buf, in_sem, out_sem, small_sem, near_sem = refs[-6:]
+    blocks = [(i, r) for i in range(pairs - 1) for r in range(0, ins[i].shape[0], COPY_ROWS)]
+    near = pltpu.make_async_copy(ins[-1], outs[-1], near_sem.at[0])
 
     def read(b):
         i, r = blocks[b]
@@ -999,6 +1056,7 @@
     ahead = COPY_BUFS // 2
     for b in range(min(ahead, len(blocks))):
         read(b).start()
+    near.start()
     pltpu.make_async_copy(small, small_buf, small_sem.at[4]).start()
 
     def small_write(row):
@@ -1018,6 +1076,7 @@
                 small_write(row).start()
     for row in range(4):
         small_write(row).wait()
+    near.wait()
     for b in range(max(0, len(blocks) - COPY_BUFS), len(blocks)):
         write(b).wait()
 
@@ -1032,7 +1091,7 @@
         copy_kernel,
         name="copy_out",
         out_shape=[jax.ShapeDtypeStruct(a.shape, a.dtype) for a in arrays] + [row] * 4 + [jax.ShapeDtypeStruct((1, 1), jnp.float32)],
-        in_specs=[any_spec] * (len(arrays) + 1),
+        in_specs=[any_spec] * (len(arrays) - 1) + [vmem_spec, any_spec],
         out_specs=[any_spec] * (len(arrays) + 4) + [vmem_spec],
         scratch_shapes=[
             pltpu.VMEM((COPY_BUFS, COPY_ROWS, width), jnp.float32),
@@ -1040,9 +1099,10 @@
             dma((COPY_BUFS,)),
             dma((COPY_BUFS,)),
             dma((5,)),
+            dma((1,)),
         ],
-        compiler_params=pltpu.CompilerParams(vmem_limit_bytes=VMEM_BYTES),
-    )(*arrays, small)
+        compiler_params=pltpu.CompilerParams(vmem_limit_bytes=COPY_VMEM),
+    )(*arrays[:-1], pltpu.with_memory_space_constraint(arrays[-1], pltpu.VMEM), small)
 
 
 def solution(mesh):

time: 563 us -> 553 us (0.982)
  Pallas kernels: 562 us -> 551 us
where the time goes in v12:
time: 553 us
  Pallas kernels  551 us (100%)
    pallas_call x1, Pallas kernels, backward(): pl.pallas_call(back_kernel, name='backward', out_shape=[mat, mat, pltpu.V...  343 us
    pallas_call x1, Pallas kernels, front(): pl.pallas_call(front_kernel, name='front', out_shape=[wide_f32, wide_f32,...  176 us
    pallas_call x1, Pallas kernels, copy_out(): pl.pallas_call(copy_kernel, name='copy_out', out_shape=[jax.ShapeDtypeStr...  31.8 us

profile of v12, /device:TPU:0, one launch (start us, length us, event | category | flops | bytes accessed | tf_op | source)
XLA Modules:
  0.0 552.7 jit_solution(8543158758649081518)
XLA Ops:
  1.3 176.2 %front.1 = (f32[512,2048]{1,0:T(8,128)}, f32[512,2048]{1,0:T(8,128)}, bf16[1024,1024]{1,0:T(8,128)(2,1)}, bf16[1024,1024]{1,0:T(8,128)(2,1)}, bf16[1024,1024]{1,...) custom-call(bf16[512,2048]{1,0:T(8,128)(2,1)} %feat_a.1, ...), custom_call_target="tpu_custom_call" | custom-call | tf_op jit(solution)/shard_map/front/pallas_call | solution.py:755
  177.5 343.4 %backward.1 = (f32[2048,2048]{1,0:T(8,128)}, f32[2048,2048]{1,0:T(8,128)}, f32[2048,2048]{1,0:T(8,128)S(1)}, f32[5,2048]{1,0:T(8,128)}) custom-call(bf16[1024,2048]{1,0:T(8,128)(2,1)} %get-tuple-element.31.dz_hbm, bf16[1024,1024]{1,0:T(8,128)(2,1)} %get-tuple-element.32.x2, bf16[1024,1024]{1,0:T(8,128)(2,1)} %get-tuple-element.33.x1, ...), custom_call_target="tpu_custom_call" | custom-call | tf_op jit(solution)/shard_map/backward/pallas_call | solution.py:1019
  520.9 31.8 %copy_out.1 = (f32[512,2048]{1,0:T(8,128)}, f32[2048,2048]{1,0:T(8,128)}, f32[2048,2048]{1,0:T(8,128)}, f32[2048,2048]{1,0:T(8,128)}, f32[1,2048]{1,0:T(1,128)},...) custom-call(f32[512,2048]{1,0:T(8,128)} %get-tuple-element.30.refs_0_, ...), custom_call_target="tpu_custom_call" | custom-call | tf_op jit(solution)/shard_map/copy_out/pallas_call | solution.py:1090

commit v13 on v12

--- a/solution.py
+++ b/solution.py
@@ -20,17 +20,19 @@
 PARTS = 16
 GROUP = 4
 MATS = 3
-ACC_SLOTS = 16
-GATHER_SLOTS = 14
+BACK_PARTS = 32
+BACK_GROUP = 8
+ACC_SLOTS = 32
+GATHER_SLOTS = 28
 BACK_VMEM = 49_800_000
-COPY_VMEM = 40 * 1024 * 1024
+COPY_VMEM = 42 * 1024 * 1024
 JOBS = 6
 W_BUFS = 3
 LAYER_SLOTS = 15
 COPY_ROWS = 256
-COPY_BUFS = 16
+COPY_BUFS = 18
 FRONT_PLAN = ((0, 0, 3, 5, 7, 9, 12, 13, 16, 17, 18), (0, 6, 3, 4, 9, 10, 8, 5, 2, 7, 1))
-BACK_PLAN = ((0, 0, 3, 5, 7, 8, 9, 11, 14, 17, 19), (0, 4, 8, 7, 10, 1, 2, 3, 5, 6, 9))
+BACK_PLAN = ((0, 0, 6, 10, 14, 16, 19, 23, 27, 32, 34), (0, 4, 10, 2, 7, 8, 3, 1, 9, 5, 6))
 
 
 def front_kind(kind, k):
@@ -39,7 +41,8 @@
 
 
 def back_kind(kind, k):
-    l = ((k % 5 == 2) & (k < 43)) | ((k % 5 == 0) & (k >= 10) & (k < 36))
+    p = k // 2
+    l = ((p % 5 == 2) & (p < 43)) | ((p % 5 == 0) & (p >= 10) & (p < 36)) | (k == 58)
     return l if kind == "l" else jnp.logical_not(l)
 
 
@@ -199,7 +202,7 @@
         return Homed(self.homes(k), lambda home: self.copy(home(off, size), home(off, size), stage, k, mate))
 
     def add(self, k, off, size, buf):
-        step = min(size, 16)
+        step = min(self.s4, 16)
         j = k % self.slots
 
         def body(i):
@@ -384,9 +387,9 @@
                 rest_back().wait_send()
 
 
-def form_next(k, form):
-    pl.when(k == 1)(lambda: form(GROUP // 2, GROUP // 2))
-    pl.when((k % GROUP == 0) & (k > 0))(lambda: form(k, GROUP))
+def form_next(k, group, form):
+    pl.when(k == 1)(lambda: form(group // 2, group // 2))
+    pl.when((k % group == 0) & (k > 0))(lambda: form(k, group))
 
 
 def run_slots(plan, count, stage, between):
@@ -677,7 +680,7 @@
 
     def stage(i, k):
         if i == 0:
-            form_next(k, form)
+            form_next(k, GROUP, form)
             return
         chunks.stage(i, k)
         if i == 8:
@@ -795,8 +798,8 @@
     tiles = width // wide
     row_count = rows_dev * DEPTH * PLANE
     half = width // 2
-    part_rows = half // PARTS
-    count = MATS * PARTS
+    part_rows = half // BACK_PARTS
+    count = MATS * BACK_PARTS
     mats_in, outs, weights, pres = (x2, x1, x0), (out2, out1), (w_out, w_mid), (u2, u1)
     dpre = out0.at[pl.ds(0, rows_dev)]
 
@@ -886,11 +889,11 @@
 
         row_loop(block, 0)
 
-    in_last = (MATS - 1) * PARTS
+    in_last = (MATS - 1) * BACK_PARTS
     quarter = part_rows // 4
 
     def home_row(k):
-        return core * half + (k % PARTS) * part_rows
+        return core * half + (k % BACK_PARTS) * part_rows
 
     def homes(k):
         return [
@@ -913,14 +916,14 @@
     chunks = ChunkSum(place, "xl", back_kind, acc, homes, landing, send, recv, finish)
 
     def form(k, group):
-        w, j = k // PARTS, k % ACC_SLOTS
-
-        @pl.when(k % PARTS == 0)
+        w, j = k // BACK_PARTS, k % ACC_SLOTS
+
+        @pl.when(k % BACK_PARTS == 0)
         def _():
             pltpu.make_async_copy(xs.at[w % 2], xs.at[w % 2], in_sem.at[w]).wait()
             pl.when(w > 0)(lambda: peer_dy(w).wait_recv())
 
-        at = rows((k % PARTS) * part_rows, group * part_rows)
+        at = rows((k % BACK_PARTS) * part_rows, group * part_rows)
 
         def col(c):
             pl.when(k == 0)(lambda: load_dz(c).wait())
@@ -930,7 +933,7 @@
         loop(0, width // size, col)
 
     def out_rows(k, side):
-        return pl.ds(pl.multiple_of(side * half + (k % PARTS) * part_rows, part_rows), part_rows)
+        return pl.ds(pl.multiple_of(side * half + (k % BACK_PARTS) * part_rows, part_rows), part_rows)
 
     def last_copy(out, k, side):
         return chunks.copy(gathered.at[k % GATHER_SLOTS], out.at[out_rows(k, side)], 7, k, other_core)
@@ -940,19 +943,19 @@
 
     def stage(i, k):
         if i == 0:
-            form_next(k, form)
+            form_next(k, BACK_GROUP, form)
             return
         chunks.stage(i, k)
         own_rows = out0.at[pl.ds(pl.multiple_of(home_row(k), part_rows), part_rows)]
         in_place = chunks.copy(own_rows, own_rows, 7, k, other_core)
-        last = k // PARTS == MATS - 1
+        last = k // BACK_PARTS == MATS - 1
 
         def emit(out):
             last_copy(out, k, core).start()
             store_copy(out, k).start()
 
         def emit_any():
-            pick(k // PARTS, outs, emit)
+            pick(k // BACK_PARTS, outs, emit)
             pl.when(last)(lambda: in_place.start())
 
         if i == 8:
@@ -966,7 +969,7 @@
                 store_copy(out, k).wait()
                 last_copy(out, k, core).wait_send()
 
-            pick(k // PARTS, outs, close)
+            pick(k // BACK_PARTS, outs, close)
 
             @pl.when(last)
             def _():
@@ -997,9 +1000,9 @@
 
             pl.when(layer == 1)(lambda: load_x(2).start())
 
-    form(0, GROUP // 2)
+    form(0, BACK_GROUP // 2)
     place.all_here()
-    run_slots(BACK_PLAN, count, stage, lambda t: pl.when(t < 2 * LAYER_SLOTS)(lambda: layer_work(t)))
+    run_slots(BACK_PLAN, count, stage, lambda t: pl.when((t % 2 == 0) & (t < 4 * LAYER_SLOTS))(lambda: layer_work(t // 2)))
     for w in (1, 2):
         peer_dy(w).wait_send()
     for c in range(PLANE):
@@ -1010,8 +1013,8 @@
 
 def backward(grad_z, x2, x1, x0, w_out, w_mid, u2, u1, vec):
     rows_dev, width = u2.shape
-    part_rows = width // 2 // PARTS
-    count = MATS * PARTS
+    part_rows = width // 2 // BACK_PARTS
+    count = MATS * BACK_PARTS
     any_spec = pl.BlockSpec(memory_space=pl.ANY)
     vmem_spec = pl.BlockSpec(memory_space=pltpu.VMEM)
     mat = jax.ShapeDtypeStruct((width, width), jnp.float32)
@@ -1053,31 +1056,27 @@
         i, r = blocks[b]
         return pltpu.make_async_copy(buf.at[b % COPY_BUFS], outs[i].at[pl.ds(r, COPY_ROWS)], out_sem.at[b % COPY_BUFS])
 
-    ahead = COPY_BUFS // 2
-    for b in range(min(ahead, len(blocks))):
+    for b in range(len(blocks)):
         read(b).start()
-    near.start()
-    pltpu.make_async_copy(small, small_buf, small_sem.at[4]).start()
+    small_read = pltpu.make_async_copy(small, small_buf, small_sem.at[4])
+    small_read.start()
 
     def small_write(row):
         return pltpu.make_async_copy(small_buf.at[pl.ds(row, 1)], small_outs[row], small_sem.at[row])
 
     for b in range(len(blocks)):
-        if b + ahead < len(blocks):
-            if b + ahead >= COPY_BUFS:
-                write(b + ahead - COPY_BUFS).wait()
-            read(b + ahead).start()
         read(b).wait()
+    near.start()
+    for b in range(len(blocks)):
         write(b).start()
-        if b == 0:
-            pltpu.make_async_copy(small, small_buf, small_sem.at[4]).wait()
-            small_outs[4][...] = small_buf[4:5, :1]
-            for row in range(4):
-                small_write(row).start()
+    small_read.wait()
+    small_outs[4][...] = small_buf[4:5, :1]
+    for row in range(4):
+        small_write(row).start()
     for row in range(4):
         small_write(row).wait()
     near.wait()
-    for b in range(max(0, len(blocks) - COPY_BUFS), len(blocks)):
+    for b in range(len(blocks)):
         write(b).wait()
 
 

time: 553 us -> 555 us (level)
  no operation moved by 1% of the time
where the time goes in v13:
time: 555 us; the launch traced here: 554 us
  Pallas kernels  553 us (100%)
    pallas_call x1, Pallas kernels, backward(): pl.pallas_call(back_kernel, name='backward', out_shape=[mat, mat, pltpu.V...  347 us
    pallas_call x1, Pallas kernels, front(): pl.pallas_call(front_kernel, name='front', out_shape=[wide_f32, wide_f32,...  176 us
    pallas_call x1, Pallas kernels, copy_out(): pl.pallas_call(copy_kernel, name='copy_out', out_shape=[jax.ShapeDtypeStr...  29.9 us

profile of v13, /device:TPU:0, one launch (start us, length us, event | category | flops | bytes accessed | tf_op | source)
XLA Modules:
  0.0 554.5 jit_solution(540742571958840422)
XLA Ops:
  1.3 176.2 %front.1 = (f32[512,2048]{1,0:T(8,128)}, f32[512,2048]{1,0:T(8,128)}, bf16[1024,1024]{1,0:T(8,128)(2,1)}, bf16[1024,1024]{1,0:T(8,128)(2,1)}, bf16[1024,1024]{1,...) custom-call(bf16[512,2048]{1,0:T(8,128)(2,1)} %feat_a.1, ...), custom_call_target="tpu_custom_call" | custom-call | tf_op jit(solution)/shard_map/front/pallas_call | solution.py:758
  177.5 346.9 %backward.1 = (f32[2048,2048]{1,0:T(8,128)}, f32[2048,2048]{1,0:T(8,128)}, f32[2048,2048]{1,0:T(8,128)S(1)}, f32[5,2048]{1,0:T(8,128)}) custom-call(bf16[1024,2048]{1,0:T(8,128)(2,1)} %get-tuple-element.31.dz_hbm, bf16[1024,1024]{1,0:T(8,128)(2,1)} %get-tuple-element.32.x2, bf16[1024,1024]{1,0:T(8,128)(2,1)} %get-tuple-element.33.x1, ...), custom_call_target="tpu_custom_call" | custom-call | tf_op jit(solution)/shard_map/backward/pallas_call | solution.py:1022
  524.4 29.9 %copy_out.1 = (f32[512,2048]{1,0:T(8,128)}, f32[2048,2048]{1,0:T(8,128)}, f32[2048,2048]{1,0:T(8,128)}, f32[2048,2048]{1,0:T(8,128)}, f32[1,2048]{1,0:T(1,128)},...) custom-call(f32[512,2048]{1,0:T(8,128)} %get-tuple-element.30.refs_0_, ...), custom_call_target="tpu_custom_call" | custom-call | tf_op jit(solution)/shard_map/copy_out/pallas_call | solution.py:1089

commit v14 on v12

--- a/solution.py
+++ b/solution.py
@@ -17,18 +17,19 @@
 WIDE = 512
 BLOCK = 128
 SUM_ROWS = 2
+SUM_PARTS = ((0, 6), (6, 2))
 PARTS = 16
 GROUP = 4
 MATS = 3
 ACC_SLOTS = 16
 GATHER_SLOTS = 14
 BACK_VMEM = 49_800_000
-COPY_VMEM = 40 * 1024 * 1024
+COPY_VMEM = 42 * 1024 * 1024
 JOBS = 6
 W_BUFS = 3
 LAYER_SLOTS = 15
 COPY_ROWS = 256
-COPY_BUFS = 16
+COPY_BUFS = 18
 FRONT_PLAN = ((0, 0, 3, 5, 7, 9, 12, 13, 16, 17, 18), (0, 6, 3, 4, 9, 10, 8, 5, 2, 7, 1))
 BACK_PLAN = ((0, 0, 3, 5, 7, 8, 9, 11, 14, 17, 19), (0, 4, 8, 7, 10, 1, 2, 3, 5, 6, 9))
 
@@ -99,48 +100,54 @@
         self.p, self.payload, self.total = place, payload, total
         self.depth_buf, self.line_sum, self.plane_buf, self.sems = depth_buf, line_sum, plane_buf, sems
 
-    def along(self, j, lv, slot):
-        s, r = self.sems[0], self.sems[1]
-        return remote_copy(self.payload.at[j], self.depth_buf.at[j, slot], s.at[j, lv], r.at[j, slot], lv * PLANE + self.p.pos)
-
-    def within(self, j, m, slot):
-        s, r = self.sems[2], self.sems[3]
-        return remote_copy(self.line_sum.at[j], self.plane_buf.at[j, slot], s.at[j, m], r.at[j, slot], self.p.plane * PLANE + m)
-
-    def begin(self, j):
+    def along(self, j, part, lv, slot):
+        (s, r), at = self.sems[:2], pl.ds(*SUM_PARTS[part])
+        n = part * DEPTH
+        return remote_copy(self.payload.at[j, at], self.depth_buf.at[j, slot, at], s.at[j, n + lv], r.at[j, n + slot], lv * PLANE + self.p.pos)
+
+    def within(self, j, part, m, slot):
+        (s, r), at = self.sems[2:], pl.ds(*SUM_PARTS[part])
+        n = part * PLANE
+        return remote_copy(self.line_sum.at[j, at], self.plane_buf.at[j, slot, at], s.at[j, n + m], r.at[j, n + slot], self.p.plane * PLANE + m)
+
+    def begin(self, j, part):
+        at = pl.ds(*SUM_PARTS[part])
         for lv in self.p.levels:
-            self.along(j, lv, self.p.plane).start()
-        self.depth_buf[j, self.p.plane] = self.payload[j]
-
-    def middle(self, j):
+            self.along(j, part, lv, self.p.plane).start()
+        self.depth_buf[j, self.p.plane, at] = self.payload[j, at]
+
+    def middle(self, j, part):
+        at = pl.ds(*SUM_PARTS[part])
         for lv in self.p.levels:
-            self.along(j, lv, lv).wait_recv()
-        total = self.depth_buf[j, 0]
+            self.along(j, part, lv, lv).wait_recv()
+        total = self.depth_buf[j, 0, at]
         for i in range(1, DEPTH):
-            total = total + self.depth_buf[j, i]
-        self.line_sum[j] = total
+            total = total + self.depth_buf[j, i, at]
+        self.line_sum[j, at] = total
         for m in self.p.mates:
-            self.within(j, m, self.p.pos).start()
-        self.plane_buf[j, self.p.pos] = total
+            self.within(j, part, m, self.p.pos).start()
+        self.plane_buf[j, self.p.pos, at] = total
 
     def end(self, j):
-        for m in self.p.mates:
-            self.within(j, m, m).wait_recv()
+        for part in range(len(SUM_PARTS)):
+            for m in self.p.mates:
+                self.within(j, part, m, m).wait_recv()
         total = self.plane_buf[j, 0]
         for i in range(1, PLANE):
             total = total + self.plane_buf[j, i]
         self.total[j] = total
-        for lv in self.p.levels:
-            self.along(j, lv, self.p.plane).wait_send()
-        for m in self.p.mates:
-            self.within(j, m, self.p.pos).wait_send()
+        for part in range(len(SUM_PARTS)):
+            for lv in self.p.levels:
+                self.along(j, part, lv, self.p.plane).wait_send()
+            for m in self.p.mates:
+                self.within(j, part, m, self.p.pos).wait_send()
 
 
 def small_scratch(count):
     def buf(*lead):
         return pltpu.VMEM((count, *lead, PLANE, SUM_ROWS, TILE), jnp.float32)
 
-    return [buf(), buf(), buf(DEPTH), buf(), buf(PLANE)] + [pltpu.SemaphoreType.DMA((count, n)) for n in (DEPTH, DEPTH, PLANE, PLANE)]
+    return [buf(), buf(), buf(DEPTH), buf(), buf(PLANE)] + [pltpu.SemaphoreType.DMA((count, n * len(SUM_PARTS))) for n in (DEPTH, DEPTH, PLANE, PLANE)]
 
 
 SMALL_REFS = 9
@@ -508,9 +515,7 @@
         for row, value in enumerate(row_loop(block, (zero, zero))):
             put_sums(job, i * (wide // TILE), row, value)
 
-    def begin(job):
-        small.begin(job)
-
+    def keep(job):
         @pl.when(job % 2 == 0)
         def _():
             pick(job // 2, (pre1, pre2), lambda ref: keep_pre(ref).start())
@@ -605,15 +610,19 @@
             place.all_here()
             start_x(0)
 
-        pl.when((i == 1) & (job > 0))(lambda: small.middle(job - 1))
+        pl.when(i == tiles - 2)(lambda: small.begin(job, 0))
+        pl.when((i == 0) & (job > 0))(lambda: small.middle(job - 1, 0))
+        pl.when((i == 1) & (job > 0))(lambda: small.middle(job - 1, 1))
 
         @pl.when(i == tiles - 1)
         def _():
-            begin(job)
+            small.begin(job, 1)
+            keep(job)
+            pl.when(job == JOBS - 1)(lambda: small.middle(job, 0))
             pl.when(job > 0)(lambda: norm(job - 1))
 
     loop(0, JOBS * tiles, step)
-    small.middle(JOBS - 1)
+    small.middle(JOBS - 1, 1)
     norm(JOBS - 1)
     for j, source in enumerate((affine.at[2], affine.at[3], stats.at[2, 0], stats.at[2, 1], affine.at[0], affine.at[1], stats.at[0, 0], stats.at[0, 1])):
         vec[j] = source[...]
@@ -673,7 +682,7 @@
 
         zero = jnp.zeros((8, GROUP * part_rows), jnp.float32)
         for row, value in enumerate(row_loop(block, (zero, zero))):
-            payload[JOBS, (side * half + k * part_rows) // TILE, row : row + 1] = jnp.sum(value, axis=0, keepdims=True)
+            payload[JOBS, 2 * (k // GROUP) + side, row : row + 1] = jnp.sum(value, axis=0, keepdims=True)
 
     def stage(i, k):
         if i == 0:
@@ -697,18 +706,21 @@
             def _():
                 embed(k - GROUP + 1, 1 - core, g_peer[pl.ds(k - GROUP + 1, GROUP)])
 
+            pl.when(k == PARTS - GROUP - 1)(lambda: small.begin(JOBS, 0))
+            pl.when(k == PARTS - 2)(lambda: small.middle(JOBS, 0))
+
     ea_copy().wait_recv()
     form(0, GROUP // 2)
     run_slots(FRONT_PLAN, PARTS, stage, lambda t: None)
-    small.begin(JOBS)
+    small.begin(JOBS, 1)
     for c in range(PLANE):
         payload[JOBS + 1, c, 0:1] = loss[:, c * TILE : (c + 1) * TILE]
-    small.begin(JOBS + 1)
     ea_copy().wait_send()
     for i in range(tiles):
         eb_copy(i).wait_send()
-    small.middle(JOBS)
-    small.middle(JOBS + 1)
+    small.middle(JOBS, 1)
+    for part in range(len(SUM_PARTS)):
+        small.begin(JOBS + 1, part)
     for k in range(0, PARTS, GROUP):
         for side in range(2):
             ge_copy(k, side).wait()
@@ -716,7 +728,9 @@
 
     def dz_tile(i):
         at_cols = rows(i * wide, wide)
-        sums = jnp.concatenate([total[JOBS, i * (wide // TILE) + c] for c in range(wide // TILE)], axis=1) / row_count
+        groups, side = tiles // 2, i // (tiles // 2)
+        first = (i % groups) * (wide // TILE)
+        sums = jnp.concatenate([total[JOBS, 2 * (first + c) + side] for c in range(wide // TILE)], axis=1) / row_count
         mean_gn, mean_g = sums[0:1], sums[1:2]
         inv = stats[JOBS - 2, 1, :, at_cols]
 
@@ -730,6 +744,8 @@
             c.start()
 
     loop(0, tiles, dz_tile)
+    for part in range(len(SUM_PARTS)):
+        small.middle(JOBS + 1, part)
     small.end(JOBS + 1)
     for c in range(PLANE):
         vec[8, :, c * TILE : (c + 1) * TILE] = total[JOBS + 1, c, 0:1]
@@ -978,8 +994,16 @@
         at = t - LAYER_SLOTS * layer
         first_du = 2 * tiles + 3
         pl.when((at < 2 * tiles) & (at % 2 == 1))(lambda: chain_tile(layer, at // 2))
-        pl.when(at == 2 * tiles)(lambda: small.begin(layer))
-        pl.when(at == 2 * tiles + 1)(lambda: small.middle(layer))
+        @pl.when(at == 2 * tiles)
+        def _():
+            for part in range(len(SUM_PARTS)):
+                small.begin(layer, part)
+
+        @pl.when(at == 2 * tiles + 1)
+        def _():
+            for part in range(len(SUM_PARTS)):
+                small.middle(layer, part)
+
 
         pl.when(at == 2 * tiles + 2)(lambda: start_u(layer, 0))
 
@@ -1053,31 +1077,27 @@
         i, r = blocks[b]
         return pltpu.make_async_copy(buf.at[b % COPY_BUFS], outs[i].at[pl.ds(r, COPY_ROWS)], out_sem.at[b % COPY_BUFS])
 
-    ahead = COPY_BUFS // 2
-    for b in range(min(ahead, len(blocks))):
+    for b in range(len(blocks)):
         read(b).start()
-    near.start()
-    pltpu.make_async_copy(small, small_buf, small_sem.at[4]).start()
+    small_read = pltpu.make_async_copy(small, small_buf, small_sem.at[4])
+    small_read.start()
 
     def small_write(row):
         return pltpu.make_async_copy(small_buf.at[pl.ds(row, 1)], small_outs[row], small_sem.at[row])
 
     for b in range(len(blocks)):
-        if b + ahead < len(blocks):
-            if b + ahead >= COPY_BUFS:
-                write(b + ahead - COPY_BUFS).wait()
-            read(b + ahead).start()
         read(b).wait()
+    near.start()
+    for b in range(len(blocks)):
         write(b).start()
-        if b == 0:
-            pltpu.make_async_copy(small, small_buf, small_sem.at[4]).wait()
-            small_outs[4][...] = small_buf[4:5, :1]
-            for row in range(4):
-                small_write(row).start()
+    small_read.wait()
+    small_outs[4][...] = small_buf[4:5, :1]
+    for row in range(4):
+        small_write(row).start()
     for row in range(4):
         small_write(row).wait()
     near.wait()
-    for b in range(max(0, len(blocks) - COPY_BUFS), len(blocks)):
+    for b in range(len(blocks)):
         write(b).wait()
 
 

time: 553 us -> 550 us (level)
  no operation moved by 1% of the time
where the time goes in v14:
time: 550 us
  Pallas kernels  548 us (100%)
    pallas_call x1, Pallas kernels, backward(): pl.pallas_call(back_kernel, name='backward', out_shape=[mat, mat, pltpu.V...  343 us
    pallas_call x1, Pallas kernels, front(): pl.pallas_call(front_kernel, name='front', out_shape=[wide_f32, wide_f32,...  175 us
    pallas_call x1, Pallas kernels, copy_out(): pl.pallas_call(copy_kernel, name='copy_out', out_shape=[jax.ShapeDtypeStr...  29.9 us

profile of v14, /device:TPU:0, one launch (start us, length us, event | category | flops | bytes accessed | tf_op | source)
XLA Modules:
  0.0 549.6 jit_solution(14719321991132070973)
XLA Ops:
  1.3 175.3 %front.1 = (f32[512,2048]{1,0:T(8,128)}, f32[512,2048]{1,0:T(8,128)}, bf16[1024,1024]{1,0:T(8,128)(2,1)}, bf16[1024,1024]{1,0:T(8,128)(2,1)}, bf16[1024,1024]{1,...) custom-call(bf16[512,2048]{1,0:T(8,128)(2,1)} %feat_a.1, ...), custom_call_target="tpu_custom_call" | custom-call | tf_op jit(solution)/shard_map/front/pallas_call | solution.py:771
  176.6 342.9 %backward.1 = (f32[2048,2048]{1,0:T(8,128)}, f32[2048,2048]{1,0:T(8,128)}, f32[2048,2048]{1,0:T(8,128)S(1)}, f32[5,2048]{1,0:T(8,128)}) custom-call(bf16[1024,2048]{1,0:T(8,128)(2,1)} %get-tuple-element.31.dz_hbm, bf16[1024,1024]{1,0:T(8,128)(2,1)} %get-tuple-element.32.x2, bf16[1024,1024]{1,0:T(8,128)(2,1)} %get-tuple-element.33.x1, ...), custom_call_target="tpu_custom_call" | custom-call | tf_op jit(solution)/shard_map/backward/pallas_call | solution.py:1043
  519.5 29.9 %copy_out.1 = (f32[512,2048]{1,0:T(8,128)}, f32[2048,2048]{1,0:T(8,128)}, f32[2048,2048]{1,0:T(8,128)}, f32[2048,2048]{1,0:T(8,128)}, f32[1,2048]{1,0:T(1,128)},...) custom-call(f32[512,2048]{1,0:T(8,128)} %get-tuple-element.30.refs_0_, ...), custom_call_target="tpu_custom_call" | custom-call | tf_op jit(solution)/shard_map/copy_out/pallas_call | solution.py:1110

commit v15 on v14

--- a/solution.py
+++ b/solution.py
@@ -428,11 +428,11 @@
     return jnp.sum(value.reshape(value.shape[0] // 8, 8, value.shape[1]), axis=0)
 
 
-def front_kernel(feat_a, feat_b, w_in, t_in, w_mid, t_mid, w_out, t_out, gain1, bias1, gain2, bias2, off_weight, pre1, pre2, xs2, xs1, xs0, dz, grad_emb, vec, *scratch):
-    (x_buf, u_buf, w_buf, stats, affine, loss, ea, eb, g_peer) = scratch[:9]
-    (x_sem, w_sem, pre_sem, keep_sem, keep_send, keep_recv, ge_sem, e_send, e_recv) = scratch[9:18]
-    small_refs = scratch[18 : 18 + SMALL_REFS]
-    acc, gathered, *landing, send, recv = scratch[18 + SMALL_REFS :]
+def front_kernel(feat_a, feat_b, w_in, t_in, w_mid, t_mid, w_out, t_out, gain1, bias1, gain2, bias2, off_hbm, pre1, pre2, xs2, xs1, xs0, dz, grad_emb, vec_hbm, *scratch):
+    (x_buf, u_buf, w_buf, stats, affine, loss, vec, off_weight, ea, eb, g_peer) = scratch[:11]
+    (x_sem, w_sem, row_sem, pre_sem, keep_sem, keep_send, keep_recv, ge_sem, e_send, e_recv) = scratch[11:21]
+    small_refs = scratch[21 : 21 + SMALL_REFS]
+    acc, gathered, *landing, send, recv = scratch[21 + SMALL_REFS :]
     rows_dev, width = feat_a.shape
     wide = w_buf.shape[2]
     tiles = width // wide
@@ -461,8 +461,12 @@
     feat(1).start()
     for g in range(1, W_BUFS - 1):
         start_w(g)
-    for j, ref in enumerate((gain1, bias1, gain2, bias2)):
-        affine[j] = ref[...]
+    row_loads = [pltpu.make_async_copy(ref, affine.at[j], row_sem.at[j]) for j, ref in enumerate((gain1, bias1, gain2, bias2))]
+    row_loads.append(pltpu.make_async_copy(off_hbm, off_weight, row_sem.at[4]))
+    for c in row_loads:
+        c.start()
+    early_rows = pltpu.make_async_copy(vec.at[pl.ds(0, 8)], vec_hbm.at[pl.ds(0, 8)], row_sem.at[5])
+    late_row = pltpu.make_async_copy(vec.at[pl.ds(8, 1)], vec_hbm.at[pl.ds(8, 1)], row_sem.at[6])
     feat(0).wait()
     payload[...] = jnp.zeros_like(payload)
 
@@ -609,6 +613,8 @@
         def _():
             place.all_here()
             start_x(0)
+            for c in row_loads:
+                c.wait()
 
         pl.when(i == tiles - 2)(lambda: small.begin(job, 0))
         pl.when((i == 0) & (job > 0))(lambda: small.middle(job - 1, 0))
@@ -626,6 +632,7 @@
     norm(JOBS - 1)
     for j, source in enumerate((affine.at[2], affine.at[3], stats.at[2, 0], stats.at[2, 1], affine.at[0], affine.at[1], stats.at[0, 0], stats.at[0, 1])):
         vec[j] = source[...]
+    early_rows.start()
 
     loss[...] = jnp.zeros_like(loss)
 
@@ -749,12 +756,15 @@
     small.end(JOBS + 1)
     for c in range(PLANE):
         vec[8, :, c * TILE : (c + 1) * TILE] = total[JOBS + 1, c, 0:1]
+    late_row.start()
     for w in range(3):
         keep_x(w)[1].wait_recv()
     for i in range(tiles):
         here, there = keep_dz(i)
         here.wait()
         there.wait()
+    early_rows.wait()
+    late_row.wait()
 
 
 def front(feat_a, feat_b, weights, affine, off_weight):
@@ -762,7 +772,6 @@
     half = width // 2
     part_rows = half // PARTS
     any_spec = pl.BlockSpec(memory_space=pl.ANY)
-    vmem_spec = pl.BlockSpec(memory_space=pltpu.VMEM)
     wide_f32 = jax.ShapeDtypeStruct((rows_dev, width), jnp.float32)
     kept = jax.ShapeDtypeStruct((2 * rows_dev, half), jnp.bfloat16)
     both_dz = jax.ShapeDtypeStruct((2 * rows_dev, width), jnp.bfloat16)
@@ -773,8 +782,8 @@
         name="front",
         out_shape=[wide_f32, wide_f32, kept, kept, kept, both_dz, wide_f32]
         + [jax.ShapeDtypeStruct((9, 1, width), jnp.float32)],
-        in_specs=[any_spec] * 8 + [vmem_spec] * 4 + [pl.BlockSpec(memory_space=pltpu.SMEM)],
-        out_specs=[any_spec] * 7 + [vmem_spec],
+        in_specs=[any_spec] * 13,
+        out_specs=[any_spec] * 8,
         scratch_shapes=[
             pltpu.VMEM((2, rows_dev, width), jnp.bfloat16),
             pltpu.VMEM((2, rows_dev, width), jnp.float32),
@@ -782,11 +791,14 @@
             pltpu.VMEM((JOBS, 2, 1, width), jnp.float32),
             pltpu.VMEM((4, 1, width), jnp.float32),
             pltpu.VMEM((1, width), jnp.float32),
+            pltpu.VMEM((9, 1, width), jnp.float32),
+            pltpu.SMEM((1,), jnp.float32),
             pltpu.VMEM((2 * rows_dev, half), jnp.bfloat16),
             pltpu.VMEM((2 * rows_dev, width), jnp.bfloat16),
             pltpu.VMEM((PARTS, part_rows, width), jnp.bfloat16),
             dma((2,)),
             dma((W_BUFS,)),
+            dma((7,)),
             dma((1,)),
             dma((keeps,)),
             dma((keeps,)),
@@ -801,11 +813,11 @@
     )(feat_a, feat_b, *weights, *affine, off_weight)
 
 
-def back_kernel(dz_hbm, x2, x1, x0, w_out, w_mid, u2, u1, vec, out2, out1, out0, sums_out, *scratch):
-    (dy, xs, w_buf) = scratch[:3]
-    (in_sem, tile_sem, peer_send, peer_recv, store_sem) = scratch[3:8]
-    small_refs = scratch[8 : 8 + SMALL_REFS]
-    acc, gathered, *landing, send, recv = scratch[8 + SMALL_REFS :]
+def back_kernel(dz_hbm, x2, x1, x0, w_out, w_mid, u2, u1, vec_hbm, out2, out1, out0, sums_hbm, *scratch):
+    (dy, xs, w_buf, vec, sums_out) = scratch[:5]
+    (in_sem, tile_sem, row_sem, peer_send, peer_recv, store_sem) = scratch[5:11]
+    small_refs = scratch[11 : 11 + SMALL_REFS]
+    acc, gathered, *landing, send, recv = scratch[11 + SMALL_REFS :]
     rows_dev, width = u2.shape
     wide = w_buf.shape[0]
     tiles = width // wide
@@ -855,7 +867,10 @@
         load_dz(c).start()
     w_tile(weights[0], 0).start()
     u_tile(pres[0], 0).start()
+    vec_load = pltpu.make_async_copy(vec_hbm, vec, row_sem.at[0])
+    vec_load.start()
     load_x(1).start()
+    sums_store = pltpu.make_async_copy(sums_out, sums_hbm, row_sem.at[1])
     payload[...] = jnp.zeros_like(payload)
 
     def row_loop(body, carry):
@@ -1019,17 +1034,23 @@
                 w_tile(weights[1], 0).start()
                 u_tile(pres[1], 0).start()
 
-            pl.when(layer == 1)(lambda: load_x(2).start())
+            @pl.when(layer == 1)
+            def _():
+                load_x(2).start()
+                for c in range(PLANE):
+                    for row in range(4):
+                        sums_out[row : row + 1, c * TILE : (c + 1) * TILE] = sums[row // 2, c, row % 2 : row % 2 + 1]
+                sums_out[4:5] = jnp.full((1, width), jnp.sum(vec[8]))
+                sums_store.start()
+
 
     form(0, GROUP // 2)
     place.all_here()
+    vec_load.wait()
     run_slots(BACK_PLAN, count, stage, lambda t: pl.when(t < 2 * LAYER_SLOTS)(lambda: layer_work(t)))
     for w in (1, 2):
         peer_dy(w).wait_send()
-    for c in range(PLANE):
-        for row in range(4):
-            sums_out[row : row + 1, c * TILE : (c + 1) * TILE] = sums[row // 2, c, row % 2 : row % 2 + 1]
-    sums_out[4:5] = jnp.full((1, width), jnp.sum(vec[8]))
+    sums_store.wait()
 
 
 def backward(grad_z, x2, x1, x0, w_out, w_mid, u2, u1, vec):
@@ -1044,14 +1065,17 @@
         back_kernel,
         name="backward",
         out_shape=[mat, mat, pltpu.VMEM((width, width), jnp.float32), jax.ShapeDtypeStruct((5, width), jnp.float32)],
-        in_specs=[any_spec] * 8 + [vmem_spec],
-        out_specs=[any_spec] * 2 + [vmem_spec] * 2,
+        in_specs=[any_spec] * 9,
+        out_specs=[any_spec] * 2 + [vmem_spec, any_spec],
         scratch_shapes=[
             pltpu.VMEM((2, 2 * rows_dev, width), jnp.bfloat16),
             pltpu.VMEM((2, 2 * rows_dev, width // 2), jnp.bfloat16),
             pltpu.VMEM((WIDE, width), jnp.bfloat16),
+            pltpu.VMEM((9, 1, width), jnp.float32),
+            pltpu.VMEM((5, width), jnp.float32),
             dma((MATS + 2,)),
             dma((2, 2)),
+            dma((2,)),
             dma((MATS,)),
             dma((MATS,)),
             dma((count,)),

time: 550 us -> 548 us (level)
  no operation moved by 1% of the time
where the time goes in v15:
time: 548 us
  Pallas kernels  547 us (100%)
    pallas_call x1, Pallas kernels, backward(): pl.pallas_call(back_kernel, name='backward', out_shape=[mat, mat, pltpu.V...  342 us
    pallas_call x1, Pallas kernels, front(): pl.pallas_call(front_kernel, name='front', out_shape=[wide_f32, wide_f32,...  175 us
    pallas_call x1, Pallas kernels, copy_out(): pl.pallas_call(copy_kernel, name='copy_out', out_shape=[jax.ShapeDtypeStr...  29.9 us

profile of v15, /device:TPU:0, one launch (start us, length us, event | category | flops | bytes accessed | tf_op | source)
XLA Modules:
  0.0 548.0 jit_solution(6497565467213080989)
XLA Ops:
  1.3 174.7 %front.1 = (f32[512,2048]{1,0:T(8,128)}, f32[512,2048]{1,0:T(8,128)}, bf16[1024,1024]{1,0:T(8,128)(2,1)}, bf16[1024,1024]{1,0:T(8,128)(2,1)}, bf16[1024,1024]{1,...) custom-call(bf16[512,2048]{1,0:T(8,128)(2,1)} %feat_a.1, ...), custom_call_target="tpu_custom_call" | custom-call | tf_op jit(solution)/shard_map/front/pallas_call | solution.py:780
  176.0 341.9 %backward.1 = (f32[2048,2048]{1,0:T(8,128)}, f32[2048,2048]{1,0:T(8,128)}, f32[2048,2048]{1,0:T(8,128)S(1)}, f32[5,2048]{1,0:T(8,128)}) custom-call(bf16[1024,2048]{1,0:T(8,128)(2,1)} %get-tuple-element.31.dz_hbm, bf16[1024,1024]{1,0:T(8,128)(2,1)} %get-tuple-element.32.x2, bf16[1024,1024]{1,0:T(8,128)(2,1)} %get-tuple-element.33.x1, ...), custom_call_target="tpu_custom_call" | custom-call | tf_op jit(solution)/shard_map/backward/pallas_call | solution.py:1064
  517.9 29.9 %copy_out.1 = (f32[512,2048]{1,0:T(8,128)}, f32[2048,2048]{1,0:T(8,128)}, f32[2048,2048]{1,0:T(8,128)}, f32[2048,2048]{1,0:T(8,128)}, f32[1,2048]{1,0:T(1,128)},...) custom-call(f32[512,2048]{1,0:T(8,128)} %get-tuple-element.30.refs_0_, ...), custom_call_target="tpu_custom_call" | custom-call | tf_op jit(solution)/shard_map/copy_out/pallas_call | solution.py:1134

commit v16 on v15

--- a/solution.py
+++ b/solution.py
@@ -15,7 +15,8 @@
 DEPTH = 4
 TILE = 256
 WIDE = 512
-BLOCK = 128
+BLOCK = 256
+BACK_BLOCK = 128
 SUM_ROWS = 2
 SUM_PARTS = ((0, 6), (6, 2))
 PARTS = 16
@@ -862,9 +863,17 @@
     def load_dz(c):
         return pltpu.make_async_copy(dz_hbm.at[:, rows(c * size, size)], dy.at[0, :, rows(c * size, size)], in_sem.at[MATS + c])
 
-    load_x(0).start()
+    ahead = GROUP // 2 * part_rows
+
+    def load_first(lo, n, sem):
+        return pltpu.make_async_copy(mats_in[0].at[:, pl.ds(lo, n)], xs.at[0, :, pl.ds(lo, n)], sem)
+
+    first_x = load_first(0, ahead, row_sem.at[2])
+    rest_x = load_first(ahead, half - ahead, in_sem.at[0])
+    first_x.start()
     for c in range(width // size):
         load_dz(c).start()
+    rest_x.start()
     w_tile(weights[0], 0).start()
     u_tile(pres[0], 0).start()
     vec_load = pltpu.make_async_copy(vec_hbm, vec, row_sem.at[0])
@@ -874,7 +883,7 @@
     payload[...] = jnp.zeros_like(payload)
 
     def row_loop(body, carry):
-        return lax.fori_loop(0, rows_dev // BLOCK, body, carry)
+        return lax.fori_loop(0, rows_dev // BACK_BLOCK, body, carry)
 
     def chain_tile(layer, i):
         w_tile(w_out, i).wait()
@@ -887,8 +896,8 @@
         gain, bias, mean, inv = (vec[layer * 4 + j, :, at_cols] for j in range(4))
 
         def block(r, carry):
-            at = rows(r * BLOCK, BLOCK)
-            n = (out0[rows(rows_dev + r * BLOCK, BLOCK), rows((i % 2) * wide, wide)] - mean) * inv
+            at = rows(r * BACK_BLOCK, BACK_BLOCK)
+            n = (out0[rows(rows_dev + r * BACK_BLOCK, BACK_BLOCK), rows((i % 2) * wide, wide)] - mean) * inv
             g = jnp.where(n * gain + bias > 0.0, dpre[at, at_cols], 0.0)
             dpre[at, at_cols] = g
             return carry[0] + fold(g * n), carry[1] + fold(g)
@@ -909,10 +918,10 @@
         scale = gain * inv
 
         def block(r, c):
-            at = rows(r * BLOCK, BLOCK)
-            n = (out0[rows(rows_dev + r * BLOCK, BLOCK), rows((i % 2) * wide, wide)] - mean) * inv
+            at = rows(r * BACK_BLOCK, BACK_BLOCK)
+            n = (out0[rows(rows_dev + r * BACK_BLOCK, BACK_BLOCK), rows((i % 2) * wide, wide)] - mean) * inv
             value = (dpre[at, at_cols] - mean_g - n * mean_gn) * scale
-            dy[1 - layer, rows(core * rows_dev + r * BLOCK, BLOCK), at_cols] = value.astype(jnp.bfloat16)
+            dy[1 - layer, rows(core * rows_dev + r * BACK_BLOCK, BACK_BLOCK), at_cols] = value.astype(jnp.bfloat16)
             return c
 
         row_loop(block, 0)
@@ -946,10 +955,14 @@
     def form(k, group):
         w, j = k // PARTS, k % ACC_SLOTS
 
-        @pl.when(k % PARTS == 0)
-        def _():
-            pltpu.make_async_copy(xs.at[w % 2], xs.at[w % 2], in_sem.at[w]).wait()
-            pl.when(w > 0)(lambda: peer_dy(w).wait_recv())
+        if isinstance(k, int):
+            (rest_x if k else first_x).wait()
+        else:
+
+            @pl.when(k % PARTS == 0)
+            def _():
+                pltpu.make_async_copy(xs.at[w % 2], xs.at[w % 2], in_sem.at[w]).wait()
+                peer_dy(w).wait_recv()
 
         at = rows((k % PARTS) * part_rows, group * part_rows)
 
@@ -1075,7 +1088,7 @@
             pltpu.VMEM((5, width), jnp.float32),
             dma((MATS + 2,)),
             dma((2, 2)),
-            dma((2,)),
+            dma((3,)),
             dma((MATS,)),
             dma((MATS,)),
             dma((count,)),

time: 548 us -> 548 us (level)
  no operation moved by 1% of the time
where the time goes in v16:
time: 548 us; the launch traced here: 547 us
  Pallas kernels  546 us (100%)
    pallas_call x1, Pallas kernels, backward(): pl.pallas_call(back_kernel, name='backward', out_shape=[mat, mat, pltpu.V...  342 us
    pallas_call x1, Pallas kernels, front(): pl.pallas_call(front_kernel, name='front', out_shape=[wide_f32, wide_f32,...  174 us
    pallas_call x1, Pallas kernels, copy_out(): pl.pallas_call(copy_kernel, name='copy_out', out_shape=[jax.ShapeDtypeStr...  29.9 us

profile of v16, /device:TPU:0, one launch (start us, length us, event | category | flops | bytes accessed | tf_op | source)
XLA Modules:
  0.0 547.4 jit_solution(15590433356238515608)
XLA Ops:
  1.3 174.2 %front.1 = (f32[512,2048]{1,0:T(8,128)}, f32[512,2048]{1,0:T(8,128)}, bf16[1024,1024]{1,0:T(8,128)(2,1)}, bf16[1024,1024]{1,0:T(8,128)(2,1)}, bf16[1024,1024]{1,...) custom-call(bf16[512,2048]{1,0:T(8,128)(2,1)} %feat_a.1, ...), custom_call_target="tpu_custom_call" | custom-call | tf_op jit(solution)/shard_map/front/pallas_call | solution.py:781
  175.5 341.9 %backward.1 = (f32[2048,2048]{1,0:T(8,128)}, f32[2048,2048]{1,0:T(8,128)}, f32[2048,2048]{1,0:T(8,128)S(1)}, f32[5,2048]{1,0:T(8,128)}) custom-call(bf16[1024,2048]{1,0:T(8,128)(2,1)} %get-tuple-element.31.dz_hbm, bf16[1024,1024]{1,0:T(8,128)(2,1)} %get-tuple-element.32.x2, bf16[1024,1024]{1,0:T(8,128)(2,1)} %get-tuple-element.33.x1, ...), custom_call_target="tpu_custom_call" | custom-call | tf_op jit(solution)/shard_map/backward/pallas_call | solution.py:1077
  517.4 29.9 %copy_out.1 = (f32[512,2048]{1,0:T(8,128)}, f32[2048,2048]{1,0:T(8,128)}, f32[2048,2048]{1,0:T(8,128)}, f32[2048,2048]{1,0:T(8,128)}, f32[1,2048]{1,0:T(1,128)},...) custom-call(f32[512,2048]{1,0:T(8,128)} %get-tuple-element.30.refs_0_, ...), custom_call_target="tpu_custom_call" | custom-call | tf_op jit(solution)/shard_map/copy_out/pallas_call | solution.py:1147
